TPU v7x, 16 devices: a whole 2x2x2 slice. The times are simulated.
16 devices in a mesh: tp: 4 (over z, y), dp: 4 (over x, core).
Axes of the slice: x: 2, y: 2, z: 2, core: 2. Of those that a mesh axis runs over, the one named last changes fastest.
Arguments:
- hidden: bfloat16 [4, 1024, 768], P('dp')
- ln_gamma: float32 [768], replicated
- ln_beta: float32 [768], replicated
- embed_table: bfloat16 [50304, 768], P('tp')
- labels: int32 [4, 1024], P('dp')
- loss_mask: int32 [4, 1024], P('dp')
Outputs:
- output 1: float32 [], replicated
- output 2: bfloat16 [4, 1024, 768], P('dp')
- output 3: float32 [50304, 768], P('tp')
- output 4: float32 [768], replicated
- output 5: float32 [768], replicated
All inputs are finite; a program needn't handle non-finite values.
Results may differ from a plain program's by a relative error of at most 0.001.
Values sent between devices are 32-bit elements.
A program may use at most 1 GiB of HBM per device.

v0:
```python
import functools

import jax
import jax.numpy as jnp
from jax import lax
from jax.experimental import pallas as pl
from jax.experimental.pallas import tpu as pltpu
from jax.sharding import PartitionSpec as P


LAYER_EPS = 1e-5
BLOCK = 256
PAIR = 2 * BLOCK
BIG = 1e30
VMEM_LIMIT = 62 * 1024 * 1024


CORE, NEAR_PAIRS, FAR_PAIRS, ALL_PAIRS, ROW_START = 0, 1, 2, 3, 4
NEAR_ORDER, NEAR_PIECES, FAR_PIECES, PAIR_IDS = 8, 16, 24, 32


def chunk_list(total, size):
    return [(start, min(size, total - start)) for start in range(0, total, size)]


def last(i, count):
    return jnp.minimum(i, count - 1)


def logits_kernel(count, idx_ref, e_ref, za_ref, zb_ref, *rest):
    l_ref, zc_ref, st_ref = rest[-3:]
    pl.when(pl.program_id(0) < idx_ref[count])(lambda: logits_step(e_ref, za_ref, zb_ref, l_ref, zc_ref, st_ref))


def logits_step(e_ref, za_ref, zb_ref, l_ref, zc_ref, st_ref):
    zc_ref[0, :BLOCK, :] = za_ref[0]
    zc_ref[0, BLOCK:, :] = zb_ref[0]
    rows = e_ref.shape[0]
    size = 528

    top = jnp.full((1, PAIR), -BIG, jnp.float32)
    total = jnp.zeros((1, PAIR), jnp.float32)

    def add(start, n, old_top, top, total):
        return total * jnp.exp(old_top - top) + jnp.sum(jnp.exp(l_ref[0, start:start + n, :] - top), axis=0, keepdims=True)

    waiting = None
    for start, n in chunk_list(rows, size):
        tile = lax.dot_general(e_ref[start:start + n, :], zc_ref[0], (((1,), (1,)), ((), ())), preferred_element_type=jnp.float32)
        l_ref[0, start:start + n, :] = tile
        new_top = jnp.maximum(top, jnp.max(tile, axis=0, keepdims=True))
        if waiting is not None:
            total = add(*waiting, total)
        waiting = (start, n, top, new_top)
        top = new_top
    total = add(*waiting, total)
    st_ref[0, 0:1, :] = top
    st_ref[0, 1:2, :] = total


def grad_tile(tile, lse, weight, is_target):
    probs = jnp.exp(tile - lse)
    return (jnp.where(is_target, probs - 1.0, probs) * weight).astype(jnp.bfloat16)


def dz_kernel(idx_ref, e_ref, l_ref, tok_ref, lab_ref, own_ref, mate_ref, tl_ref, l_out_ref, acc_ref, out_ref, et_ref, sem):
    i = pl.program_id(0)
    rows = e_ref.shape[0]
    size = 512
    full = rows // size

    @pl.when(i == 0)
    def _():
        def turn(k, carry):
            start = pl.multiple_of(k * size, size)
            et_ref[:, pl.ds(start, size)] = e_ref[pl.ds(start, size), :].T
            return carry

        lax.fori_loop(0, full, turn, 0)
        if rows > full * size:
            et_ref[:, full * size:] = e_ref[full * size:, :].T

    live = i < idx_ref[NEAR_PAIRS]
    pl.when(live)(lambda: dz_step(idx_ref, et_ref, l_ref, tok_ref, lab_ref, tl_ref, acc_ref))

    @pl.when(live)
    def _():
        out_ref[...] = acc_ref[...].T

    @pl.when(jnp.logical_not(live))
    def _():
        out_ref[...] = jnp.zeros_like(out_ref)

    for h in range(2):
        block = idx_ref[NEAR_ORDER + 2 * i + h]
        for seq in range(2):
            target = own_ref if seq == 0 else mate_ref
            copy = pltpu.make_async_copy(out_ref.at[pl.ds(h * BLOCK, BLOCK), :], target.at[block % 4], sem.at[h])
            pl.when(block // 4 == (idx_ref[CORE] + seq) % 2)(copy.start)
    for h in range(2):
        pltpu.make_async_copy(out_ref.at[pl.ds(h * BLOCK, BLOCK), :], own_ref.at[0], sem.at[h]).wait()


def dz_step(idx_ref, et_ref, l_ref, tok_ref, lab_ref, tl_ref, acc_ref):
    lse = tok_ref[0, 0:1, :]
    weight = tok_ref[0, 1:2, :]
    label = lab_ref[0] - idx_ref[ROW_START]
    target = jnp.zeros((1, PAIR), jnp.float32)
    for start, n in chunk_list(et_ref.shape[1], 1024):
        tile = l_ref[0, start:start + n, :]
        is_target = lax.broadcasted_iota(jnp.int32, (n, PAIR), 0) == label - start
        grad = grad_tile(tile, lse, weight, is_target)
        target = target + jnp.sum(jnp.where(is_target, tile, 0.0), axis=0, keepdims=True)
        part = jnp.dot(et_ref[:, start:start + n], grad, preferred_element_type=jnp.float32)
        if start == 0:
            acc_ref[...] = part
        else:
            acc_ref[...] += part
    tl_ref[0] = target


def de_kernel(offset, rows, got_offset, idx_ref, l_ref, z_ref, tok_ref, lab_ref, *rest):
    if got_offset is None:
        part_ref, out_ref, sem = rest[-3:]
        got_ref = None
    else:
        got_ref, part_ref, out_ref, sem = rest[0], rest[-3], rest[-2], rest[-1]
    i = pl.program_id(0)
    core = idx_ref[CORE]
    half = out_ref.shape[0] // 2
    count = idx_ref[ALL_PAIRS]
    lse = tok_ref[0, 0:1, :]
    weight = tok_ref[0, 1:2, :]
    label = lab_ref[0] - idx_ref[ROW_START] - offset

    def rows_at(side, start, n):
        return out_ref.at[pl.ds(pl.multiple_of(side * half + start, 8), n), :]

    own = pltpu.make_async_copy(part_ref, rows_at(core, offset, rows), sem.at[0])
    got = None
    if got_ref is not None:
        got = pltpu.make_async_copy(got_ref, rows_at(1 - core, got_offset, got_ref.shape[0]), sem.at[1])
        pl.when(i == 0)(got.start)

    @pl.when(i == 0)
    def _():
        part_ref[...] = jnp.zeros_like(part_ref)

    @pl.when(i < count)
    def _():
        for start, n in chunk_list(rows, 528):
            is_target = lax.broadcasted_iota(jnp.int32, (n, PAIR), 0) == label - start
            grad = grad_tile(l_ref[0, start:start + n, :], lse, weight, is_target)
            part_ref[start:start + n, :] += jnp.dot(grad, z_ref[0], preferred_element_type=jnp.float32)

    pl.when(i == count - 1)(own.start)

    @pl.when(i == pl.num_programs(0) - 1)
    def _():
        own.wait()
        if got is not None:
            got.wait()


def place_kernel(got_offset, idx_ref, got_ref, de_ref, out_ref, sem):
    half = out_ref.shape[0] // 2
    start = pl.multiple_of((1 - idx_ref[CORE]) * half + got_offset, 8)
    copy = pltpu.make_async_copy(got_ref, out_ref.at[pl.ds(start, got_ref.shape[0]), :], sem)
    copy.start()
    copy.wait()


def params(limit=VMEM_LIMIT):
    return pltpu.CompilerParams(vmem_limit_bytes=limit, dimension_semantics=("arbitrary",))


def cost(pairs, rows, width):
    n = PAIR * pairs * rows
    return pl.CostEstimate(flops=2 * n * width, bytes_accessed=4 * n, transcendentals=n)


ANY = pl.BlockSpec(memory_space=pl.ANY)


def call_logits(idx, e, z, previous, rows):
    pairs = 8
    base, count, order = (0, NEAR_PAIRS, NEAR_PIECES) if previous is None else (4, FAR_PAIRS, FAR_PIECES)
    width = e.shape[1]
    extra = [] if previous is None else list(previous)
    spec = pltpu.PrefetchScalarGridSpec(
        num_scalar_prefetch=1,
        grid=(4,),
        in_specs=[
            pl.BlockSpec((rows, width), lambda i, s: (s[CORE], 0), pipeline_mode=pl.Buffered(1)),
            pl.BlockSpec((1, BLOCK, width), lambda i, s: (s[order + 2 * last(i, s[count])], 0, 0)),
            pl.BlockSpec((1, BLOCK, width), lambda i, s: (s[order + 1 + 2 * last(i, s[count])], 0, 0)),
        ] + [ANY] * len(extra),
        out_specs=[
            pl.BlockSpec((1, rows, PAIR), lambda i, s: (base + last(i, s[count]), 0, 0)),
            pl.BlockSpec((1, PAIR, width), lambda i, s: (base + last(i, s[count]), 0, 0)),
            pl.BlockSpec((1, 2, PAIR), lambda i, s: (last(i, s[count]), 0, 0)),
        ],
    )
    return pl.pallas_call(
        functools.partial(logits_kernel, count),
        grid_spec=spec,
        out_shape=[
            jax.ShapeDtypeStruct((pairs, rows, PAIR), jnp.float32),
            jax.ShapeDtypeStruct((pairs, PAIR, width), jnp.bfloat16),
            jax.ShapeDtypeStruct((4, 2, PAIR), jnp.float32),
        ],
        input_output_aliases={} if previous is None else {4: 0, 5: 1},
        compiler_params=params(),
        cost_estimate=cost(3, rows, width),
        name="logits_near" if previous is None else "logits_far",
    )(idx, e, z, z, *extra)


def call_dz(idx, e, l, tok, lab):
    width, rows = e.shape[1], l.shape[1]
    pick_row = lambda i, s: (last(i, s[NEAR_PAIRS]), 0, 0)
    spec = pltpu.PrefetchScalarGridSpec(
        num_scalar_prefetch=1,
        grid=(4,),
        in_specs=[
            pl.BlockSpec((rows, width), lambda i, s: (s[CORE], 0), pipeline_mode=pl.Buffered(1)),
            pl.BlockSpec((1, rows, PAIR), pick_row),
            pl.BlockSpec((1, 2, PAIR), pick_row),
            pl.BlockSpec((1, 1, PAIR), pick_row),
        ],
        out_specs=[ANY, ANY, pl.BlockSpec((1, 1, PAIR), pick_row), ANY],
        scratch_shapes=[
            pltpu.VMEM((width, PAIR), jnp.float32),
            pltpu.VMEM((PAIR, width), jnp.float32),
            pltpu.VMEM((width, rows), jnp.bfloat16),
            pltpu.SemaphoreType.DMA((2,)),
        ],
    )
    half = jax.ShapeDtypeStruct((4, BLOCK, width), jnp.float32)
    return pl.pallas_call(
        dz_kernel,
        grid_spec=spec,
        out_shape=[half, half, jax.ShapeDtypeStruct((4, 1, PAIR), jnp.float32), jax.ShapeDtypeStruct(l.shape, l.dtype)],
        input_output_aliases={2: 3},
        compiler_params=params(),
        cost_estimate=cost(3, rows, width),
        name="dz_part",
    )(idx, e, l, tok, lab)


def call_de(idx, l, zc, tok, lab, de, offset, rows, got, got_offset):
    total, width = l.shape[1], zc.shape[2]
    j = offset // rows
    extra = [] if de is None else [de]
    extra_specs = [ANY] * len(extra)
    if got is not None:
        extra = [got] + extra
        extra_specs = [pl.BlockSpec(got.shape, lambda i, s: (0, 0), pipeline_mode=pl.Buffered(1))] + extra_specs
    spec = pltpu.PrefetchScalarGridSpec(
        num_scalar_prefetch=1,
        grid=(8,),
        in_specs=[
            pl.BlockSpec((1, rows, PAIR), lambda i, s: (s[PAIR_IDS + last(i, s[ALL_PAIRS])], j, 0)),
            pl.BlockSpec((1, PAIR, width), lambda i, s: (s[PAIR_IDS + last(i, s[ALL_PAIRS])], 0, 0)),
            pl.BlockSpec((1, 2, PAIR), lambda i, s: (s[PAIR_IDS + last(i, s[ALL_PAIRS])], 0, 0)),
            pl.BlockSpec((1, 1, PAIR), lambda i, s: (s[PAIR_IDS + last(i, s[ALL_PAIRS])], 0, 0)),
        ] + extra_specs,
        out_specs=[pl.BlockSpec((rows, width), lambda i, s: (0, 0)), ANY],
        scratch_shapes=[pltpu.SemaphoreType.DMA((2,))],
    )
    return pl.pallas_call(
        functools.partial(de_kernel, offset, rows, got_offset if got is not None else None),
        grid_spec=spec,
        out_shape=[jax.ShapeDtypeStruct((rows, width), jnp.float32), jax.ShapeDtypeStruct((2 * total, width), jnp.float32)],
        input_output_aliases={} if de is None else {4 + len(extra): 1},
        compiler_params=params(),
        cost_estimate=cost(5, rows, width),
    )(idx, l, zc, tok, lab, *extra)


def call_place(idx, got, de, got_offset):
    spec = pltpu.PrefetchScalarGridSpec(
        num_scalar_prefetch=1,
        grid=(1,),
        in_specs=[pl.BlockSpec(got.shape, lambda i, s: (0, 0), pipeline_mode=pl.Buffered(1)), ANY],
        out_specs=ANY,
        scratch_shapes=[pltpu.SemaphoreType.DMA],
    )
    return pl.pallas_call(
        functools.partial(place_kernel, got_offset),
        grid_spec=spec,
        out_shape=jax.ShapeDtypeStruct(de.shape, de.dtype),
        input_output_aliases={2: 0},
        compiler_params=params(),
        name="place",
    )(idx, got, de)


def order_blocks(active):
    n = active.shape[1]
    act = active.astype(jnp.int32)
    ids = jnp.arange(n, dtype=jnp.int32)
    before = (ids[None, :] < ids[:, None]).astype(jnp.int32)
    ahead = jnp.sum(before[None] * act[:, None, :], axis=2)
    count = jnp.sum(act, axis=1, keepdims=True)
    place = jnp.where(act > 0, ahead, count + ids - ahead)
    hit = place[:, None, :] == ids[None, :, None]
    return jnp.sum(jnp.where(hit, ids, 0), axis=2), count[:, 0], hit


def solution(mesh):
    n_tp, n_dp = mesh.shape['tp'], mesh.shape['dp']

    def flip(x, axis, bits):
        n = n_tp if axis == 'tp' else n_dp
        return lax.ppermute(x, axis, [(k, k ^ bits) for k in range(n)])

    def flip_both(x, tp_bits, dp_bits):
        return lax.ppermute(x, ('tp', 'dp'), [(k, ((k // n_dp) ^ tp_bits) * n_dp + ((k % n_dp) ^ dp_bits)) for k in range(n_tp * n_dp)])

    def from_group(x):
        return jnp.stack([x] + [flip_both(x, t, d) for t in range(4) for d in range(2) if (t, d) != (0, 0)])

    def pick(x, index):
        return lax.dynamic_index_in_dim(x, index, 0, keepdims=False)

    def local_step(hidden, ln_gamma, ln_beta, embed_shard, labels, loss_mask):
        tp, dp = lax.axis_index('tp'), lax.axis_index('dp')
        core = dp & 1
        y, z = tp & 1, tp >> 1
        seq, width = hidden.shape[1:]
        quarters, piece = seq // BLOCK, BLOCK // 2
        rows = embed_shard.shape[0] // 2
        row_start = tp * (2 * rows) + core * rows

        def by_core(mine, other):
            return jnp.stack([jnp.where(core == 0, mine, other), jnp.where(core == 0, other, mine)])

        marked = jnp.where(loss_mask[0] > 0, labels[0], -1)
        far_marks = [flip(marked, 'dp', 2), flip(marked, 'dp', 3)]
        mate_marks = flip(marked, 'dp', 1)

        x_float = hidden[0].astype(jnp.float32)
        centered = x_float - jnp.mean(x_float, axis=-1, keepdims=True)
        inv_std = lax.rsqrt(jnp.mean(centered * centered, axis=-1, keepdims=True) + LAYER_EPS)
        x_hat = (centered * inv_std).reshape(quarters, BLOCK, width)

        def to_z(values):
            return (values * ln_gamma + ln_beta).astype(jnp.bfloat16)

        mate = flip(x_hat, 'dp', 1)
        own_quarter, far_quarter = lax.optimization_barrier((pick(x_hat, tp), pick(x_hat, tp ^ 3)))
        far0, far3 = flip(own_quarter, 'dp', 2), flip(far_quarter, 'dp', 2)

        marks = jnp.concatenate([by_core(marked, mate_marks), by_core(*far_marks)]).reshape(2, 8, BLOCK)
        token_count = jnp.sum((marks >= 0).astype(jnp.float32))
        order, active, hit = order_blocks(jnp.any(marks >= 0, axis=2))
        lab = jnp.sum(jnp.where(hit[..., None], marks[:, None], 0), axis=2).reshape(8, 1, PAIR)
        pairs = (active + 1) // 2
        pair_ids = jnp.arange(8, dtype=jnp.int32)
        pair_idx = jnp.where(pair_ids < pairs[0], pair_ids, jnp.minimum(4 + pair_ids - pairs[0], 7))
        zero = jnp.zeros((), jnp.int32)
        scalars = jnp.stack([core, pairs[0], pairs[1], pairs[0] + pairs[1], row_start, zero, zero, zero])
        idx = jnp.concatenate([scalars, order[0], order[0] ^ (core * 4), order[1] ^ (core * 4 + tp), pair_idx])

        near_z = to_z(jnp.concatenate([x_hat, mate]))
        logits, z_pairs, near_stats = call_logits(idx, embed_shard, near_z, None, rows)

        def combine(every, labels_here):
            top = jnp.max(every[:, :, 0], axis=0)
            total = jnp.sum(every[:, :, 1] * jnp.exp(every[:, :, 0] - top), axis=0)
            live = labels_here[:, 0] >= 0
            lse = jnp.where(live, top + jnp.log(total), BIG)
            return jnp.stack([lse, jnp.where(live, 1.0 / token_count, 0.0)], axis=1), lse, live

        near_tok, near_lse, near_live = combine(from_group(near_stats), lab[:4])
        mate0, mate3 = flip(far0, 'dp', 1), flip(far3, 'dp', 1)
        far1, far2 = flip(far0, 'tp', 1), flip(far0, 'tp', 2)
        dz_own, dz_mate, target, logits = call_dz(idx, embed_shard, logits, near_tok, lab[:4])

        mate1, mate2 = flip(far1, 'dp', 1), flip(far2, 'dp', 1)
        part = dz_own + flip(dz_mate, 'dp', 1)
        grid_part = part.reshape(2, 2, BLOCK, width)
        a_part, b_part = grid_part[:, :, :piece], grid_part[:, :, piece:]
        a_got = flip(lax.dynamic_index_in_dim(a_part, 1 - y, 1, keepdims=False), 'tp', 1)
        b_got = flip(pick(b_part, 1 - z), 'tp', 2)
        a_keep = lax.dynamic_index_in_dim(a_part, y, 1, keepdims=False) + a_got
        b_keep = pick(b_part, z) + b_got

        pieces, logits = lax.optimization_barrier(([far0, far1, far2, far3, mate0, mate1, mate2, mate3], logits))
        far_z = to_z(jnp.stack(pieces))
        logits, z_pairs, far_stats = call_logits(idx, embed_shard, far_z, (logits, z_pairs), rows)
        far_tok, _, _ = combine(from_group(far_stats), lab[4:])
        a_grad = flip(pick(a_keep, 1 - z), 'tp', 2)
        b_grad = flip(pick(b_keep, 1 - y), 'tp', 1)
        grad = jnp.concatenate([pick(a_keep, z) + a_grad, pick(b_keep, y) + b_grad])
        tok = jnp.concatenate([near_tok, far_tok])

        hat = own_quarter
        scaled = grad * ln_gamma
        inner = scaled - jnp.mean(scaled, axis=-1, keepdims=True) - hat * jnp.mean(scaled * hat, axis=-1, keepdims=True)
        a0, b0 = inner[:piece], inner[piece:]
        a1, b2 = flip(a0, 'tp', 1), flip(b0, 'tp', 2)
        a2, a3 = flip(a0, 'tp', 2), flip(a1, 'tp', 2)
        b1, b3 = flip(b0, 'tp', 1), flip(b2, 'tp', 1)
        gathered = jnp.stack([jnp.concatenate(v) for v in ((a0, b0), (a1, b1), (a2, b2), (a3, b3))])
        gathered = jnp.stack([pick(gathered, tp ^ q) for q in range(quarters)]).reshape(seq, width)
        d_hidden = (gathered * inv_std).astype(jnp.bfloat16)[None]

        lead = ((tp == 0) & (core == 0)).astype(jnp.float32)
        loss = jnp.sum(jnp.where(near_live, lead * near_lse - target[:, 0], 0.0)) / token_count
        sums = jnp.concatenate([jnp.sum(grad * hat, axis=0), jnp.sum(grad, axis=0), jnp.broadcast_to(loss, (512,))]).reshape(4, 512)
        for bits in (1, 2):
            got_sums = flip(sums, 'dp', bits)
            sums = sums + got_sums
        got_sums = [flip(sums, 'tp', k) for k in (1, 2, 3)]
        sums = (sums + got_sums[0] + (got_sums[1] + got_sums[2])).reshape(-1)

        chunks = [(0, rows // 3), (rows // 3, rows // 3), (4 * (rows // 6), rows // 6), (5 * (rows // 6), rows // 6)]
        d_embed, got = None, []
        for n, (offset, size) in enumerate(chunks):
            arrived = got[n - 2] if n >= 2 else None
            d_chunk, d_embed = call_de(idx, logits, z_pairs, tok, lab, d_embed, offset, size, arrived, chunks[n - 2][0] if n >= 2 else None)
            got.append(flip(d_chunk, 'dp', 1))
        for n in (2, 3):
            d_embed = call_place(idx, got[n], d_embed, chunks[n][0])

        return sums[2 * width], d_hidden, d_embed, sums[:width], sums[width:2 * width]


    return jax.shard_map(local_step, mesh=mesh, in_specs=(P('dp', None, None), P(None), P(None), P('tp', None), P('dp', None), P('dp', None)), out_specs=(P(), P('dp', None, None), P('tp', None), P(None), P(None)), check_vma=False)
```

profile of v0, /device:TPU:0, one launch (start us, length us, event | category | flops | bytes accessed | tf_op | source)
XLA Modules:
  0.0 395.3 jit_solution(5088071232040262035)
XLA Ops:
  2.3 2.0 fusion.4
  7.7 2.5 collective-permute-start.1
  13.6 2.3 collective-permute-start.30
  17.9 14.5 %collective-permute-done.27 = f32[256,768]{1,0:T(8,128)} collective-permute-done((f32[256,768]{1,0:T(8,128)}, f32[256,768]{1,0:T(8,128)}, u32[]{:S(2)}, u32[]{:S(2)}) %collective-permute-start.27) | collective-permute-done | bytes 786464 | tf_op jit(solution)/shard_map/ppermute | solution.py:316
  40.0 8.7 %collective-permute-done.30 = f32[256,768]{1,0:T(8,128)} collective-permute-done((f32[256,768]{1,0:T(8,128)}, f32[256,768]{1,0:T(8,128)}, u32[]{:S(2)}, u32[]{:S(2)}) %collective-permute-start.30) | collective-permute-done | bytes 786464 | tf_op jit(solution)/shard_map/ppermute | solution.py:316
  48.7 2.5 collective-permute-done.28
  52.4 4.2 %fusion.1.za_ref.zb_ref = bf16[8,256,768]{2,1,0:T(8,128)(2,1)} fusion(f32[4,256,768]{2,1,0:T(8,128)} %collective-permute-done.3, f32[4,256,768]{2,1,0:T(8,128)S(1)} %subtract_multiply_fusion, f32[768]{0:T(1024)S(1)} %copy-done.10, f32[768]{0:T(1024)S(1)} %copy-done.6), kind=kLoop, calls=%fused_computation.2 | loop fusion | flops 6291456 | bytes 9443328 | tf_op jit(solution)/shard_map/convert_element_type | solution.py:349
  56.6 23.6 %logits_near.1 = (f32[8,6288,512]{2,1,0:T(8,128)}, bf16[8,512,768]{2,1,0:T(8,128)(2,1)}, f32[4,2,512]{2,1,0:T(2,128)}) custom-call(s32[40]{0:T(128)} %concatenate.29.idx_ref, bf16[12576,768]{1,0:T(8,128)(2,1)} %e_ref.5, bf16[8,256,768]{2,1,0:T(8,128)(2,1)} %fusion.1.za_ref.zb_ref, bf16[8,256,768]{2,1,0:T(8,128)(2,1)} %fusion.1.za_ref.zb_ref), custom_call_target="tpu_custom_call" | custom-call | flops 14835253248 | bytes 38633472 | tf_op jit(solution)/shard_map/logits_near/pallas_call | solution.py:204
  82.4 3.3 collective-permute-done.5
  85.7 3.4 collective-permute-done.6
  90.6 2.4 collective-permute-done.7
  93.0 3.4 collective-permute-done.8
  98.2 3.1 collective-permute-done.9
  101.3 4.3 %collective-permute-done.10 = f32[4,2,512]{2,1,0:T(2,128)S(1)} collective-permute-done((f32[4,2,512]{2,1,0:T(2,128)}, f32[4,2,512]{2,1,0:T(2,128)S(1)}, u32[]{:S(2)}, u32[]{:S(2)}) %collective-permute-start.10) | collective-permute-done | bytes 16416 | tf_op jit(solution)/shard_map/ppermute | solution.py:319
  107.0 28.2 %dz_part.1 = (f32[4,256,768]{2,1,0:T(8,128)}, f32[4,256,768]{2,1,0:T(8,128)}, f32[4,1,512]{2,1,0:T(1,128)}, f32[8,6288,512]{2,1,0:T(8,128)}) custom-call(s32[40]{0:T(128)} %concatenate.29.idx_ref, bf16[12576,768]{1,0:T(8,128)(2,1)} %e_ref.5, f32[8,6288,512]{2,1,0:T(8,128)} %get-tuple-element.34.l_ref, ...), custom_call_target="tpu_custom_call", output_to_operand_aliasing={{3}: (2, {})} | custom-call | flops 14835253248 | bytes 38633472 | tf_op jit(solution)/shard_map/dz_part/pallas_call | solution.py:240
  144.7 2.4 add_convert_fusion.za_ref.zb_ref
  147.1 36.7 %logits_far.1 = (f32[8,6288,512]{2,1,0:T(8,128)}, bf16[8,512,768]{2,1,0:T(8,128)(2,1)}, f32[4,2,512]{2,1,0:T(2,128)}) custom-call(s32[40]{0:T(128)} %concatenate.29.idx_ref, bf16[12576,768]{1,0:T(8,128)(2,1)} %e_ref.5, bf16[8,256,768]{2,1,0:T(8,128)(2,1)} %add_convert_fusion.za_ref.zb_ref, ...), custom_call_target="tpu_custom_call", output_to_operand_aliasing={{0}: (4, {}), {1}: (5, {})} | custom-call | flops 14835253248 | bytes 38633472 | tf_op jit(solution)/shard_map/logits_far/pallas_call | solution.py:204
  194.9 22.2 %shard_map.101 = (f32[2096,768]{1,0:T(8,128)}, f32[12576,768]{1,0:T(8,128)}) custom-call(s32[40]{0:T(128)} %concatenate.29.idx_ref, f32[8,6288,512]{2,1,0:T(8,128)} %get-tuple-element.52.l_ref, bf16[8,512,768]{2,1,0:T(8,128)(2,1)} %get-tuple-element.53.z_ref, f32[8,2,512]{2,1,0:T(2,128)} %maximum_maximum_fusion.tok_ref, s32[8,1,512]{2,1,0:T(1,128)} %reshape.265.lab_ref), custom_call_target="tpu_custom_call" | custom-call | flops 8241807360 | bytes 21463040 | tf_op jit(solution)/shard_map/pallas_call | solution.py:271
  217.3 22.2 %shard_map.102 = (f32[2096,768]{1,0:T(8,128)}, f32[12576,768]{1,0:T(8,128)}) custom-call(s32[40]{0:T(128)} %concatenate.29.idx_ref, f32[8,6288,512]{2,1,0:T(8,128)} %get-tuple-element.52.l_ref, bf16[8,512,768]{2,1,0:T(8,128)(2,1)} %get-tuple-element.53.z_ref, f32[8,2,512]{2,1,0:T(2,128)} %maximum_maximum_fusion.tok_ref, ...), custom_call_target="tpu_custom_call", output_to_operand_aliasing={{1}: (5, {})} | custom-call | flops 8241807360 | bytes 21463040 | tf_op jit(solution)/shard_map/pallas_call | solution.py:271
  240.2 14.6 %collective-permute-done.11 = f32[4,256,768]{2,1,0:T(8,128)S(1)} collective-permute-done((f32[4,256,768]{2,1,0:T(8,128)}, f32[4,256,768]{2,1,0:T(8,128)S(1)}, u32[]{:S(2)}, u32[]{:S(2)}) %collective-permute-start.11) | collective-permute-done | bytes 3145760 | tf_op jit(solution)/shard_map/ppermute | solution.py:316
  254.7 2.3 add.176
  261.0 17.3 %collective-permute-done.12 = f32[2,128,768]{2,1,0:T(8,128)} collective-permute-done((f32[2,128,768]{2,1,0:T(8,128)}, f32[2,128,768]{2,1,0:T(8,128)}, u32[]{:S(2)}, u32[]{:S(2)}) %collective-permute-start.12) | collective-permute-done | bytes 786464 | tf_op jit(solution)/shard_map/ppermute | solution.py:316
  282.8 7.3 %collective-permute-done.13 = f32[128,768]{1,0:T(8,128)S(1)} collective-permute-done((f32[128,768]{1,0:T(8,128)S(1)}, f32[128,768]{1,0:T(8,128)S(1)}, u32[]{:S(2)}, u32[]{:S(2)}) %collective-permute-start.13) | collective-permute-done | bytes 393248 | tf_op jit(solution)/shard_map/ppermute | solution.py:316
  291.8 17.6 %shard_map.103 = (f32[1048,768]{1,0:T(8,128)}, f32[12576,768]{1,0:T(8,128)}) custom-call(s32[40]{0:T(128)} %concatenate.29.idx_ref, f32[8,6288,512]{2,1,0:T(8,128)} %get-tuple-element.52.l_ref, bf16[8,512,768]{2,1,0:T(8,128)(2,1)} %get-tuple-element.53.z_ref, f32[8,2,512]{2,1,0:T(2,128)} %maximum_maximum_fusion.tok_ref, ...), custom_call_target="tpu_custom_call", output_to_operand_aliasing={{1}: (6, {})} | custom-call | flops 4120903680 | bytes 10731520 | tf_op jit(solution)/shard_map/pallas_call | solution.py:271
  309.4 17.5 %shard_map.104 = (f32[1048,768]{1,0:T(8,128)}, f32[12576,768]{1,0:T(8,128)}) custom-call(s32[40]{0:T(128)} %concatenate.29.idx_ref, f32[8,6288,512]{2,1,0:T(8,128)} %get-tuple-element.52.l_ref, bf16[8,512,768]{2,1,0:T(8,128)(2,1)} %get-tuple-element.53.z_ref, f32[8,2,512]{2,1,0:T(2,128)} %maximum_maximum_fusion.tok_ref, ...), custom_call_target="tpu_custom_call", output_to_operand_aliasing={{1}: (6, {})} | custom-call | flops 4120903680 | bytes 10731520 | tf_op jit(solution)/shard_map/pallas_call | solution.py:271
  333.7 4.0 %collective-permute-done.16 = f32[4,512]{1,0:T(4,128)S(1)} collective-permute-done((f32[4,512]{1,0:T(4,128)S(1)}, f32[4,512]{1,0:T(4,128)S(1)}, u32[]{:S(2)}, u32[]{:S(2)}) %collective-permute-start.16) | collective-permute-done | bytes 8224 | tf_op jit(solution)/shard_map/ppermute | solution.py:316
  337.7 12.6 %collective-permute-start.17 = (f32[4,512]{1,0:T(4,128)S(1)}, f32[4,512]{1,0:T(4,128)S(1)}, u32[]{:S(2)}, u32[]{:S(2)}) collective-permute-start(f32[4,512]{1,0:T(4,128)S(1)} %add.188), channel_id=1, source_target_pairs={{0,2},{1,3},{2,0},{3,1},{4,6},{5,7},{6,4},{7,5},{8,10},{9,11},{10,... | collective-permute-start | bytes 24584 | tf_op jit(solution)/shard_map/ppermute | solution.py:316
  362.6 7.3 %collective-permute-done.21 = f32[128,768]{1,0:T(8,128)S(1)} collective-permute-done((f32[128,768]{1,0:T(8,128)S(1)}, f32[128,768]{1,0:T(8,128)S(1)}, u32[]{:S(2)}, u32[]{:S(2)}) %collective-permute-start.21) | collective-permute-done | bytes 393248 | tf_op jit(solution)/shard_map/ppermute | solution.py:316
  372.3 6.0 %collective-permute-done.22 = f32[128,768]{1,0:T(8,128)S(1)} collective-permute-done((f32[128,768]{1,0:T(8,128)S(1)}, f32[128,768]{1,0:T(8,128)S(1)}, u32[]{:S(2)}, u32[]{:S(2)}) %collective-permute-start.22) | collective-permute-done | bytes 393248 | tf_op jit(solution)/shard_map/ppermute | solution.py:316
  378.4 5.3 %collective-permute-done.26 = f32[128,768]{1,0:T(8,128)S(1)} collective-permute-done((f32[128,768]{1,0:T(8,128)S(1)}, f32[128,768]{1,0:T(8,128)S(1)}, u32[]{:S(2)}, u32[]{:S(2)}) %collective-permute-start.26) | collective-permute-done | bytes 393248 | tf_op jit(solution)/shard_map/ppermute | solution.py:316
  386.5 4.3 %place.2.de_ref = f32[12576,768]{1,0:T(8,128)} custom-call(s32[40]{0:T(128)} %concatenate.29.idx_ref, f32[1048,768]{1,0:T(8,128)} %collective-permute-done.45.got_ref, f32[12576,768]{1,0:T(8,128)} %get-tuple-element.62.de_ref), custom_call_target="tpu_custom_call", output_to_operand_aliasing={{}: (2, {})} | custom-call | tf_op jit(solution)/shard_map/place/pallas_call | solution.py:289
  390.8 4.3 %place.3 = f32[12576,768]{1,0:T(8,128)} custom-call(s32[40]{0:T(128)} %concatenate.29.idx_ref, f32[1048,768]{1,0:T(8,128)} %collective-permute-done.44.got_ref, f32[12576,768]{1,0:T(8,128)} %place.2.de_ref), custom_call_target="tpu_custom_call", output_to_operand_aliasing={{}: (2, {})} | custom-call | tf_op jit(solution)/shard_map/place/pallas_call | solution.py:289
  (202 shorter events, 78.4 us)
Async XLA Ops:
  6.9 45.5 %collective-permute-start.3 = (f32[4,256,768]{2,1,0:T(8,128)S(1)}, f32[4,256,768]{2,1,0:T(8,128)}, u32[]{:S(2)}, u32[]{:S(2)}) collective-permute-start(f32[4,256,768]{2,1,0:T(8,128)S(1)} %subtract_multiply_fusion), channel_id=1, source_target_pairs={{0,1},{1,0},{2,3},{3,2},{4,5},{5,4},{6,7},{7,6},{8,9},{9,8},{10,11... | collective-permute-start | bytes 9437192 | tf_op jit(solution)/shard_map/ppermute | solution.py:316
  7.7 8.3 %collective-permute-start.1 = (s32[1024]{0:T(1024)S(1)}, s32[1024]{0:T(1024)S(1)}, u32[]{:S(2)}, u32[]{:S(2)}) collective-permute-start(s32[1024]{0:T(1024)S(1)} %bitcast.141), channel_id=1, source_target_pairs={{0,2},{1,3},{2,0},{3,1},{4,6},{5,7},{6,4},{7,5},{8,10},{9,11},{10,... | collective-permute-start | bytes 12296 | tf_op jit(solution)/shard_map/ppermute | solution.py:316
  10.2 5.7 %collective-permute-start.2 = (s32[1024]{0:T(1024)S(1)}, s32[1024]{0:T(1024)S(1)}, u32[]{:S(2)}, u32[]{:S(2)}) collective-permute-start(s32[1024]{0:T(1024)S(1)} %bitcast.142), channel_id=1, source_target_pairs={{0,3},{1,2},{2,1},{3,0},{4,7},{5,6},{6,5},{7,4},{8,11},{9,10},{10,... | collective-permute-start | bytes 12296 | tf_op jit(solution)/shard_map/ppermute | solution.py:316
  11.7 20.7 %collective-permute-start.27 = (f32[256,768]{1,0:T(8,128)}, f32[256,768]{1,0:T(8,128)}, u32[]{:S(2)}, u32[]{:S(2)}) collective-permute-start(f32[256,768]{1,0:T(8,128)} %get-tuple-element.38), channel_id=1, source_target_pairs={{0,2},{1,3},{2,0},{3,1},{4,6},{5,7},{6,4},{7,5},{8,10},{9,11},{10,... | collective-permute-start | bytes 2359304 | tf_op jit(solution)/shard_map/ppermute | solution.py:316
  13.6 35.1 %collective-permute-start.30 = (f32[256,768]{1,0:T(8,128)}, f32[256,768]{1,0:T(8,128)}, u32[]{:S(2)}, u32[]{:S(2)}) collective-permute-start(f32[256,768]{1,0:T(8,128)} %get-tuple-element.40), channel_id=1, source_target_pairs={{0,2},{1,3},{2,0},{3,1},{4,6},{5,7},{6,4},{7,5},{8,10},{9,11},{10,... | collective-permute-start | bytes 2359304 | tf_op jit(solution)/shard_map/ppermute | solution.py:316
  32.4 18.8 %collective-permute-start.28 = (f32[256,768]{1,0:T(8,128)}, f32[256,768]{1,0:T(8,128)}, u32[]{:S(2)}, u32[]{:S(2)}) collective-permute-start(f32[256,768]{1,0:T(8,128)} %collective-permute-done.27), channel_id=1, source_target_pairs={{0,4},{4,0},{8,12},{12,8},{1,5},{5,1},{9,13},{13,9},{2,6},{6,2},{1... | collective-permute-start | bytes 2359304 | tf_op jit(solution)/shard_map/ppermute | solution.py:316
  34.4 18.0 %collective-permute-start.29 = (f32[256,768]{1,0:T(8,128)}, f32[256,768]{1,0:T(8,128)}, u32[]{:S(2)}, u32[]{:S(2)}) collective-permute-start(f32[256,768]{1,0:T(8,128)} %collective-permute-done.27), channel_id=1, source_target_pairs={{0,8},{4,12},{8,0},{12,4},{1,9},{5,13},{9,1},{13,5},{2,10},{6,14},... | collective-permute-start | bytes 2359304 | tf_op jit(solution)/shard_map/ppermute | solution.py:316
  40.0 95.1 %collective-permute-start.31 = (f32[256,768]{1,0:T(8,128)}, f32[256,768]{1,0:T(8,128)}, u32[]{:S(2)}, u32[]{:S(2)}) collective-permute-start(f32[256,768]{1,0:T(8,128)} %collective-permute-done.27), channel_id=1, source_target_pairs={{0,1},{1,0},{2,3},{3,2},{4,5},{5,4},{6,7},{7,6},{8,9},{9,8},{10,11... | collective-permute-start | bytes 2359304 | tf_op jit(solution)/shard_map/ppermute | solution.py:316
  48.7 86.5 %collective-permute-start.34 = (f32[256,768]{1,0:T(8,128)}, f32[256,768]{1,0:T(8,128)}, u32[]{:S(2)}, u32[]{:S(2)}) collective-permute-start(f32[256,768]{1,0:T(8,128)} %collective-permute-done.30), channel_id=1, source_target_pairs={{0,1},{1,0},{2,3},{3,2},{4,5},{5,4},{6,7},{7,6},{8,9},{9,8},{10,11... | collective-permute-start | bytes 2359304 | tf_op jit(solution)/shard_map/ppermute | solution.py:316
  51.2 84.0 %collective-permute-start.32 = (f32[256,768]{1,0:T(8,128)}, f32[256,768]{1,0:T(8,128)}, u32[]{:S(2)}, u32[]{:S(2)}) collective-permute-start(f32[256,768]{1,0:T(8,128)} %collective-permute-done.28), channel_id=1, source_target_pairs={{0,1},{1,0},{2,3},{3,2},{4,5},{5,4},{6,7},{7,6},{8,9},{9,8},{10,11... | collective-permute-start | bytes 2359304 | tf_op jit(solution)/shard_map/ppermute | solution.py:316
  52.4 82.8 %collective-permute-start.33 = (f32[256,768]{1,0:T(8,128)}, f32[256,768]{1,0:T(8,128)}, u32[]{:S(2)}, u32[]{:S(2)}) collective-permute-start(f32[256,768]{1,0:T(8,128)} %collective-permute-done.29), channel_id=1, source_target_pairs={{0,1},{1,0},{2,3},{3,2},{4,5},{5,4},{6,7},{7,6},{8,9},{9,8},{10,11... | collective-permute-start | bytes 2359304 | tf_op jit(solution)/shard_map/ppermute | solution.py:316
  96.4 4.8 %collective-permute-start.9 = (f32[4,2,512]{2,1,0:T(2,128)}, f32[4,2,512]{2,1,0:T(2,128)S(1)}, u32[]{:S(2)}, u32[]{:S(2)}) collective-permute-start(f32[4,2,512]{2,1,0:T(2,128)} %get-tuple-element.35), channel_id=1, source_target_pairs={{0,12},{1,13},{2,14},{3,15},{4,8},{5,9},{6,10},{7,11},{8,4},{9,5},... | collective-permute-start | bytes 49160 | tf_op jit(solution)/shard_map/ppermute | solution.py:319
  184.5 5.2 %collective-permute-start.36 = (f32[4,2,512]{2,1,0:T(2,128)}, f32[4,2,512]{2,1,0:T(2,128)S(1)}, u32[]{:S(2)}, u32[]{:S(2)}) collective-permute-start(f32[4,2,512]{2,1,0:T(2,128)} %get-tuple-element.54), channel_id=1, source_target_pairs={{0,4},{1,5},{2,6},{3,7},{4,0},{5,1},{6,2},{7,3},{8,12},{9,13},{10,... | collective-permute-start | bytes 49160 | tf_op jit(solution)/shard_map/ppermute | solution.py:319
  185.4 5.4 %collective-permute-start.37 = (f32[4,2,512]{2,1,0:T(2,128)}, f32[4,2,512]{2,1,0:T(2,128)S(1)}, u32[]{:S(2)}, u32[]{:S(2)}) collective-permute-start(f32[4,2,512]{2,1,0:T(2,128)} %get-tuple-element.54), channel_id=1, source_target_pairs={{0,5},{1,4},{2,7},{3,6},{4,1},{5,0},{6,3},{7,2},{8,13},{9,12},{10,... | collective-permute-start | bytes 49160 | tf_op jit(solution)/shard_map/ppermute | solution.py:319
  188.0 4.8 %collective-permute-start.40 = (f32[4,2,512]{2,1,0:T(2,128)}, f32[4,2,512]{2,1,0:T(2,128)S(1)}, u32[]{:S(2)}, u32[]{:S(2)}) collective-permute-start(f32[4,2,512]{2,1,0:T(2,128)} %get-tuple-element.54), channel_id=1, source_target_pairs={{0,12},{1,13},{2,14},{3,15},{4,8},{5,9},{6,10},{7,11},{8,4},{9,5},... | collective-permute-start | bytes 49160 | tf_op jit(solution)/shard_map/ppermute | solution.py:319
  217.1 74.7 %collective-permute-start.43 = (f32[2096,768]{1,0:T(8,128)}, f32[2096,768]{1,0:T(8,128)}, u32[]{:S(2)}, u32[]{:S(2)}) collective-permute-start(f32[2096,768]{1,0:T(8,128)} %get-tuple-element.57), channel_id=1, source_target_pairs={{0,1},{1,0},{2,3},{3,2},{4,5},{5,4},{6,7},{7,6},{8,9},{9,8},{10,11... | collective-permute-start | bytes 19316744 | tf_op jit(solution)/shard_map/ppermute | solution.py:316
  239.6 69.8 %collective-permute-start.42 = (f32[2096,768]{1,0:T(8,128)}, f32[2096,768]{1,0:T(8,128)}, u32[]{:S(2)}, u32[]{:S(2)}) collective-permute-start(f32[2096,768]{1,0:T(8,128)} %get-tuple-element.56), channel_id=1, source_target_pairs={{0,1},{1,0},{2,3},{3,2},{4,5},{5,4},{6,7},{7,6},{8,9},{9,8},{10,11... | collective-permute-start | bytes 19316744 | tf_op jit(solution)/shard_map/ppermute | solution.py:316
  239.9 14.8 %collective-permute-start.11 = (f32[4,256,768]{2,1,0:T(8,128)}, f32[4,256,768]{2,1,0:T(8,128)S(1)}, u32[]{:S(2)}, u32[]{:S(2)}) collective-permute-start(f32[4,256,768]{2,1,0:T(8,128)} %get-tuple-element.37), channel_id=1, source_target_pairs={{0,1},{1,0},{2,3},{3,2},{4,5},{5,4},{6,7},{7,6},{8,9},{9,8},{10,11... | collective-permute-start | bytes 9437192 | tf_op jit(solution)/shard_map/ppermute | solution.py:316
  258.3 20.0 %collective-permute-start.12 = (f32[2,128,768]{2,1,0:T(8,128)}, f32[2,128,768]{2,1,0:T(8,128)}, u32[]{:S(2)}, u32[]{:S(2)}) collective-permute-start(f32[2,128,768]{2,1,0:T(8,128)} %dynamic-slice_bitcast_fusion.3), channel_id=1, source_target_pairs={{0,4},{4,0},{8,12},{12,8},{1,5},{5,1},{9,13},{13,9},{2,6},{6,2},{1... | collective-permute-start | bytes 2359304 | tf_op jit(solution)/shard_map/ppermute | solution.py:316
  260.5 19.8 %collective-permute-start.14 = (f32[2,128,768]{2,1,0:T(8,128)}, f32[2,128,768]{2,1,0:T(8,128)}, u32[]{:S(2)}, u32[]{:S(2)}) collective-permute-start(f32[2,128,768]{2,1,0:T(8,128)} %dynamic-slice_bitcast_fusion.2), channel_id=1, source_target_pairs={{0,8},{4,12},{8,0},{12,4},{1,9},{5,13},{9,1},{13,5},{2,10},{6,14},... | collective-permute-start | bytes 2359304 | tf_op jit(solution)/shard_map/ppermute | solution.py:316
  279.6 10.5 %collective-permute-start.13 = (f32[128,768]{1,0:T(8,128)S(1)}, f32[128,768]{1,0:T(8,128)S(1)}, u32[]{:S(2)}, u32[]{:S(2)}) collective-permute-start(f32[128,768]{1,0:T(8,128)S(1)} %dynamic-slice_bitcast_fusion.5), channel_id=1, source_target_pairs={{0,8},{4,12},{8,0},{12,4},{1,9},{5,13},{9,1},{13,5},{2,10},{6,14},... | collective-permute-start | bytes 1179656 | tf_op jit(solution)/shard_map/ppermute | solution.py:316
  281.5 10.2 %collective-permute-start.15 = (f32[128,768]{1,0:T(8,128)S(1)}, f32[128,768]{1,0:T(8,128)S(1)}, u32[]{:S(2)}, u32[]{:S(2)}) collective-permute-start(f32[128,768]{1,0:T(8,128)S(1)} %dynamic-slice_bitcast_fusion.4), channel_id=1, source_target_pairs={{0,4},{4,0},{8,12},{12,8},{1,5},{5,1},{9,13},{13,9},{2,6},{6,2},{1... | collective-permute-start | bytes 1179656 | tf_op jit(solution)/shard_map/ppermute | solution.py:316
  326.9 63.8 %collective-permute-start.44 = (f32[1048,768]{1,0:T(8,128)}, f32[1048,768]{1,0:T(8,128)}, u32[]{:S(2)}, u32[]{:S(2)}) collective-permute-start(f32[1048,768]{1,0:T(8,128)} %get-tuple-element.60), channel_id=1, source_target_pairs={{0,1},{1,0},{2,3},{3,2},{4,5},{5,4},{6,7},{7,6},{8,9},{9,8},{10,11... | collective-permute-start | bytes 9658376 | tf_op jit(solution)/shard_map/ppermute | solution.py:316
  327.0 59.5 %collective-permute-start.45 = (f32[1048,768]{1,0:T(8,128)}, f32[1048,768]{1,0:T(8,128)}, u32[]{:S(2)}, u32[]{:S(2)}) collective-permute-start(f32[1048,768]{1,0:T(8,128)} %get-tuple-element.61), channel_id=1, source_target_pairs={{0,1},{1,0},{2,3},{3,2},{4,5},{5,4},{6,7},{7,6},{8,9},{9,8},{10,11... | collective-permute-start | bytes 9658376 | tf_op jit(solution)/shard_map/ppermute | solution.py:316
  330.3 30.5 %collective-permute-start.24 = (f32[128,768]{1,0:T(8,128)S(1)}, f32[128,768]{1,0:T(8,128)S(1)}, u32[]{:S(2)}, u32[]{:S(2)}) collective-permute-start(f32[128,768]{1,0:T(8,128)S(1)} %get-tuple-element.81), channel_id=1, source_target_pairs={{0,8},{4,12},{8,0},{12,4},{1,9},{5,13},{9,1},{13,5},{2,10},{6,14},... | collective-permute-start | bytes 1179656 | tf_op jit(solution)/shard_map/ppermute | solution.py:316
  337.7 14.3 %collective-permute-start.17 = (f32[4,512]{1,0:T(4,128)S(1)}, f32[4,512]{1,0:T(4,128)S(1)}, u32[]{:S(2)}, u32[]{:S(2)}) collective-permute-start(f32[4,512]{1,0:T(4,128)S(1)} %add.188), channel_id=1, source_target_pairs={{0,2},{1,3},{2,0},{3,1},{4,6},{5,7},{6,4},{7,5},{8,10},{9,11},{10,... | collective-permute-start | bytes 24584 | tf_op jit(solution)/shard_map/ppermute | solution.py:316
  353.3 4.5 %collective-permute-start.20 = (f32[4,512]{1,0:T(4,128)S(1)}, f32[4,512]{1,0:T(4,128)S(1)}, u32[]{:S(2)}, u32[]{:S(2)}) collective-permute-start(f32[4,512]{1,0:T(4,128)S(1)} %add.189), channel_id=1, source_target_pairs={{0,12},{4,8},{8,4},{12,0},{1,13},{5,9},{9,5},{13,1},{2,14},{6,10},... | collective-permute-start | bytes 24584 | tf_op jit(solution)/shard_map/ppermute | solution.py:316
  357.9 12.0 %collective-permute-start.21 = (f32[128,768]{1,0:T(8,128)S(1)}, f32[128,768]{1,0:T(8,128)S(1)}, u32[]{:S(2)}, u32[]{:S(2)}) collective-permute-start(f32[128,768]{1,0:T(8,128)S(1)} %get-tuple-element.80), channel_id=1, source_target_pairs={{0,4},{4,0},{8,12},{12,8},{1,5},{5,1},{9,13},{13,9},{2,6},{6,2},{1... | collective-permute-start | bytes 1179656 | tf_op jit(solution)/shard_map/ppermute | solution.py:316
  359.4 11.8 %collective-permute-start.23 = (f32[128,768]{1,0:T(8,128)S(1)}, f32[128,768]{1,0:T(8,128)S(1)}, u32[]{:S(2)}, u32[]{:S(2)}) collective-permute-start(f32[128,768]{1,0:T(8,128)S(1)} %get-tuple-element.80), channel_id=1, source_target_pairs={{0,8},{4,12},{8,0},{12,4},{1,9},{5,13},{9,1},{13,5},{2,10},{6,14},... | collective-permute-start | bytes 1179656 | tf_op jit(solution)/shard_map/ppermute | solution.py:316
  360.7 17.6 %collective-permute-start.22 = (f32[128,768]{1,0:T(8,128)S(1)}, f32[128,768]{1,0:T(8,128)S(1)}, u32[]{:S(2)}, u32[]{:S(2)}) collective-permute-start(f32[128,768]{1,0:T(8,128)S(1)} %get-tuple-element.81), channel_id=1, source_target_pairs={{0,4},{4,0},{8,12},{12,8},{1,5},{5,1},{9,13},{13,9},{2,6},{6,2},{1... | collective-permute-start | bytes 1179656 | tf_op jit(solution)/shard_map/ppermute | solution.py:316
  369.9 13.8 %collective-permute-start.26 = (f32[128,768]{1,0:T(8,128)S(1)}, f32[128,768]{1,0:T(8,128)S(1)}, u32[]{:S(2)}, u32[]{:S(2)}) collective-permute-start(f32[128,768]{1,0:T(8,128)S(1)} %collective-permute-done.24), channel_id=1, source_target_pairs={{0,4},{4,0},{8,12},{12,8},{1,5},{5,1},{9,13},{13,9},{2,6},{6,2},{1... | collective-permute-start | bytes 1179656 | tf_op jit(solution)/shard_map/ppermute | solution.py:316
  371.2 12.5 %collective-permute-start.25 = (f32[128,768]{1,0:T(8,128)S(1)}, f32[128,768]{1,0:T(8,128)S(1)}, u32[]{:S(2)}, u32[]{:S(2)}) collective-permute-start(f32[128,768]{1,0:T(8,128)S(1)} %collective-permute-done.21), channel_id=1, source_target_pairs={{0,8},{4,12},{8,0},{12,4},{1,9},{5,13},{9,1},{13,5},{2,10},{6,14},... | collective-permute-start | bytes 1179656 | tf_op jit(solution)/shard_map/ppermute | solution.py:316
  (28 other events, 354.4 us)
where the time goes:
time: 397 us; the launch traced here: 395 us
  Pallas kernels  176 us (44%)
  waiting for transfers between devices  117 us (29%)
  starting transfers between devices  50.4 us (13%)
  other arithmetic  27.4 us (7%)
  local copies, waits for them, and re-layouts  19.6 us (5%)
  between operations  4.74 us (1%)
    ppermute x32, waiting for transfers between devices, flip(): return lax.ppermute(x, axis, [(k, k ^ bits) for k in range(n)])  93.4 us
    pallas_call x4, Pallas kernels, call_de(): pl.pallas_call(functools.partial(de_kernel, offset, rows, got_offset if g...  79.5 us
    pallas_call x2, Pallas kernels, call_logits(): pl.pallas_call(functools.partial(logits_kernel, count), grid_spec=spec, o...  60.2 us
    ppermute x32, starting transfers between devices, flip(): return lax.ppermute(x, axis, [(k, k ^ bits) for k in range(n)])  39.7 us
    pallas_call x1, Pallas kernels, call_dz(): pl.pallas_call(dz_kernel, grid_spec=spec, out_shape=[half, half, jax.Shap...  28.2 us
    ppermute x14, waiting for transfers between devices, flip_both(): lax.ppermute(x, ('tp', 'dp'), [(k, (k // n_dp ^ tp_bits) * n_dp + (k % n_...  23.4 us
    unnamed x50, local copies, waits for them, and re-layouts  11.4 us
    ppermute x14, starting transfers between devices, flip_both(): lax.ppermute(x, ('tp', 'dp'), [(k, (k // n_dp ^ tp_bits) * n_dp + (k % n_...  10.7 us
  transfers between devices with their start and end apart: 46, of which 26 were waited for; matrix products, arithmetic and copies ran while one was open for 7% of the time, Pallas kernels for 24%

commit v1 on v0

--- a/solution.py
+++ b/solution.py
@@ -13,6 +13,7 @@
 PAIR = 2 * BLOCK
 BIG = 1e30
 VMEM_LIMIT = 62 * 1024 * 1024
+DE_VMEM = 28 * 1024 * 1024
 
 
 CORE, NEAR_PAIRS, FAR_PAIRS, ALL_PAIRS, ROW_START = 0, 1, 2, 3, 4
@@ -27,14 +28,34 @@
     return jnp.minimum(i, count - 1)
 
 
-def logits_kernel(count, idx_ref, e_ref, za_ref, zb_ref, *rest):
-    l_ref, zc_ref, st_ref = rest[-3:]
-    pl.when(pl.program_id(0) < idx_ref[count])(lambda: logits_step(e_ref, za_ref, zb_ref, l_ref, zc_ref, st_ref))
-
-
-def logits_step(e_ref, za_ref, zb_ref, l_ref, zc_ref, st_ref):
-    zc_ref[0, :BLOCK, :] = za_ref[0]
-    zc_ref[0, BLOCK:, :] = zb_ref[0]
+def logits_kernel(count, order, n_pieces, idx_ref, e_ref, gamma_ref, beta_ref, *rest):
+    pieces = rest[:n_pieces]
+    l_ref, zc_ref, st_ref, x_ref, sem = rest[-5:]
+    i = pl.program_id(0)
+
+    def copies(block, slot, h):
+        target = x_ref.at[slot, pl.ds(h * BLOCK, BLOCK), :]
+        if len(pieces[0].shape) == 3:
+            return [(block >> 2 == k, pltpu.make_async_copy(ref.at[block & 3], target, sem.at[slot, h])) for k, ref in enumerate(pieces)]
+        return [(block == k, pltpu.make_async_copy(ref, target, sem.at[slot, h])) for k, ref in enumerate(pieces)]
+
+    def fetch(pair):
+        for h in range(2):
+            for chosen, copy in copies(idx_ref[order + 2 * pair + h], pair % 2, h):
+                pl.when(chosen)(copy.start)
+
+    pl.when(i == 0)(lambda: fetch(0))
+    pl.when(i + 1 < idx_ref[count])(lambda: fetch(i + 1))
+
+    @pl.when(i < idx_ref[count])
+    def _():
+        for h in range(2):
+            copies(0, i % 2, h)[0][1].wait()
+        zc_ref[0] = (x_ref[i % 2] * gamma_ref[...] + beta_ref[...]).astype(jnp.bfloat16)
+        logits_step(e_ref, l_ref, zc_ref, st_ref)
+
+
+def logits_step(e_ref, l_ref, zc_ref, st_ref):
     rows = e_ref.shape[0]
     size = 528
 
@@ -182,7 +203,7 @@
 ANY = pl.BlockSpec(memory_space=pl.ANY)
 
 
-def call_logits(idx, e, z, previous, rows):
+def call_logits(idx, e, gamma, beta, pieces, previous, rows):
     pairs = 8
     base, count, order = (0, NEAR_PAIRS, NEAR_PIECES) if previous is None else (4, FAR_PAIRS, FAR_PIECES)
     width = e.shape[1]
@@ -190,30 +211,29 @@
     spec = pltpu.PrefetchScalarGridSpec(
         num_scalar_prefetch=1,
         grid=(4,),
-        in_specs=[
-            pl.BlockSpec((rows, width), lambda i, s: (s[CORE], 0), pipeline_mode=pl.Buffered(1)),
-            pl.BlockSpec((1, BLOCK, width), lambda i, s: (s[order + 2 * last(i, s[count])], 0, 0)),
-            pl.BlockSpec((1, BLOCK, width), lambda i, s: (s[order + 1 + 2 * last(i, s[count])], 0, 0)),
-        ] + [ANY] * len(extra),
+        in_specs=[pl.BlockSpec((rows, width), lambda i, s: (s[CORE], 0), pipeline_mode=pl.Buffered(1))]
+        + [pl.BlockSpec((1, width), lambda i, s: (0, 0))] * 2 + [ANY] * (len(pieces) + len(extra)),
         out_specs=[
             pl.BlockSpec((1, rows, PAIR), lambda i, s: (base + last(i, s[count]), 0, 0)),
             pl.BlockSpec((1, PAIR, width), lambda i, s: (base + last(i, s[count]), 0, 0)),
             pl.BlockSpec((1, 2, PAIR), lambda i, s: (last(i, s[count]), 0, 0)),
         ],
+        scratch_shapes=[pltpu.VMEM((2, PAIR, width), jnp.float32), pltpu.SemaphoreType.DMA((2, 2))],
     )
+    first = 4 + len(pieces)
     return pl.pallas_call(
-        functools.partial(logits_kernel, count),
+        functools.partial(logits_kernel, count, order, len(pieces)),
         grid_spec=spec,
         out_shape=[
             jax.ShapeDtypeStruct((pairs, rows, PAIR), jnp.float32),
             jax.ShapeDtypeStruct((pairs, PAIR, width), jnp.bfloat16),
             jax.ShapeDtypeStruct((4, 2, PAIR), jnp.float32),
         ],
-        input_output_aliases={} if previous is None else {4: 0, 5: 1},
+        input_output_aliases={} if previous is None else {first: 0, first + 1: 1},
         compiler_params=params(),
         cost_estimate=cost(3, rows, width),
         name="logits_near" if previous is None else "logits_far",
-    )(idx, e, z, z, *extra)
+    )(idx, e, gamma[None], beta[None], *pieces, *extra)
 
 
 def call_dz(idx, e, l, tok, lab):
@@ -273,7 +293,7 @@
         grid_spec=spec,
         out_shape=[jax.ShapeDtypeStruct((rows, width), jnp.float32), jax.ShapeDtypeStruct((2 * total, width), jnp.float32)],
         input_output_aliases={} if de is None else {4 + len(extra): 1},
-        compiler_params=params(),
+        compiler_params=params(DE_VMEM),
         cost_estimate=cost(5, rows, width),
     )(idx, l, zc, tok, lab, *extra)
 
@@ -291,7 +311,7 @@
         grid_spec=spec,
         out_shape=jax.ShapeDtypeStruct(de.shape, de.dtype),
         input_output_aliases={2: 0},
-        compiler_params=params(),
+        compiler_params=params(DE_VMEM),
         name="place",
     )(idx, got, de)
 
@@ -345,9 +365,6 @@
         inv_std = lax.rsqrt(jnp.mean(centered * centered, axis=-1, keepdims=True) + LAYER_EPS)
         x_hat = (centered * inv_std).reshape(quarters, BLOCK, width)
 
-        def to_z(values):
-            return (values * ln_gamma + ln_beta).astype(jnp.bfloat16)
-
         mate = flip(x_hat, 'dp', 1)
         own_quarter, far_quarter = lax.optimization_barrier((pick(x_hat, tp), pick(x_hat, tp ^ 3)))
         far0, far3 = flip(own_quarter, 'dp', 2), flip(far_quarter, 'dp', 2)
@@ -363,8 +380,7 @@
         scalars = jnp.stack([core, pairs[0], pairs[1], pairs[0] + pairs[1], row_start, zero, zero, zero])
         idx = jnp.concatenate([scalars, order[0], order[0] ^ (core * 4), order[1] ^ (core * 4 + tp), pair_idx])
 
-        near_z = to_z(jnp.concatenate([x_hat, mate]))
-        logits, z_pairs, near_stats = call_logits(idx, embed_shard, near_z, None, rows)
+        logits, z_pairs, near_stats = call_logits(idx, embed_shard, ln_gamma, ln_beta, [x_hat, mate], None, rows)
 
         def combine(every, labels_here):
             top = jnp.max(every[:, :, 0], axis=0)
@@ -387,9 +403,8 @@
         a_keep = lax.dynamic_index_in_dim(a_part, y, 1, keepdims=False) + a_got
         b_keep = pick(b_part, z) + b_got
 
-        pieces, logits = lax.optimization_barrier(([far0, far1, far2, far3, mate0, mate1, mate2, mate3], logits))
-        far_z = to_z(jnp.stack(pieces))
-        logits, z_pairs, far_stats = call_logits(idx, embed_shard, far_z, (logits, z_pairs), rows)
+        pieces = [far0, far1, far2, far3, mate0, mate1, mate2, mate3]
+        logits, z_pairs, far_stats = call_logits(idx, embed_shard, ln_gamma, ln_beta, pieces, (logits, z_pairs), rows)
         far_tok, _, _ = combine(from_group(far_stats), lab[4:])
         a_grad = flip(pick(a_keep, 1 - z), 'tp', 2)
         b_grad = flip(pick(b_keep, 1 - y), 'tp', 1)
@@ -416,13 +431,13 @@
         got_sums = [flip(sums, 'tp', k) for k in (1, 2, 3)]
         sums = (sums + got_sums[0] + (got_sums[1] + got_sums[2])).reshape(-1)
 
-        chunks = [(0, rows // 3), (rows // 3, rows // 3), (4 * (rows // 6), rows // 6), (5 * (rows // 6), rows // 6)]
+        chunks = [(k * (rows // 6), rows // 6) for k in range(6)]
         d_embed, got = None, []
         for n, (offset, size) in enumerate(chunks):
             arrived = got[n - 2] if n >= 2 else None
             d_chunk, d_embed = call_de(idx, logits, z_pairs, tok, lab, d_embed, offset, size, arrived, chunks[n - 2][0] if n >= 2 else None)
             got.append(flip(d_chunk, 'dp', 1))
-        for n in (2, 3):
+        for n in (4, 5):
             d_embed = call_place(idx, got[n], d_embed, chunks[n][0])
 
         return sums[2 * width], d_hidden, d_embed, sums[:width], sums[width:2 * width]

time: 397 us -> 380 us (0.957)
  waiting for transfers between devices: 117 us -> 101 us
  local copies, waits for them, and re-layouts: 19.6 us -> 24.4 us
  other arithmetic: 27.4 us -> 22.7 us
    ppermute x32 -> x34, waiting for transfers between devices: 93.4 us -> 78.1 us  [flip(): return lax.ppermute(x, axis, [(k, k ^ bits) for k in range(n)])]
    convert_element_type x2 -> x0, other arithmetic: 6.58 us -> none  [to_z(): return (values * ln_gamma + ln_beta).astype(jnp.bfloat16)]
    ppermute x32 -> x34, starting transfers between devices: 39.7 us -> 37.5 us  [flip(): return lax.ppermute(x, axis, [(k, k ^ bits) for k in range(n)])]
    unnamed x50 -> x69, local copies, waits for them, and re-layouts: 11.4 us -> 10.9 us
    pallas_call x4 -> x6, Pallas kernels: 79.5 us -> 80 us  [call_de(): pl.pallas_call(functools.partial(de_kernel, offset, rows, got_offset if g...]
  transfers between devices with their start and end apart: 46 -> 48, of which waited for: 26 -> 26; matrix products, arithmetic and copies ran while one was open for 7% -> 8% of each run, Pallas kernels for 24% -> 29%
where the time goes in v1:
time: 380 us; the launch traced here: 379 us
  Pallas kernels  177 us (47%)
  waiting for transfers between devices  101 us (27%)
  starting transfers between devices  48.4 us (13%)
  local copies, waits for them, and re-layouts  24.4 us (6%)
  other arithmetic  22.7 us (6%)
  between operations  4.64 us (1%)
    pallas_call x6, Pallas kernels, call_de(): pl.pallas_call(functools.partial(de_kernel, offset, rows, got_offset if g...  80 us
    ppermute x34, waiting for transfers between devices, flip(): return lax.ppermute(x, axis, [(k, k ^ bits) for k in range(n)])  78.1 us
    pallas_call x2, Pallas kernels, call_logits(): pl.pallas_call(functools.partial(logits_kernel, count, order, len(pieces)...  62.8 us
    ppermute x34, starting transfers between devices, flip(): return lax.ppermute(x, axis, [(k, k ^ bits) for k in range(n)])  37.5 us
    pallas_call x1, Pallas kernels, call_dz(): pl.pallas_call(dz_kernel, grid_spec=spec, out_shape=[half, half, jax.Shap...  28.2 us
    ppermute x14, waiting for transfers between devices, flip_both(): lax.ppermute(x, ('tp', 'dp'), [(k, (k // n_dp ^ tp_bits) * n_dp + (k % n_...  23.2 us
    unnamed x69, local copies, waits for them, and re-layouts  10.9 us
    ppermute x14, starting transfers between devices, flip_both(): lax.ppermute(x, ('tp', 'dp'), [(k, (k // n_dp ^ tp_bits) * n_dp + (k % n_...  10.9 us
  transfers between devices with their start and end apart: 48, of which 26 were waited for; matrix products, arithmetic and copies ran while one was open for 8% of the time, Pallas kernels for 29%

profile of v1, /device:TPU:0, one launch (start us, length us, event | category | flops | bytes accessed | tf_op | source)
XLA Modules:
  0.0 378.8 jit_solution(13752893537196198894)
XLA Ops:
  8.0 2.5 collective-permute-start.1
  10.7 2.4 dynamic-slice_bitcast_fusion
  17.9 15.6 %collective-permute-done.27.rest_0_ = f32[256,768]{1,0:T(8,128)S(1)} collective-permute-done((f32[256,768]{1,0:T(8,128)S(1)}, f32[256,768]{1,0:T(8,128)S(1)}, u32[]{:S(2)}, u32[]{:S(2)}) %collective-permute-start.27) | collective-permute-done | bytes 786464 | tf_op jit(solution)/shard_map/ppermute | solution.py:336
  40.9 8.9 %collective-permute-done.30.rest_3_ = f32[256,768]{1,0:T(8,128)S(1)} collective-permute-done((f32[256,768]{1,0:T(8,128)}, f32[256,768]{1,0:T(8,128)S(1)}, u32[]{:S(2)}, u32[]{:S(2)}) %collective-permute-start.30) | collective-permute-done | bytes 786464 | tf_op jit(solution)/shard_map/ppermute | solution.py:336
  49.8 2.3 collective-permute-done.28.rest_1_
  53.4 24.7 %logits_near.1 = (f32[8,6288,512]{2,1,0:T(8,128)}, bf16[8,512,768]{2,1,0:T(8,128)(2,1)}, f32[4,2,512]{2,1,0:T(2,128)}) custom-call(s32[40]{0:T(128)} %concatenate.26.idx_ref, bf16[12576,768]{1,0:T(8,128)(2,1)} %e_ref.5, f32[1,768]{1,0:T(1,128)} %broadcast_in_dim.83.gamma_ref, f32[1,768]{1,0:T(1,128)} %broadcast_in_dim.84.beta_ref, ...), custom_call_target="tpu_custom_call" | custom-call | flops 14835253248 | bytes 38633472 | tf_op jit(solution)/shard_map/logits_near/pallas_call | solution.py:224
  80.3 3.3 collective-permute-done.5
  83.5 3.4 collective-permute-done.6
  88.5 2.3 collective-permute-done.7
  90.9 3.4 collective-permute-done.8
  96.1 3.0 collective-permute-done.9
  99.1 4.3 %collective-permute-done.10 = f32[4,2,512]{2,1,0:T(2,128)S(1)} collective-permute-done((f32[4,2,512]{2,1,0:T(2,128)}, f32[4,2,512]{2,1,0:T(2,128)S(1)}, u32[]{:S(2)}, u32[]{:S(2)}) %collective-permute-start.10) | collective-permute-done | bytes 16416 | tf_op jit(solution)/shard_map/ppermute | solution.py:339
  104.8 28.2 %dz_part.1 = (f32[4,256,768]{2,1,0:T(8,128)}, f32[4,256,768]{2,1,0:T(8,128)}, f32[4,1,512]{2,1,0:T(1,128)}, f32[8,6288,512]{2,1,0:T(8,128)}) custom-call(s32[40]{0:T(128)} %concatenate.26.idx_ref, bf16[12576,768]{1,0:T(8,128)(2,1)} %e_ref.5, f32[8,6288,512]{2,1,0:T(8,128)} %get-tuple-element.29.l_ref, ...), custom_call_target="tpu_custom_call", output_to_operand_aliasing={{3}: (2, {})} | custom-call | flops 14835253248 | bytes 38633472 | tf_op jit(solution)/shard_map/dz_part/pallas_call | solution.py:260
  133.0 38.1 %logits_far.1 = (f32[8,6288,512]{2,1,0:T(8,128)}, bf16[8,512,768]{2,1,0:T(8,128)(2,1)}, f32[4,2,512]{2,1,0:T(2,128)}) custom-call(s32[40]{0:T(128)} %concatenate.26.idx_ref, bf16[12576,768]{1,0:T(8,128)(2,1)} %e_ref.5, f32[1,768]{1,0:T(1,128)} %broadcast_in_dim.83.gamma_ref, ...), custom_call_target="tpu_custom_call", output_to_operand_aliasing={{0}: (12, {}), {1}: (13, {})} | custom-call | flops 14835253248 | bytes 38633472 | tf_op jit(solution)/shard_map/logits_far/pallas_call | solution.py:224
  181.8 2.8 copy-done
  184.6 12.1 %shard_map.101 = (f32[1048,768]{1,0:T(8,128)S(1)}, f32[12576,768]{1,0:T(8,128)}) custom-call(s32[40]{0:T(128)S(1)} %copy-done.2, f32[8,6288,512]{2,1,0:T(8,128)} %get-tuple-element.38.l_ref, bf16[8,512,768]{2,1,0:T(8,128)(2,1)S(1)} %copy-done, f32[8,2,512]{2,1,0:T(2,128)S(1)} %maximum_maximum_fusion.tok_ref, s32[8,1,512]{2,1,0:T(1,128)S(1)} %reshape.263.lab_ref), custom_call_target="tpu_custom_call" | custom-call | flops 4120903680 | bytes 10731520 | tf_op jit(solution)/shard_map/pallas_call | solution.py:291
  197.0 12.1 %shard_map.102 = (f32[1048,768]{1,0:T(8,128)S(1)}, f32[12576,768]{1,0:T(8,128)}) custom-call(s32[40]{0:T(128)S(1)} %copy-done.2, f32[8,6288,512]{2,1,0:T(8,128)} %get-tuple-element.38.l_ref, bf16[8,512,768]{2,1,0:T(8,128)(2,1)S(1)} %copy-done, f32[8,2,512]{2,1,0:T(2,128)S(1)} %maximum_maximum_fusion.tok_ref, ...), custom_call_target="tpu_custom_call", output_to_operand_aliasing={{1}: (5, {})} | custom-call | flops 4120903680 | bytes 10731520 | tf_op jit(solution)/shard_map/pallas_call | solution.py:291
  209.6 13.7 %shard_map.103 = (f32[1048,768]{1,0:T(8,128)}, f32[12576,768]{1,0:T(8,128)}) custom-call(s32[40]{0:T(128)S(1)} %copy-done.2, f32[8,6288,512]{2,1,0:T(8,128)} %get-tuple-element.38.l_ref, bf16[8,512,768]{2,1,0:T(8,128)(2,1)S(1)} %copy-done, f32[8,2,512]{2,1,0:T(2,128)S(1)} %maximum_maximum_fusion.tok_ref, ...), custom_call_target="tpu_custom_call", output_to_operand_aliasing={{1}: (6, {})} | custom-call | flops 4120903680 | bytes 10731520 | tf_op jit(solution)/shard_map/pallas_call | solution.py:291
  223.7 13.7 %shard_map.104 = (f32[1048,768]{1,0:T(8,128)}, f32[12576,768]{1,0:T(8,128)}) custom-call(s32[40]{0:T(128)S(1)} %copy-done.2, f32[8,6288,512]{2,1,0:T(8,128)} %get-tuple-element.38.l_ref, bf16[8,512,768]{2,1,0:T(8,128)(2,1)S(1)} %copy-done, f32[8,2,512]{2,1,0:T(2,128)S(1)} %maximum_maximum_fusion.tok_ref, ...), custom_call_target="tpu_custom_call", output_to_operand_aliasing={{1}: (6, {})} | custom-call | flops 4120903680 | bytes 10731520 | tf_op jit(solution)/shard_map/pallas_call | solution.py:291
  237.6 3.2 add.160
  248.2 16.3 %collective-permute-done.12 = f32[2,128,768]{2,1,0:T(8,128)} collective-permute-done((f32[2,128,768]{2,1,0:T(8,128)}, f32[2,128,768]{2,1,0:T(8,128)}, u32[]{:S(2)}, u32[]{:S(2)}) %collective-permute-start.12) | collective-permute-done | bytes 786464 | tf_op jit(solution)/shard_map/ppermute | solution.py:336
  270.8 6.8 %collective-permute-done.13 = f32[128,768]{1,0:T(8,128)} collective-permute-done((f32[128,768]{1,0:T(8,128)}, f32[128,768]{1,0:T(8,128)}, u32[]{:S(2)}, u32[]{:S(2)}) %collective-permute-start.13) | collective-permute-done | bytes 393248 | tf_op jit(solution)/shard_map/ppermute | solution.py:336
  281.6 2.8 copy-done.1
  284.3 13.7 %shard_map.105 = (f32[1048,768]{1,0:T(8,128)}, f32[12576,768]{1,0:T(8,128)}) custom-call(s32[40]{0:T(128)S(1)} %copy-done.2, f32[8,6288,512]{2,1,0:T(8,128)} %get-tuple-element.38.l_ref, bf16[8,512,768]{2,1,0:T(8,128)(2,1)S(1)} %copy-done.1, f32[8,2,512]{2,1,0:T(2,128)S(1)} %maximum_maximum_fusion.tok_ref, ...), custom_call_target="tpu_custom_call", output_to_operand_aliasing={{1}: (6, {})} | custom-call | flops 4120903680 | bytes 10731520 | tf_op jit(solution)/shard_map/pallas_call | solution.py:291
  298.1 14.7 %shard_map.106 = (f32[1048,768]{1,0:T(8,128)}, f32[12576,768]{1,0:T(8,128)}) custom-call(s32[40]{0:T(128)S(1)} %copy-done.2, f32[8,6288,512]{2,1,0:T(8,128)} %get-tuple-element.38.l_ref, bf16[8,512,768]{2,1,0:T(8,128)(2,1)S(1)} %copy-done.1, f32[8,2,512]{2,1,0:T(2,128)S(1)} %maximum_maximum_fusion.tok_ref, ...), custom_call_target="tpu_custom_call", output_to_operand_aliasing={{1}: (6, {})} | custom-call | flops 4120903680 | bytes 10731520 | tf_op jit(solution)/shard_map/pallas_call | solution.py:291
  318.9 4.6 %collective-permute-done.16 = f32[4,512]{1,0:T(4,128)S(1)} collective-permute-done((f32[4,512]{1,0:T(4,128)S(1)}, f32[4,512]{1,0:T(4,128)S(1)}, u32[]{:S(2)}, u32[]{:S(2)}) %collective-permute-start.16) | collective-permute-done | bytes 8224 | tf_op jit(solution)/shard_map/ppermute | solution.py:336
  323.5 12.4 %collective-permute-start.17 = (f32[4,512]{1,0:T(4,128)S(1)}, f32[4,512]{1,0:T(4,128)S(1)}, u32[]{:S(2)}, u32[]{:S(2)}) collective-permute-start(f32[4,512]{1,0:T(4,128)S(1)} %add.172), channel_id=1, source_target_pairs={{0,2},{1,3},{2,0},{3,1},{4,6},{5,7},{6,4},{7,5},{8,10},{9,11},{10,... | collective-permute-start | bytes 24584 | tf_op jit(solution)/shard_map/ppermute | solution.py:336
  348.1 7.7 %collective-permute-done.21 = f32[128,768]{1,0:T(8,128)} collective-permute-done((f32[128,768]{1,0:T(8,128)}, f32[128,768]{1,0:T(8,128)}, u32[]{:S(2)}, u32[]{:S(2)}) %collective-permute-start.21) | collective-permute-done | bytes 393248 | tf_op jit(solution)/shard_map/ppermute | solution.py:336
  359.4 4.7 %collective-permute-done.22 = f32[128,768]{1,0:T(8,128)S(1)} collective-permute-done((f32[128,768]{1,0:T(8,128)}, f32[128,768]{1,0:T(8,128)S(1)}, u32[]{:S(2)}, u32[]{:S(2)}) %collective-permute-start.22) | collective-permute-done | bytes 393248 | tf_op jit(solution)/shard_map/ppermute | solution.py:336
  365.1 4.3 %collective-permute-done.26 = f32[128,768]{1,0:T(8,128)S(1)} collective-permute-done((f32[128,768]{1,0:T(8,128)}, f32[128,768]{1,0:T(8,128)S(1)}, u32[]{:S(2)}, u32[]{:S(2)}) %collective-permute-start.26) | collective-permute-done | bytes 393248 | tf_op jit(solution)/shard_map/ppermute | solution.py:336
  372.2 4.1 %place.2.de_ref = f32[12576,768]{1,0:T(8,128)} custom-call(s32[40]{0:T(128)S(1)} %copy-done.2, f32[1048,768]{1,0:T(8,128)} %collective-permute-done.47.got_ref, f32[12576,768]{1,0:T(8,128)} %get-tuple-element.52.de_ref), custom_call_target="tpu_custom_call", output_to_operand_aliasing={{}: (2, {})} | custom-call | tf_op jit(solution)/shard_map/place/pallas_call | solution.py:309
  376.4 2.2 place.3
  (226 shorter events, 80.0 us)
Async XLA Ops:
  7.3 46.1 %collective-permute-start.3 = (f32[4,256,768]{2,1,0:T(8,128)}, f32[4,256,768]{2,1,0:T(8,128)}, u32[]{:S(2)}, u32[]{:S(2)}) collective-permute-start(f32[4,256,768]{2,1,0:T(8,128)} %subtract_multiply_fusion.rest_0_), channel_id=1, source_target_pairs={{0,1},{1,0},{2,3},{3,2},{4,5},{5,4},{6,7},{7,6},{8,9},{9,8},{10,11... | collective-permute-start | bytes 9437192 | tf_op jit(solution)/shard_map/ppermute | solution.py:336
  8.0 8.5 %collective-permute-start.1 = (s32[1024]{0:T(1024)S(1)}, s32[1024]{0:T(1024)S(1)}, u32[]{:S(2)}, u32[]{:S(2)}) collective-permute-start(s32[1024]{0:T(1024)S(1)} %bitcast.125), channel_id=1, source_target_pairs={{0,2},{1,3},{2,0},{3,1},{4,6},{5,7},{6,4},{7,5},{8,10},{9,11},{10,... | collective-permute-start | bytes 12296 | tf_op jit(solution)/shard_map/ppermute | solution.py:336
  10.5 5.9 %collective-permute-start.2 = (s32[1024]{0:T(1024)S(1)}, s32[1024]{0:T(1024)S(1)}, u32[]{:S(2)}, u32[]{:S(2)}) collective-permute-start(s32[1024]{0:T(1024)S(1)} %bitcast.126), channel_id=1, source_target_pairs={{0,3},{1,2},{2,1},{3,0},{4,7},{5,6},{6,5},{7,4},{8,11},{9,10},{10,... | collective-permute-start | bytes 12296 | tf_op jit(solution)/shard_map/ppermute | solution.py:336
  10.7 5.5 %collective-permute-start = (s32[1024]{0:T(1024)S(1)}, s32[1024]{0:T(1024)S(1)}, u32[]{:S(2)}, u32[]{:S(2)}) collective-permute-start(s32[1024]{0:T(1024)S(1)} %bitcast.127), channel_id=1, source_target_pairs={{0,1},{1,0},{2,3},{3,2},{4,5},{5,4},{6,7},{7,6},{8,9},{9,8},{10,11... | collective-permute-start | bytes 12296 | tf_op jit(solution)/shard_map/ppermute | solution.py:336
  13.1 20.4 %collective-permute-start.27 = (f32[256,768]{1,0:T(8,128)S(1)}, f32[256,768]{1,0:T(8,128)S(1)}, u32[]{:S(2)}, u32[]{:S(2)}) collective-permute-start(f32[256,768]{1,0:T(8,128)S(1)} %get-tuple-element.33), channel_id=1, source_target_pairs={{0,2},{1,3},{2,0},{3,1},{4,6},{5,7},{6,4},{7,5},{8,10},{9,11},{10,... | collective-permute-start | bytes 2359304 | tf_op jit(solution)/shard_map/ppermute | solution.py:336
  16.2 33.6 %collective-permute-start.30 = (f32[256,768]{1,0:T(8,128)}, f32[256,768]{1,0:T(8,128)S(1)}, u32[]{:S(2)}, u32[]{:S(2)}) collective-permute-start(f32[256,768]{1,0:T(8,128)} %get-tuple-element.35), channel_id=1, source_target_pairs={{0,2},{1,3},{2,0},{3,1},{4,6},{5,7},{6,4},{7,5},{8,10},{9,11},{10,... | collective-permute-start | bytes 2359304 | tf_op jit(solution)/shard_map/ppermute | solution.py:336
  33.5 18.6 %collective-permute-start.28 = (f32[256,768]{1,0:T(8,128)S(1)}, f32[256,768]{1,0:T(8,128)}, u32[]{:S(2)}, u32[]{:S(2)}) collective-permute-start(f32[256,768]{1,0:T(8,128)S(1)} %collective-permute-done.27.rest_0_), channel_id=1, source_target_pairs={{0,4},{4,0},{8,12},{12,8},{1,5},{5,1},{9,13},{13,9},{2,6},{6,2},{1... | collective-permute-start | bytes 2359304 | tf_op jit(solution)/shard_map/ppermute | solution.py:336
  35.5 17.9 %collective-permute-start.29 = (f32[256,768]{1,0:T(8,128)S(1)}, f32[256,768]{1,0:T(8,128)}, u32[]{:S(2)}, u32[]{:S(2)}) collective-permute-start(f32[256,768]{1,0:T(8,128)S(1)} %collective-permute-done.27.rest_0_), channel_id=1, source_target_pairs={{0,8},{4,12},{8,0},{12,4},{1,9},{5,13},{9,1},{13,5},{2,10},{6,14},... | collective-permute-start | bytes 2359304 | tf_op jit(solution)/shard_map/ppermute | solution.py:336
  40.9 92.1 %collective-permute-start.31 = (f32[256,768]{1,0:T(8,128)S(1)}, f32[256,768]{1,0:T(8,128)}, u32[]{:S(2)}, u32[]{:S(2)}) collective-permute-start(f32[256,768]{1,0:T(8,128)S(1)} %collective-permute-done.27.rest_0_), channel_id=1, source_target_pairs={{0,1},{1,0},{2,3},{3,2},{4,5},{5,4},{6,7},{7,6},{8,9},{9,8},{10,11... | collective-permute-start | bytes 2359304 | tf_op jit(solution)/shard_map/ppermute | solution.py:336
  49.8 83.1 %collective-permute-start.34 = (f32[256,768]{1,0:T(8,128)S(1)}, f32[256,768]{1,0:T(8,128)}, u32[]{:S(2)}, u32[]{:S(2)}) collective-permute-start(f32[256,768]{1,0:T(8,128)S(1)} %collective-permute-done.30.rest_3_), channel_id=1, source_target_pairs={{0,1},{1,0},{2,3},{3,2},{4,5},{5,4},{6,7},{7,6},{8,9},{9,8},{10,11... | collective-permute-start | bytes 2359304 | tf_op jit(solution)/shard_map/ppermute | solution.py:336
  52.1 80.9 %collective-permute-start.32 = (f32[256,768]{1,0:T(8,128)}, f32[256,768]{1,0:T(8,128)}, u32[]{:S(2)}, u32[]{:S(2)}) collective-permute-start(f32[256,768]{1,0:T(8,128)} %collective-permute-done.28.rest_1_), channel_id=1, source_target_pairs={{0,1},{1,0},{2,3},{3,2},{4,5},{5,4},{6,7},{7,6},{8,9},{9,8},{10,11... | collective-permute-start | bytes 2359304 | tf_op jit(solution)/shard_map/ppermute | solution.py:336
  53.3 79.6 %collective-permute-start.33 = (f32[256,768]{1,0:T(8,128)}, f32[256,768]{1,0:T(8,128)}, u32[]{:S(2)}, u32[]{:S(2)}) collective-permute-start(f32[256,768]{1,0:T(8,128)} %collective-permute-done.29.rest_2_), channel_id=1, source_target_pairs={{0,1},{1,0},{2,3},{3,2},{4,5},{5,4},{6,7},{7,6},{8,9},{9,8},{10,11... | collective-permute-start | bytes 2359304 | tf_op jit(solution)/shard_map/ppermute | solution.py:336
  171.9 5.3 %collective-permute-start.36 = (f32[4,2,512]{2,1,0:T(2,128)}, f32[4,2,512]{2,1,0:T(2,128)S(1)}, u32[]{:S(2)}, u32[]{:S(2)}) collective-permute-start(f32[4,2,512]{2,1,0:T(2,128)} %get-tuple-element.40), channel_id=1, source_target_pairs={{0,4},{1,5},{2,6},{3,7},{4,0},{5,1},{6,2},{7,3},{8,12},{9,13},{10,... | collective-permute-start | bytes 49160 | tf_op jit(solution)/shard_map/ppermute | solution.py:339
  172.9 5.3 %collective-permute-start.37 = (f32[4,2,512]{2,1,0:T(2,128)}, f32[4,2,512]{2,1,0:T(2,128)S(1)}, u32[]{:S(2)}, u32[]{:S(2)}) collective-permute-start(f32[4,2,512]{2,1,0:T(2,128)} %get-tuple-element.40), channel_id=1, source_target_pairs={{0,5},{1,4},{2,7},{3,6},{4,1},{5,0},{6,3},{7,2},{8,13},{9,12},{10,... | collective-permute-start | bytes 49160 | tf_op jit(solution)/shard_map/ppermute | solution.py:339
  196.7 12.9 %collective-permute-start.43 = (f32[1048,768]{1,0:T(8,128)S(1)}, f32[1048,768]{1,0:T(8,128)S(1)}, u32[]{:S(2)}, u32[]{:S(2)}) collective-permute-start(f32[1048,768]{1,0:T(8,128)S(1)} %get-tuple-element.43), channel_id=1, source_target_pairs={{0,1},{1,0},{2,3},{3,2},{4,5},{5,4},{6,7},{7,6},{8,9},{9,8},{10,11... | collective-permute-start | bytes 9658376 | tf_op jit(solution)/shard_map/ppermute | solution.py:336
  209.1 14.6 %collective-permute-start.42 = (f32[1048,768]{1,0:T(8,128)S(1)}, f32[1048,768]{1,0:T(8,128)S(1)}, u32[]{:S(2)}, u32[]{:S(2)}) collective-permute-start(f32[1048,768]{1,0:T(8,128)S(1)} %get-tuple-element.42), channel_id=1, source_target_pairs={{0,1},{1,0},{2,3},{3,2},{4,5},{5,4},{6,7},{7,6},{8,9},{9,8},{10,11... | collective-permute-start | bytes 9658376 | tf_op jit(solution)/shard_map/ppermute | solution.py:336
  209.4 28.2 %collective-permute-start.11 = (f32[4,256,768]{2,1,0:T(8,128)}, f32[4,256,768]{2,1,0:T(8,128)}, u32[]{:S(2)}, u32[]{:S(2)}) collective-permute-start(f32[4,256,768]{2,1,0:T(8,128)} %get-tuple-element.32), channel_id=1, source_target_pairs={{0,1},{1,0},{2,3},{3,2},{4,5},{5,4},{6,7},{7,6},{8,9},{9,8},{10,11... | collective-permute-start | bytes 9437192 | tf_op jit(solution)/shard_map/ppermute | solution.py:336
  223.3 58.2 %collective-permute-start.45 = (f32[1048,768]{1,0:T(8,128)}, f32[1048,768]{1,0:T(8,128)S(1)}, u32[]{:S(2)}, u32[]{:S(2)}) collective-permute-start(f32[1048,768]{1,0:T(8,128)} %get-tuple-element.47), channel_id=1, source_target_pairs={{0,1},{1,0},{2,3},{3,2},{4,5},{5,4},{6,7},{7,6},{8,9},{9,8},{10,11... | collective-permute-start | bytes 9658376 | tf_op jit(solution)/shard_map/ppermute | solution.py:336
  237.4 60.6 %collective-permute-start.44 = (f32[1048,768]{1,0:T(8,128)}, f32[1048,768]{1,0:T(8,128)}, u32[]{:S(2)}, u32[]{:S(2)}) collective-permute-start(f32[1048,768]{1,0:T(8,128)} %get-tuple-element.46), channel_id=1, source_target_pairs={{0,1},{1,0},{2,3},{3,2},{4,5},{5,4},{6,7},{7,6},{8,9},{9,8},{10,11... | collective-permute-start | bytes 9658376 | tf_op jit(solution)/shard_map/ppermute | solution.py:336
  244.4 20.1 %collective-permute-start.12 = (f32[2,128,768]{2,1,0:T(8,128)}, f32[2,128,768]{2,1,0:T(8,128)}, u32[]{:S(2)}, u32[]{:S(2)}) collective-permute-start(f32[2,128,768]{2,1,0:T(8,128)} %dynamic-slice_bitcast_fusion.3), channel_id=1, source_target_pairs={{0,4},{4,0},{8,12},{12,8},{1,5},{5,1},{9,13},{13,9},{2,6},{6,2},{1... | collective-permute-start | bytes 2359304 | tf_op jit(solution)/shard_map/ppermute | solution.py:336
  247.8 19.8 %collective-permute-start.14 = (f32[2,128,768]{2,1,0:T(8,128)}, f32[2,128,768]{2,1,0:T(8,128)}, u32[]{:S(2)}, u32[]{:S(2)}) collective-permute-start(f32[2,128,768]{2,1,0:T(8,128)} %dynamic-slice_bitcast_fusion.2), channel_id=1, source_target_pairs={{0,8},{4,12},{8,0},{12,4},{1,9},{5,13},{9,1},{13,5},{2,10},{6,14},... | collective-permute-start | bytes 2359304 | tf_op jit(solution)/shard_map/ppermute | solution.py:336
  266.8 10.8 %collective-permute-start.13 = (f32[128,768]{1,0:T(8,128)}, f32[128,768]{1,0:T(8,128)}, u32[]{:S(2)}, u32[]{:S(2)}) collective-permute-start(f32[128,768]{1,0:T(8,128)} %dynamic-slice_bitcast_fusion.5), channel_id=1, source_target_pairs={{0,8},{4,12},{8,0},{12,4},{1,9},{5,13},{9,1},{13,5},{2,10},{6,14},... | collective-permute-start | bytes 1179656 | tf_op jit(solution)/shard_map/ppermute | solution.py:336
  269.8 10.5 %collective-permute-start.15 = (f32[128,768]{1,0:T(8,128)}, f32[128,768]{1,0:T(8,128)}, u32[]{:S(2)}, u32[]{:S(2)}) collective-permute-start(f32[128,768]{1,0:T(8,128)} %dynamic-slice_bitcast_fusion.4), channel_id=1, source_target_pairs={{0,4},{4,0},{8,12},{12,8},{1,5},{5,1},{9,13},{13,9},{2,6},{6,2},{1... | collective-permute-start | bytes 1179656 | tf_op jit(solution)/shard_map/ppermute | solution.py:336
  312.8 63.6 %collective-permute-start.46 = (f32[1048,768]{1,0:T(8,128)}, f32[1048,768]{1,0:T(8,128)S(1)}, u32[]{:S(2)}, u32[]{:S(2)}) collective-permute-start(f32[1048,768]{1,0:T(8,128)} %get-tuple-element.50), channel_id=1, source_target_pairs={{0,1},{1,0},{2,3},{3,2},{4,5},{5,4},{6,7},{7,6},{8,9},{9,8},{10,11... | collective-permute-start | bytes 9658376 | tf_op jit(solution)/shard_map/ppermute | solution.py:336
  312.8 59.4 %collective-permute-start.47 = (f32[1048,768]{1,0:T(8,128)}, f32[1048,768]{1,0:T(8,128)}, u32[]{:S(2)}, u32[]{:S(2)}) collective-permute-start(f32[1048,768]{1,0:T(8,128)} %get-tuple-element.51), channel_id=1, source_target_pairs={{0,1},{1,0},{2,3},{3,2},{4,5},{5,4},{6,7},{7,6},{8,9},{9,8},{10,11... | collective-permute-start | bytes 9658376 | tf_op jit(solution)/shard_map/ppermute | solution.py:336
  315.6 30.7 %collective-permute-start.24 = (f32[128,768]{1,0:T(8,128)}, f32[128,768]{1,0:T(8,128)}, u32[]{:S(2)}, u32[]{:S(2)}) collective-permute-start(f32[128,768]{1,0:T(8,128)} %get-tuple-element.71), channel_id=1, source_target_pairs={{0,8},{4,12},{8,0},{12,4},{1,9},{5,13},{9,1},{13,5},{2,10},{6,14},... | collective-permute-start | bytes 1179656 | tf_op jit(solution)/shard_map/ppermute | solution.py:336
  323.5 14.1 %collective-permute-start.17 = (f32[4,512]{1,0:T(4,128)S(1)}, f32[4,512]{1,0:T(4,128)S(1)}, u32[]{:S(2)}, u32[]{:S(2)}) collective-permute-start(f32[4,512]{1,0:T(4,128)S(1)} %add.172), channel_id=1, source_target_pairs={{0,2},{1,3},{2,0},{3,1},{4,6},{5,7},{6,4},{7,5},{8,10},{9,11},{10,... | collective-permute-start | bytes 24584 | tf_op jit(solution)/shard_map/ppermute | solution.py:336
  343.4 12.3 %collective-permute-start.21 = (f32[128,768]{1,0:T(8,128)}, f32[128,768]{1,0:T(8,128)}, u32[]{:S(2)}, u32[]{:S(2)}) collective-permute-start(f32[128,768]{1,0:T(8,128)} %get-tuple-element.70), channel_id=1, source_target_pairs={{0,4},{4,0},{8,12},{12,8},{1,5},{5,1},{9,13},{13,9},{2,6},{6,2},{1... | collective-permute-start | bytes 1179656 | tf_op jit(solution)/shard_map/ppermute | solution.py:336
  345.0 12.0 %collective-permute-start.23 = (f32[128,768]{1,0:T(8,128)}, f32[128,768]{1,0:T(8,128)}, u32[]{:S(2)}, u32[]{:S(2)}) collective-permute-start(f32[128,768]{1,0:T(8,128)} %get-tuple-element.70), channel_id=1, source_target_pairs={{0,8},{4,12},{8,0},{12,4},{1,9},{5,13},{9,1},{13,5},{2,10},{6,14},... | collective-permute-start | bytes 1179656 | tf_op jit(solution)/shard_map/ppermute | solution.py:336
  346.3 17.8 %collective-permute-start.22 = (f32[128,768]{1,0:T(8,128)}, f32[128,768]{1,0:T(8,128)S(1)}, u32[]{:S(2)}, u32[]{:S(2)}) collective-permute-start(f32[128,768]{1,0:T(8,128)} %get-tuple-element.71), channel_id=1, source_target_pairs={{0,4},{4,0},{8,12},{12,8},{1,5},{5,1},{9,13},{13,9},{2,6},{6,2},{1... | collective-permute-start | bytes 1179656 | tf_op jit(solution)/shard_map/ppermute | solution.py:336
  355.7 13.7 %collective-permute-start.26 = (f32[128,768]{1,0:T(8,128)}, f32[128,768]{1,0:T(8,128)S(1)}, u32[]{:S(2)}, u32[]{:S(2)}) collective-permute-start(f32[128,768]{1,0:T(8,128)} %collective-permute-done.24), channel_id=1, source_target_pairs={{0,4},{4,0},{8,12},{12,8},{1,5},{5,1},{9,13},{13,9},{2,6},{6,2},{1... | collective-permute-start | bytes 1179656 | tf_op jit(solution)/shard_map/ppermute | solution.py:336
  357.0 12.4 %collective-permute-start.25 = (f32[128,768]{1,0:T(8,128)}, f32[128,768]{1,0:T(8,128)S(1)}, u32[]{:S(2)}, u32[]{:S(2)}) collective-permute-start(f32[128,768]{1,0:T(8,128)} %collective-permute-done.21), channel_id=1, source_target_pairs={{0,8},{4,12},{8,0},{12,4},{1,9},{5,13},{9,1},{13,5},{2,10},{6,14},... | collective-permute-start | bytes 1179656 | tf_op jit(solution)/shard_map/ppermute | solution.py:336
  (43 other events, 482.2 us)

commit v2 on v1

--- a/solution.py
+++ b/solution.py
@@ -13,7 +13,7 @@
 PAIR = 2 * BLOCK
 BIG = 1e30
 VMEM_LIMIT = 62 * 1024 * 1024
-DE_VMEM = 28 * 1024 * 1024
+DE_VMEM = 16 * 1024 * 1024
 
 
 CORE, NEAR_PAIRS, FAR_PAIRS, ALL_PAIRS, ROW_START = 0, 1, 2, 3, 4
@@ -141,46 +141,44 @@
 
 
 def de_kernel(offset, rows, got_offset, idx_ref, l_ref, z_ref, tok_ref, lab_ref, *rest):
-    if got_offset is None:
-        part_ref, out_ref, sem = rest[-3:]
-        got_ref = None
-    else:
-        got_ref, part_ref, out_ref, sem = rest[0], rest[-3], rest[-2], rest[-1]
-    i = pl.program_id(0)
+    got_ref = None if got_offset is None else rest[0]
+    part_ref, out_ref, buf_ref, sem = rest[-4:]
     core = idx_ref[CORE]
     half = out_ref.shape[0] // 2
     count = idx_ref[ALL_PAIRS]
-    lse = tok_ref[0, 0:1, :]
-    weight = tok_ref[0, 1:2, :]
-    label = lab_ref[0] - idx_ref[ROW_START] - offset
 
     def rows_at(side, start, n):
         return out_ref.at[pl.ds(pl.multiple_of(side * half + start, 8), n), :]
 
-    own = pltpu.make_async_copy(part_ref, rows_at(core, offset, rows), sem.at[0])
+    def fetch(i):
+        return pltpu.make_async_copy(l_ref.at[idx_ref[PAIR_IDS + i], pl.ds(offset, rows), :], buf_ref.at[i % 2], sem.at[i % 2])
+
+    fetch(0).start()
     got = None
     if got_ref is not None:
-        got = pltpu.make_async_copy(got_ref, rows_at(1 - core, got_offset, got_ref.shape[0]), sem.at[1])
-        pl.when(i == 0)(got.start)
-
-    @pl.when(i == 0)
-    def _():
-        part_ref[...] = jnp.zeros_like(part_ref)
-
-    @pl.when(i < count)
-    def _():
+        got = pltpu.make_async_copy(got_ref, rows_at(1 - core, got_offset, got_ref.shape[0]), sem.at[2])
+        got.start()
+    part_ref[...] = jnp.zeros_like(part_ref)
+
+    def step(i, carry):
+        fetch(i).wait()
+        pl.when(i + 1 < count)(lambda: fetch(i + 1).start())
+        pair = idx_ref[PAIR_IDS + i]
+        lse = tok_ref[pair, 0:1, :]
+        weight = tok_ref[pair, 1:2, :]
+        label = lab_ref[pair] - idx_ref[ROW_START] - offset
         for start, n in chunk_list(rows, 528):
             is_target = lax.broadcasted_iota(jnp.int32, (n, PAIR), 0) == label - start
-            grad = grad_tile(l_ref[0, start:start + n, :], lse, weight, is_target)
-            part_ref[start:start + n, :] += jnp.dot(grad, z_ref[0], preferred_element_type=jnp.float32)
-
-    pl.when(i == count - 1)(own.start)
-
-    @pl.when(i == pl.num_programs(0) - 1)
-    def _():
-        own.wait()
-        if got is not None:
-            got.wait()
+            grad = grad_tile(buf_ref[i % 2, start:start + n, :], lse, weight, is_target)
+            part_ref[start:start + n, :] += jnp.dot(grad, z_ref[pair], preferred_element_type=jnp.float32)
+        return carry
+
+    lax.fori_loop(0, count, step, 0)
+    own = pltpu.make_async_copy(part_ref, rows_at(core, offset, rows), sem.at[3])
+    own.start()
+    own.wait()
+    if got is not None:
+        got.wait()
 
 
 def place_kernel(got_offset, idx_ref, got_ref, de_ref, out_ref, sem):
@@ -189,6 +187,140 @@
     copy = pltpu.make_async_copy(got_ref, out_ref.at[pl.ds(start, got_ref.shape[0]), :], sem)
     copy.start()
     copy.wait()
+
+
+def lse_kernel(st_ref, lab_ref, scale_ref, tok_ref, got_ref, send_sem, recv_sem):
+    tp, dp = lax.axis_index('tp'), lax.axis_index('dp')
+    peers = []
+    for k in range(1, 8):
+        z, y, c = k // 4, k // 2 % 2, k % 2
+        peer_tp = (tp // 2 + z) % 2 * 2 + (tp % 2 + y) % 2
+        peers.append({'tp': peer_tp, 'dp': dp // 2 * 2 + (dp % 2 + c) % 2})
+    barrier = pltpu.get_barrier_semaphore()
+    for peer in peers:
+        pl.semaphore_signal(barrier, inc=1, device_id=peer, device_id_type=pl.DeviceIdType.MESH)
+    pl.semaphore_wait(barrier, 7)
+    copies = [
+        pltpu.make_async_remote_copy(st_ref, got_ref.at[k], send_sem.at[k], recv_sem.at[k], device_id=peer, device_id_type=pl.DeviceIdType.MESH)
+        for k, peer in enumerate(peers)
+    ]
+    for copy in copies:
+        copy.start()
+    for copy in copies:
+        copy.wait()
+    top = st_ref[:, 0, :]
+    for k in range(7):
+        top = jnp.maximum(top, got_ref[k, :, 0, :])
+    total = st_ref[:, 1, :] * jnp.exp(st_ref[:, 0, :] - top)
+    for k in range(7):
+        total = total + got_ref[k, :, 1, :] * jnp.exp(got_ref[k, :, 0, :] - top)
+    live = lab_ref[:, 0, :] >= 0
+    tok_ref[:, 0, :] = jnp.where(live, top + jnp.log(total), BIG)
+    tok_ref[:, 1, :] = jnp.where(live, scale_ref[...], 0.0)
+
+
+def call_lse(stats, lab, scale, collective_id):
+    vmem = pl.BlockSpec(memory_space=pltpu.VMEM)
+    return pl.pallas_call(
+        lse_kernel,
+        in_specs=[vmem, vmem, vmem],
+        out_specs=vmem,
+        out_shape=jax.ShapeDtypeStruct(stats.shape, jnp.float32),
+        scratch_shapes=[pltpu.VMEM((7,) + stats.shape, jnp.float32), pltpu.SemaphoreType.DMA((7,)), pltpu.SemaphoreType.DMA((7,))],
+        compiler_params=pltpu.CompilerParams(collective_id=collective_id, has_side_effects=True, vmem_limit_bytes=4 * 1024 * 1024),
+        cost_estimate=pl.CostEstimate(flops=10_000_000, bytes_accessed=1_000_000, transcendentals=20_000),
+    )(stats, lab, scale)
+
+
+def norm_kernel(pick_ref, h_ref, hat_ref, inv_ref, own_ref, far_ref):
+    i = pl.program_id(0)
+    x = h_ref[0].astype(jnp.float32)
+    centered = x - jnp.mean(x, axis=-1, keepdims=True)
+    inv = lax.rsqrt(jnp.mean(centered * centered, axis=-1, keepdims=True) + LAYER_EPS)
+    hat = centered * inv
+    hat_ref[0] = hat
+
+    @pl.when(i == pick_ref[0])
+    def _():
+        own_ref[...] = hat
+        inv_ref[...] = jnp.broadcast_to(inv, inv_ref.shape)
+
+    @pl.when(i == pick_ref[1])
+    def _():
+        far_ref[...] = hat
+
+
+def call_norm(picks, hidden):
+    n, block, width = hidden.shape
+    quarter = pl.BlockSpec((block, width), lambda i, s: (0, 0))
+    each = pl.BlockSpec((1, block, width), lambda i, s: (i, 0, 0))
+    one = jax.ShapeDtypeStruct((block, width), jnp.float32)
+    return pl.pallas_call(
+        norm_kernel,
+        grid_spec=pltpu.PrefetchScalarGridSpec(
+            num_scalar_prefetch=1, grid=(n,), in_specs=[each],
+            out_specs=[each, pl.BlockSpec((block, 128), lambda i, s: (0, 0)), quarter, quarter],
+        ),
+        out_shape=[jax.ShapeDtypeStruct(hidden.shape, jnp.float32), jax.ShapeDtypeStruct((block, 128), jnp.float32), one, one],
+        compiler_params=params(DE_VMEM),
+        cost_estimate=pl.CostEstimate(flops=10_000_000, bytes_accessed=8_000_000, transcendentals=1024),
+        name="norm",
+    )(picks, hidden)
+
+
+def norm_bwd_kernel(a_ref, b_ref, a_got_ref, b_got_ref, hat_ref, inv_ref, gamma_ref, loss_ref, a_out, b_out, sum_out):
+    piece = a_ref.shape[0]
+    grad = jnp.concatenate([a_ref[...] + a_got_ref[...], b_ref[...] + b_got_ref[...]])
+    hat = hat_ref[...]
+    scaled = grad * gamma_ref[...]
+    inner = scaled - jnp.mean(scaled, axis=-1, keepdims=True) - hat * jnp.mean(scaled * hat, axis=-1, keepdims=True)
+    inner = inner * inv_ref[:, 0:1]
+    a_out[...] = inner[:piece]
+    b_out[...] = inner[piece:]
+    sum_out[...] = jnp.zeros_like(sum_out)
+    sum_out[0:1, :] = jnp.sum(grad * hat, axis=0, keepdims=True)
+    sum_out[1:2, :] = jnp.sum(grad, axis=0, keepdims=True)
+    sum_out[2:3, 0:128] = loss_ref[...]
+
+
+def call_norm_bwd(*args):
+    piece, width = args[0].shape
+    vmem = pl.BlockSpec(memory_space=pltpu.VMEM)
+    half = jax.ShapeDtypeStruct((piece, width), jnp.float32)
+    return pl.pallas_call(
+        norm_bwd_kernel,
+        in_specs=[vmem] * len(args),
+        out_specs=[vmem] * 3,
+        out_shape=[half, half, jax.ShapeDtypeStruct((8, width), jnp.float32)],
+        compiler_params=pltpu.CompilerParams(vmem_limit_bytes=DE_VMEM),
+        cost_estimate=pl.CostEstimate(flops=10_000_000, bytes_accessed=4_000_000, transcendentals=0),
+        name="norm_bwd",
+    )(*args)
+
+
+def round_kernel(pick_ref, *refs):
+    out_ref = refs[-1]
+    piece = refs[0].shape[0]
+    for p in range(4):
+        start = pl.multiple_of(pick_ref[2 + p] * (2 * piece), 2 * piece)
+        out_ref[0, pl.ds(start, piece), :] = refs[2 * p][...].astype(jnp.bfloat16)
+        out_ref[0, pl.ds(start + piece, piece), :] = refs[2 * p + 1][...].astype(jnp.bfloat16)
+
+
+def call_round(picks, pieces):
+    piece, width = pieces[0].shape
+    spec = pl.BlockSpec((piece, width), lambda i, s: (0, 0), pipeline_mode=pl.Buffered(1))
+    out = (1, len(pieces) * piece, width)
+    return pl.pallas_call(
+        round_kernel,
+        grid_spec=pltpu.PrefetchScalarGridSpec(
+            num_scalar_prefetch=1, grid=(1,), in_specs=[spec] * len(pieces), out_specs=pl.BlockSpec(out, lambda i, s: (0, 0, 0)),
+        ),
+        out_shape=jax.ShapeDtypeStruct(out, jnp.bfloat16),
+        compiler_params=params(DE_VMEM),
+        cost_estimate=pl.CostEstimate(flops=1_000_000, bytes_accessed=5_000_000, transcendentals=0),
+        name="round",
+    )(picks, *pieces)
 
 
 def params(limit=VMEM_LIMIT):
@@ -270,23 +402,21 @@
 
 def call_de(idx, l, zc, tok, lab, de, offset, rows, got, got_offset):
     total, width = l.shape[1], zc.shape[2]
-    j = offset // rows
+
+    def whole(x):
+        return pl.BlockSpec(x.shape, lambda i, s: (0,) * x.ndim, pipeline_mode=pl.Buffered(1))
+
     extra = [] if de is None else [de]
     extra_specs = [ANY] * len(extra)
     if got is not None:
         extra = [got] + extra
-        extra_specs = [pl.BlockSpec(got.shape, lambda i, s: (0, 0), pipeline_mode=pl.Buffered(1))] + extra_specs
+        extra_specs = [whole(got)] + extra_specs
     spec = pltpu.PrefetchScalarGridSpec(
         num_scalar_prefetch=1,
-        grid=(8,),
-        in_specs=[
-            pl.BlockSpec((1, rows, PAIR), lambda i, s: (s[PAIR_IDS + last(i, s[ALL_PAIRS])], j, 0)),
-            pl.BlockSpec((1, PAIR, width), lambda i, s: (s[PAIR_IDS + last(i, s[ALL_PAIRS])], 0, 0)),
-            pl.BlockSpec((1, 2, PAIR), lambda i, s: (s[PAIR_IDS + last(i, s[ALL_PAIRS])], 0, 0)),
-            pl.BlockSpec((1, 1, PAIR), lambda i, s: (s[PAIR_IDS + last(i, s[ALL_PAIRS])], 0, 0)),
-        ] + extra_specs,
-        out_specs=[pl.BlockSpec((rows, width), lambda i, s: (0, 0)), ANY],
-        scratch_shapes=[pltpu.SemaphoreType.DMA((2,))],
+        grid=(1,),
+        in_specs=[ANY, whole(zc), whole(tok), whole(lab)] + extra_specs,
+        out_specs=[pl.BlockSpec((rows, width), lambda i, s: (0, 0), pipeline_mode=pl.Buffered(1)), ANY],
+        scratch_shapes=[pltpu.VMEM((2, rows, PAIR), jnp.float32), pltpu.SemaphoreType.DMA((4,))],
     )
     return pl.pallas_call(
         functools.partial(de_kernel, offset, rows, got_offset if got is not None else None),
@@ -314,6 +444,10 @@
         compiler_params=params(DE_VMEM),
         name="place",
     )(idx, got, de)
+
+
+def idx_of(scalars, order, pair_idx, core, tp):
+    return jnp.concatenate([scalars, order[0], order[0] ^ (core * 4), order[1] ^ (core * 4 + tp), pair_idx])
 
 
 def order_blocks(active):
@@ -335,19 +469,14 @@
         n = n_tp if axis == 'tp' else n_dp
         return lax.ppermute(x, axis, [(k, k ^ bits) for k in range(n)])
 
-    def flip_both(x, tp_bits, dp_bits):
-        return lax.ppermute(x, ('tp', 'dp'), [(k, ((k // n_dp) ^ tp_bits) * n_dp + ((k % n_dp) ^ dp_bits)) for k in range(n_tp * n_dp)])
-
-    def from_group(x):
-        return jnp.stack([x] + [flip_both(x, t, d) for t in range(4) for d in range(2) if (t, d) != (0, 0)])
-
     def pick(x, index):
         return lax.dynamic_index_in_dim(x, index, 0, keepdims=False)
 
     def local_step(hidden, ln_gamma, ln_beta, embed_shard, labels, loss_mask):
         tp, dp = lax.axis_index('tp'), lax.axis_index('dp')
         core = dp & 1
-        y, z = tp & 1, tp >> 1
+        y, z = (tp & 1).astype(jnp.uint32), (tp >> 1).astype(jnp.uint32)
+        not_y, not_z = 1 - y, 1 - z
         seq, width = hidden.shape[1:]
         quarters, piece = seq // BLOCK, BLOCK // 2
         rows = embed_shard.shape[0] // 2
@@ -360,13 +489,9 @@
         far_marks = [flip(marked, 'dp', 2), flip(marked, 'dp', 3)]
         mate_marks = flip(marked, 'dp', 1)
 
-        x_float = hidden[0].astype(jnp.float32)
-        centered = x_float - jnp.mean(x_float, axis=-1, keepdims=True)
-        inv_std = lax.rsqrt(jnp.mean(centered * centered, axis=-1, keepdims=True) + LAYER_EPS)
-        x_hat = (centered * inv_std).reshape(quarters, BLOCK, width)
-
+        picks = jnp.stack([tp, tp ^ 3] + [tp ^ p for p in range(4)])
+        x_hat, inv_std, own_quarter, far_quarter = call_norm(picks, hidden.reshape(quarters, BLOCK, width))
         mate = flip(x_hat, 'dp', 1)
-        own_quarter, far_quarter = lax.optimization_barrier((pick(x_hat, tp), pick(x_hat, tp ^ 3)))
         far0, far3 = flip(own_quarter, 'dp', 2), flip(far_quarter, 'dp', 2)
 
         marks = jnp.concatenate([by_core(marked, mate_marks), by_core(*far_marks)]).reshape(2, 8, BLOCK)
@@ -378,58 +503,51 @@
         pair_idx = jnp.where(pair_ids < pairs[0], pair_ids, jnp.minimum(4 + pair_ids - pairs[0], 7))
         zero = jnp.zeros((), jnp.int32)
         scalars = jnp.stack([core, pairs[0], pairs[1], pairs[0] + pairs[1], row_start, zero, zero, zero])
-        idx = jnp.concatenate([scalars, order[0], order[0] ^ (core * 4), order[1] ^ (core * 4 + tp), pair_idx])
+        idx, y, z, not_y, not_z = lax.optimization_barrier((idx_of(scalars, order, pair_idx, core, tp), y, z, not_y, not_z))
 
         logits, z_pairs, near_stats = call_logits(idx, embed_shard, ln_gamma, ln_beta, [x_hat, mate], None, rows)
 
-        def combine(every, labels_here):
-            top = jnp.max(every[:, :, 0], axis=0)
-            total = jnp.sum(every[:, :, 1] * jnp.exp(every[:, :, 0] - top), axis=0)
-            live = labels_here[:, 0] >= 0
-            lse = jnp.where(live, top + jnp.log(total), BIG)
-            return jnp.stack([lse, jnp.where(live, 1.0 / token_count, 0.0)], axis=1), lse, live
-
-        near_tok, near_lse, near_live = combine(from_group(near_stats), lab[:4])
+        scale = jnp.broadcast_to(1.0 / token_count, (1, PAIR))
+        near_tok = call_lse(near_stats, lab[:4], scale, 0)
         mate0, mate3 = flip(far0, 'dp', 1), flip(far3, 'dp', 1)
         far1, far2 = flip(far0, 'tp', 1), flip(far0, 'tp', 2)
         dz_own, dz_mate, target, logits = call_dz(idx, embed_shard, logits, near_tok, lab[:4])
 
         mate1, mate2 = flip(far1, 'dp', 1), flip(far2, 'dp', 1)
-        part = dz_own + flip(dz_mate, 'dp', 1)
-        grid_part = part.reshape(2, 2, BLOCK, width)
-        a_part, b_part = grid_part[:, :, :piece], grid_part[:, :, piece:]
-        a_got = flip(lax.dynamic_index_in_dim(a_part, 1 - y, 1, keepdims=False), 'tp', 1)
-        b_got = flip(pick(b_part, 1 - z), 'tp', 2)
-        a_keep = lax.dynamic_index_in_dim(a_part, y, 1, keepdims=False) + a_got
-        b_keep = pick(b_part, z) + b_got
-
+        lead = ((tp == 0) & (core == 0)).astype(jnp.float32)
+        loss = jnp.sum(jnp.where(lab[:4, 0] >= 0, lead * near_tok[:, 0] - target[:, 0], 0.0)) / token_count
+        loss, idx = lax.optimization_barrier((jnp.broadcast_to(loss, (1, 128)), idx))
         pieces = [far0, far1, far2, far3, mate0, mate1, mate2, mate3]
         logits, z_pairs, far_stats = call_logits(idx, embed_shard, ln_gamma, ln_beta, pieces, (logits, z_pairs), rows)
-        far_tok, _, _ = combine(from_group(far_stats), lab[4:])
-        a_grad = flip(pick(a_keep, 1 - z), 'tp', 2)
-        b_grad = flip(pick(b_keep, 1 - y), 'tp', 1)
-        grad = jnp.concatenate([pick(a_keep, z) + a_grad, pick(b_keep, y) + b_grad])
+        far_tok = call_lse(far_stats, lab[4:], scale, 1)
+        dz_got = flip(dz_mate, 'dp', 1)
+
+        def part(column, half_z, half_y):
+            def cut(x):
+                x = x.reshape(2, 2, 2, piece, width)[:, :, column]
+                return pick(x, half_z) if half_y is None else lax.dynamic_index_in_dim(x, half_y, 1, keepdims=False)
+
+            return cut(dz_own) + cut(dz_got)
+
+        a_got = flip(part(0, None, not_y), 'tp', 1)
+        b_got = flip(part(1, not_z, None), 'tp', 2)
+        a_keep = part(0, None, y) + a_got
+        b_keep = part(1, z, None) + b_got
+        a_grad = flip(pick(a_keep, not_z), 'tp', 2)
+        b_grad = flip(pick(b_keep, not_y), 'tp', 1)
         tok = jnp.concatenate([near_tok, far_tok])
 
-        hat = own_quarter
-        scaled = grad * ln_gamma
-        inner = scaled - jnp.mean(scaled, axis=-1, keepdims=True) - hat * jnp.mean(scaled * hat, axis=-1, keepdims=True)
-        a0, b0 = inner[:piece], inner[piece:]
+        a0, b0, sums = call_norm_bwd(pick(a_keep, z), pick(b_keep, y), a_grad, b_grad, own_quarter, inv_std, ln_gamma[None], loss)
         a1, b2 = flip(a0, 'tp', 1), flip(b0, 'tp', 2)
         a2, a3 = flip(a0, 'tp', 2), flip(a1, 'tp', 2)
         b1, b3 = flip(b0, 'tp', 1), flip(b2, 'tp', 1)
-        gathered = jnp.stack([jnp.concatenate(v) for v in ((a0, b0), (a1, b1), (a2, b2), (a3, b3))])
-        gathered = jnp.stack([pick(gathered, tp ^ q) for q in range(quarters)]).reshape(seq, width)
-        d_hidden = (gathered * inv_std).astype(jnp.bfloat16)[None]
-
-        lead = ((tp == 0) & (core == 0)).astype(jnp.float32)
-        loss = jnp.sum(jnp.where(near_live, lead * near_lse - target[:, 0], 0.0)) / token_count
-        sums = jnp.concatenate([jnp.sum(grad * hat, axis=0), jnp.sum(grad, axis=0), jnp.broadcast_to(loss, (512,))]).reshape(4, 512)
+        d_hidden = call_round(picks, [a0, b0, a1, b1, a2, b2, a3, b3])
+
         for bits in (1, 2):
             got_sums = flip(sums, 'dp', bits)
             sums = sums + got_sums
         got_sums = [flip(sums, 'tp', k) for k in (1, 2, 3)]
-        sums = (sums + got_sums[0] + (got_sums[1] + got_sums[2])).reshape(-1)
+        sums = sums + got_sums[0] + (got_sums[1] + got_sums[2])
 
         chunks = [(k * (rows // 6), rows // 6) for k in range(6)]
         d_embed, got = None, []
@@ -440,7 +558,7 @@
         for n in (4, 5):
             d_embed = call_place(idx, got[n], d_embed, chunks[n][0])
 
-        return sums[2 * width], d_hidden, d_embed, sums[:width], sums[width:2 * width]
+        return sums[2, 0], d_hidden, d_embed, sums[0], sums[1]
 
 
     return jax.shard_map(local_step, mesh=mesh, in_specs=(P('dp', None, None), P(None), P(None), P('tp', None), P('dp', None), P('dp', None)), out_specs=(P(), P('dp', None, None), P('tp', None), P(None), P(None)), check_vma=False)

time: 380 us -> 335 us (0.88)
  waiting for transfers between devices: 101 us -> 78.4 us
  Pallas kernels: 177 us -> 196 us
  other arithmetic: 22.7 us -> 4.64 us
  starting transfers between devices: 48.4 us -> 36.4 us
  local copies, waits for them, and re-layouts: 24.4 us -> 13 us
    ppermute x14 -> x0, waiting for transfers between devices: 23.2 us -> none  [flip_both(): lax.ppermute(x, ('tp', 'dp'), [(k, (k // n_dp ^ tp_bits) * n_dp + (k % n_...]
    pallas_call x0 -> x5, Pallas kernels: none -> 16.5 us  [the longest x2 10.8 us: call_lse(): pl.pallas_call(lse_kernel, in_specs=[vmem, vmem, vmem], out_specs=vmem, o...]
    ppermute x14 -> x0, starting transfers between devices: 10.9 us -> none  [flip_both(): lax.ppermute(x, ('tp', 'dp'), [(k, (k // n_dp ^ tp_bits) * n_dp + (k % n_...]
    reduce_sum x9 -> x1, other arithmetic: 7.15 us -> 0.6 us  [local_step(): jnp.sum(jnp.where(lab[:4, 0] >= 0, lead * near_tok[:, 0] - target[:, 0],...]
    squeeze x4 -> x2, local copies, waits for them, and re-layouts: 6.13 us -> 0.12 us  [pick(): return lax.dynamic_index_in_dim(x, index, 0, keepdims=False)]
    add x5, other arithmetic: 5.97 us -> 0.5 us  [the longest x2 0.18 us: part(): return cut(dz_own) + cut(dz_got)]
    pallas_call x6, Pallas kernels: 80 us -> 84.2 us  [call_de(): pl.pallas_call(functools.partial(de_kernel, offset, rows, got_offset if g...]
    unnamed x69 -> x36, local copies, waits for them, and re-layouts: 10.9 us -> 7.14 us
  transfers between devices with their start and end apart: 48 -> 34, of which waited for: 26 -> 15; matrix products, arithmetic and copies ran while one was open for 8% -> 3% of each run, Pallas kernels for 29% -> 40%
where the time goes in v2:
time: 335 us; the launch traced here: 333 us
  Pallas kernels  196 us (59%)
  waiting for transfers between devices  78.4 us (23%)
  starting transfers between devices  36.4 us (11%)
  local copies, waits for them, and re-layouts  13 us (4%)
  other arithmetic  4.64 us (1%)
  between operations  4.54 us (1%)
    pallas_call x6, Pallas kernels, call_de(): pl.pallas_call(functools.partial(de_kernel, offset, rows, got_offset if g...  84.2 us
    ppermute x34, waiting for transfers between devices, flip(): return lax.ppermute(x, axis, [(k, k ^ bits) for k in range(n)])  78.4 us
    pallas_call x2, Pallas kernels, call_logits(): pl.pallas_call(functools.partial(logits_kernel, count, order, len(pieces)...  62.6 us
    ppermute x34, starting transfers between devices, flip(): return lax.ppermute(x, axis, [(k, k ^ bits) for k in range(n)])  36.4 us
    pallas_call x1, Pallas kernels, call_dz(): pl.pallas_call(dz_kernel, grid_spec=spec, out_shape=[half, half, jax.Shap...  28.5 us
    pallas_call x2, Pallas kernels, call_lse(): pl.pallas_call(lse_kernel, in_specs=[vmem, vmem, vmem], out_specs=vmem, o...  10.8 us
    unnamed x36, local copies, waits for them, and re-layouts  7.14 us
  transfers between devices with their start and end apart: 34, of which 15 were waited for; matrix products, arithmetic and copies ran while one was open for 3% of the time, Pallas kernels for 40%

profile of v2, /device:TPU:0, one launch (start us, length us, event | category | flops | bytes accessed | tf_op | source)
XLA Modules:
  0.0 333.2 jit_solution(15327860271387697506)
XLA Ops:
  2.1 3.4 %norm.1 = (f32[4,256,768]{2,1,0:T(8,128)}, f32[256,128]{1,0:T(8,128)S(1)}, f32[256,768]{1,0:T(8,128)S(1)}, f32[256,768]{1,0:T(8,128)S(1)}) custom-call(s32[6]{0:T(128)S(1)} %stack.49.pick_ref, bf16[4,256,768]{2,1,0:T(8,128)(2,1)S(1)} %bitcast.76), custom_call_target="tpu_custom_call" | custom-call | flops 10000000 | bytes 8000000 | tf_op jit(solution)/shard_map/norm/pallas_call | solution.py:258
  6.9 2.5 collective-permute-start.1
  9.7 1.9 collective-permute-start.20
  18.9 11.1 %collective-permute-done.20.rest_0_ = f32[256,768]{1,0:T(8,128)S(1)} collective-permute-done((f32[256,768]{1,0:T(8,128)S(1)}, f32[256,768]{1,0:T(8,128)S(1)}, u32[]{:S(2)}, u32[]{:S(2)}) %collective-permute-start.20) | collective-permute-done | bytes 786464 | tf_op jit(solution)/shard_map/ppermute | solution.py:470
  30.1 1.9 collective-permute-start.21
  32.0 1.6 collective-permute-start.22
  35.2 11.4 %collective-permute-done.23.rest_3_ = f32[256,768]{1,0:T(8,128)} collective-permute-done((f32[256,768]{1,0:T(8,128)S(1)}, f32[256,768]{1,0:T(8,128)}, u32[]{:S(2)}, u32[]{:S(2)}) %collective-permute-start.23) | collective-permute-done | bytes 786464 | tf_op jit(solution)/shard_map/ppermute | solution.py:470
  46.6 2.2 collective-permute-done.21.rest_1_
  49.9 24.5 %logits_near.1 = (f32[8,6288,512]{2,1,0:T(8,128)}, bf16[8,512,768]{2,1,0:T(8,128)(2,1)}, f32[4,2,512]{2,1,0:T(2,128)}) custom-call(s32[40]{0:T(128)} %concatenate.11.idx_ref, bf16[12576,768]{1,0:T(8,128)(2,1)} %e_ref.5, f32[1,768]{1,0:T(1,128)} %broadcast_in_dim.63.gamma_ref, f32[1,768]{1,0:T(1,128)} %broadcast_in_dim.64.beta_ref, ...), custom_call_target="tpu_custom_call" | custom-call | flops 14835253248 | bytes 38633472 | tf_op jit(solution)/shard_map/logits_near/pallas_call | solution.py:356
  75.1 5.5 %shard_map.101.tok_ref = f32[4,2,512]{2,1,0:T(2,128)S(1)} custom-call(f32[4,2,512]{2,1,0:T(2,128)S(1)} %copy-done.10, s32[4,1,512]{2,1,0:T(1,128)S(1)} %slice.65.lab_ref, f32[1,512]{1,0:T(1,128)S(1)} %broadcast_in_dim.68.scale_ref), custom_call_target="tpu_custom_call" | custom-call | flops 10000000 | bytes 1000000 | tf_op jit(solution)/shard_map/pallas_call | solution.py:224
  81.3 28.5 %dz_part.1 = (f32[4,256,768]{2,1,0:T(8,128)}, f32[4,256,768]{2,1,0:T(8,128)}, f32[4,1,512]{2,1,0:T(1,128)}, f32[8,6288,512]{2,1,0:T(8,128)}) custom-call(s32[40]{0:T(128)} %concatenate.11.idx_ref, bf16[12576,768]{1,0:T(8,128)(2,1)} %e_ref.5, f32[8,6288,512]{2,1,0:T(8,128)} %get-tuple-element.43.l_ref, ...), custom_call_target="tpu_custom_call", output_to_operand_aliasing={{3}: (2, {})} | custom-call | flops 14835253248 | bytes 38633472 | tf_op jit(solution)/shard_map/dz_part/pallas_call | solution.py:392
  112.5 38.1 %logits_far.1 = (f32[8,6288,512]{2,1,0:T(8,128)}, bf16[8,512,768]{2,1,0:T(8,128)(2,1)}, f32[4,2,512]{2,1,0:T(2,128)}) custom-call(s32[40]{0:T(128)} %concatenate.11.idx_ref, bf16[12576,768]{1,0:T(8,128)(2,1)} %e_ref.5, f32[1,768]{1,0:T(1,128)} %broadcast_in_dim.63.gamma_ref, ...), custom_call_target="tpu_custom_call", output_to_operand_aliasing={{0}: (12, {}), {1}: (13, {})} | custom-call | flops 14835253248 | bytes 38633472 | tf_op jit(solution)/shard_map/logits_far/pallas_call | solution.py:356
  151.4 5.3 %shard_map.102 = f32[4,2,512]{2,1,0:T(2,128)S(1)} custom-call(f32[4,2,512]{2,1,0:T(2,128)S(1)} %copy-done.9, s32[4,1,512]{2,1,0:T(1,128)S(1)} %slice.73.lab_ref, f32[1,512]{1,0:T(1,128)S(1)} %broadcast_in_dim.68.scale_ref), custom_call_target="tpu_custom_call" | custom-call | flops 10000000 | bytes 1000000 | tf_op jit(solution)/shard_map/pallas_call | solution.py:224
  156.7 2.8 copy-done
  159.5 13.1 %shard_map.103 = (f32[1048,768]{1,0:T(8,128)S(1)}, f32[12576,768]{1,0:T(8,128)}) custom-call(s32[40]{0:T(128)S(1)} %copy-done.7, f32[8,6288,512]{2,1,0:T(8,128)} %get-tuple-element.62.l_ref, bf16[8,512,768]{2,1,0:T(8,128)(2,1)S(1)} %copy-done, f32[8,2,512]{2,1,0:T(2,128)S(1)} %pad_maximum_fusion.tok_ref, s32[8,1,512]{2,1,0:T(1,128)S(1)} %reshape.131.lab_ref), custom_call_target="tpu_custom_call" | custom-call | flops 4120903680 | bytes 10731520 | tf_op jit(solution)/shard_map/pallas_call | solution.py:421
  172.7 13.1 %shard_map.104 = (f32[1048,768]{1,0:T(8,128)S(1)}, f32[12576,768]{1,0:T(8,128)}) custom-call(s32[40]{0:T(128)S(1)} %copy-done.7, f32[8,6288,512]{2,1,0:T(8,128)} %get-tuple-element.62.l_ref, bf16[8,512,768]{2,1,0:T(8,128)(2,1)S(1)} %copy-done, f32[8,2,512]{2,1,0:T(2,128)S(1)} %pad_maximum_fusion.tok_ref, ...), custom_call_target="tpu_custom_call", output_to_operand_aliasing={{1}: (5, {})} | custom-call | flops 4120903680 | bytes 10731520 | tf_op jit(solution)/shard_map/pallas_call | solution.py:421
  186.2 14.2 %shard_map.105 = (f32[1048,768]{1,0:T(8,128)S(1)}, f32[12576,768]{1,0:T(8,128)}) custom-call(s32[40]{0:T(128)S(1)} %copy-done.7, f32[8,6288,512]{2,1,0:T(8,128)} %get-tuple-element.62.l_ref, bf16[8,512,768]{2,1,0:T(8,128)(2,1)S(1)} %copy-done, f32[8,2,512]{2,1,0:T(2,128)S(1)} %pad_maximum_fusion.tok_ref, ...), custom_call_target="tpu_custom_call", output_to_operand_aliasing={{1}: (6, {})} | custom-call | flops 4120903680 | bytes 10731520 | tf_op jit(solution)/shard_map/pallas_call | solution.py:421
  200.6 15.5 %shard_map.106 = (f32[1048,768]{1,0:T(8,128)S(1)}, f32[12576,768]{1,0:T(8,128)}) custom-call(s32[40]{0:T(128)S(1)} %copy-done.7, f32[8,6288,512]{2,1,0:T(8,128)} %get-tuple-element.62.l_ref, bf16[8,512,768]{2,1,0:T(8,128)(2,1)S(1)} %copy-done, f32[8,2,512]{2,1,0:T(2,128)S(1)} %pad_maximum_fusion.tok_ref, ...), custom_call_target="tpu_custom_call", output_to_operand_aliasing={{1}: (6, {})} | custom-call | flops 4120903680 | bytes 10731520 | tf_op jit(solution)/shard_map/pallas_call | solution.py:421
  217.0 14.2 %shard_map.107 = (f32[1048,768]{1,0:T(8,128)S(1)}, f32[12576,768]{1,0:T(8,128)}) custom-call(s32[40]{0:T(128)S(1)} %copy-done.7, f32[8,6288,512]{2,1,0:T(8,128)} %get-tuple-element.62.l_ref, bf16[8,512,768]{2,1,0:T(8,128)(2,1)S(1)} %bitcast.75, f32[8,2,512]{2,1,0:T(2,128)S(1)} %pad_maximum_fusion.tok_ref, ...), custom_call_target="tpu_custom_call", output_to_operand_aliasing={{1}: (6, {})} | custom-call | flops 4120903680 | bytes 10731520 | tf_op jit(solution)/shard_map/pallas_call | solution.py:421
  231.2 14.2 %shard_map.108 = (f32[1048,768]{1,0:T(8,128)S(1)}, f32[12576,768]{1,0:T(8,128)}) custom-call(s32[40]{0:T(128)S(1)} %copy-done.7, f32[8,6288,512]{2,1,0:T(8,128)} %get-tuple-element.62.l_ref, bf16[8,512,768]{2,1,0:T(8,128)(2,1)S(1)} %bitcast.75, f32[8,2,512]{2,1,0:T(2,128)S(1)} %pad_maximum_fusion.tok_ref, ...), custom_call_target="tpu_custom_call", output_to_operand_aliasing={{1}: (6, {})} | custom-call | flops 4120903680 | bytes 10731520 | tf_op jit(solution)/shard_map/pallas_call | solution.py:421
  248.7 17.6 %collective-permute-done.5 = f32[2,128,768]{2,1,0:T(8,128)S(1)} collective-permute-done((f32[2,128,768]{2,1,0:T(8,128)S(1)}, f32[2,128,768]{2,1,0:T(8,128)S(1)}, u32[]{:S(2)}, u32[]{:S(2)}) %collective-permute-start.5) | collective-permute-done | bytes 786464 | tf_op jit(solution)/shard_map/ppermute | solution.py:470
  266.6 1.5 collective-permute-start.7
  269.0 8.1 %collective-permute-done.7.a_got_ref = f32[128,768]{1,0:T(8,128)S(1)} collective-permute-done((f32[128,768]{1,0:T(8,128)S(1)}, f32[128,768]{1,0:T(8,128)S(1)}, u32[]{:S(2)}, u32[]{:S(2)}) %collective-permute-start.7) | collective-permute-done | bytes 393248 | tf_op jit(solution)/shard_map/ppermute | solution.py:470
  280.3 12.5 %collective-permute-start.10 = (f32[8,768]{1,0:T(8,128)S(1)}, f32[8,768]{1,0:T(8,128)S(1)}, u32[]{:S(2)}, u32[]{:S(2)}) collective-permute-start(f32[8,768]{1,0:T(8,128)S(1)} %add.96), channel_id=1, source_target_pairs={{0,2},{1,3},{2,0},{3,1},{4,6},{5,7},{6,4},{7,5},{8,10},{9,11},{10,... | collective-permute-start | bytes 73736 | tf_op jit(solution)/shard_map/ppermute | solution.py:470
  292.9 1.8 collective-permute-done.10
  295.2 1.5 collective-permute-start.13
  302.3 8.2 %collective-permute-done.14.refs_2_ = f32[128,768]{1,0:T(8,128)S(1)} collective-permute-done((f32[128,768]{1,0:T(8,128)S(1)}, f32[128,768]{1,0:T(8,128)S(1)}, u32[]{:S(2)}, u32[]{:S(2)}) %collective-permute-start.14) | collective-permute-done | bytes 393248 | tf_op jit(solution)/shard_map/ppermute | solution.py:470
  311.0 5.6 %collective-permute-done.15.refs_3_ = f32[128,768]{1,0:T(8,128)S(1)} collective-permute-done((f32[128,768]{1,0:T(8,128)S(1)}, f32[128,768]{1,0:T(8,128)S(1)}, u32[]{:S(2)}, u32[]{:S(2)}) %collective-permute-start.15) | collective-permute-done | bytes 393248 | tf_op jit(solution)/shard_map/ppermute | solution.py:470
  319.5 7.2 %collective-permute-done.18.refs_6_ = f32[128,768]{1,0:T(8,128)S(1)} collective-permute-done((f32[128,768]{1,0:T(8,128)S(1)}, f32[128,768]{1,0:T(8,128)S(1)}, u32[]{:S(2)}, u32[]{:S(2)}) %collective-permute-start.18) | collective-permute-done | bytes 393248 | tf_op jit(solution)/shard_map/ppermute | solution.py:470
  326.7 1.8 round.1
  328.5 2.2 place.2.de_ref
  330.8 2.2 place.3
  (135 shorter events, 33.4 us)
Async XLA Ops:
  5.5 44.4 %collective-permute-start.3 = (f32[4,256,768]{2,1,0:T(8,128)}, f32[4,256,768]{2,1,0:T(8,128)}, u32[]{:S(2)}, u32[]{:S(2)}) collective-permute-start(f32[4,256,768]{2,1,0:T(8,128)} %get-tuple-element.42.rest_0_), channel_id=1, source_target_pairs={{0,1},{1,0},{2,3},{3,2},{4,5},{5,4},{6,7},{7,6},{8,9},{9,8},{10,11... | collective-permute-start | bytes 9437192 | tf_op jit(solution)/shard_map/ppermute | solution.py:470
  6.9 8.2 %collective-permute-start.1 = (s32[1024]{0:T(1024)S(1)}, s32[1024]{0:T(1024)S(1)}, u32[]{:S(2)}, u32[]{:S(2)}) collective-permute-start(s32[1024]{0:T(1024)S(1)} %bitcast.79), channel_id=1, source_target_pairs={{0,2},{1,3},{2,0},{3,1},{4,6},{5,7},{6,4},{7,5},{8,10},{9,11},{10,... | collective-permute-start | bytes 12296 | tf_op jit(solution)/shard_map/ppermute | solution.py:470
  9.4 5.7 %collective-permute-start.2 = (s32[1024]{0:T(1024)S(1)}, s32[1024]{0:T(1024)S(1)}, u32[]{:S(2)}, u32[]{:S(2)}) collective-permute-start(s32[1024]{0:T(1024)S(1)} %bitcast.80), channel_id=1, source_target_pairs={{0,3},{1,2},{2,1},{3,0},{4,7},{5,6},{6,5},{7,4},{8,11},{9,10},{10,... | collective-permute-start | bytes 12296 | tf_op jit(solution)/shard_map/ppermute | solution.py:470
  9.6 5.4 %collective-permute-start = (s32[1024]{0:T(1024)S(1)}, s32[1024]{0:T(1024)S(1)}, u32[]{:S(2)}, u32[]{:S(2)}) collective-permute-start(s32[1024]{0:T(1024)S(1)} %bitcast.81), channel_id=1, source_target_pairs={{0,1},{1,0},{2,3},{3,2},{4,5},{5,4},{6,7},{7,6},{8,9},{9,8},{10,11... | collective-permute-start | bytes 12296 | tf_op jit(solution)/shard_map/ppermute | solution.py:470
  9.7 20.4 %collective-permute-start.20 = (f32[256,768]{1,0:T(8,128)S(1)}, f32[256,768]{1,0:T(8,128)S(1)}, u32[]{:S(2)}, u32[]{:S(2)}) collective-permute-start(f32[256,768]{1,0:T(8,128)S(1)} %get-tuple-element.51.hat_ref), channel_id=1, source_target_pairs={{0,2},{1,3},{2,0},{3,1},{4,6},{5,7},{6,4},{7,5},{8,10},{9,11},{10,... | collective-permute-start | bytes 2359304 | tf_op jit(solution)/shard_map/ppermute | solution.py:470
  15.0 31.6 %collective-permute-start.23 = (f32[256,768]{1,0:T(8,128)S(1)}, f32[256,768]{1,0:T(8,128)}, u32[]{:S(2)}, u32[]{:S(2)}) collective-permute-start(f32[256,768]{1,0:T(8,128)S(1)} %get-tuple-element.59), channel_id=1, source_target_pairs={{0,2},{1,3},{2,0},{3,1},{4,6},{5,7},{6,4},{7,5},{8,10},{9,11},{10,... | collective-permute-start | bytes 2359304 | tf_op jit(solution)/shard_map/ppermute | solution.py:470
  30.1 18.7 %collective-permute-start.21 = (f32[256,768]{1,0:T(8,128)S(1)}, f32[256,768]{1,0:T(8,128)}, u32[]{:S(2)}, u32[]{:S(2)}) collective-permute-start(f32[256,768]{1,0:T(8,128)S(1)} %collective-permute-done.20.rest_0_), channel_id=1, source_target_pairs={{0,4},{4,0},{8,12},{12,8},{1,5},{5,1},{9,13},{13,9},{2,6},{6,2},{1... | collective-permute-start | bytes 2359304 | tf_op jit(solution)/shard_map/ppermute | solution.py:470
  32.0 17.9 %collective-permute-start.22 = (f32[256,768]{1,0:T(8,128)S(1)}, f32[256,768]{1,0:T(8,128)}, u32[]{:S(2)}, u32[]{:S(2)}) collective-permute-start(f32[256,768]{1,0:T(8,128)S(1)} %collective-permute-done.20.rest_0_), channel_id=1, source_target_pairs={{0,8},{4,12},{8,0},{12,4},{1,9},{5,13},{9,1},{13,5},{2,10},{6,14},... | collective-permute-start | bytes 2359304 | tf_op jit(solution)/shard_map/ppermute | solution.py:470
  35.1 77.3 %collective-permute-start.24 = (f32[256,768]{1,0:T(8,128)S(1)}, f32[256,768]{1,0:T(8,128)}, u32[]{:S(2)}, u32[]{:S(2)}) collective-permute-start(f32[256,768]{1,0:T(8,128)S(1)} %collective-permute-done.20.rest_0_), channel_id=1, source_target_pairs={{0,1},{1,0},{2,3},{3,2},{4,5},{5,4},{6,7},{7,6},{8,9},{9,8},{10,11... | collective-permute-start | bytes 2359304 | tf_op jit(solution)/shard_map/ppermute | solution.py:470
  46.6 65.9 %collective-permute-start.27 = (f32[256,768]{1,0:T(8,128)}, f32[256,768]{1,0:T(8,128)}, u32[]{:S(2)}, u32[]{:S(2)}) collective-permute-start(f32[256,768]{1,0:T(8,128)} %collective-permute-done.23.rest_3_), channel_id=1, source_target_pairs={{0,1},{1,0},{2,3},{3,2},{4,5},{5,4},{6,7},{7,6},{8,9},{9,8},{10,11... | collective-permute-start | bytes 2359304 | tf_op jit(solution)/shard_map/ppermute | solution.py:470
  48.8 63.7 %collective-permute-start.25 = (f32[256,768]{1,0:T(8,128)}, f32[256,768]{1,0:T(8,128)}, u32[]{:S(2)}, u32[]{:S(2)}) collective-permute-start(f32[256,768]{1,0:T(8,128)} %collective-permute-done.21.rest_1_), channel_id=1, source_target_pairs={{0,1},{1,0},{2,3},{3,2},{4,5},{5,4},{6,7},{7,6},{8,9},{9,8},{10,11... | collective-permute-start | bytes 2359304 | tf_op jit(solution)/shard_map/ppermute | solution.py:470
  49.9 62.6 %collective-permute-start.26 = (f32[256,768]{1,0:T(8,128)}, f32[256,768]{1,0:T(8,128)}, u32[]{:S(2)}, u32[]{:S(2)}) collective-permute-start(f32[256,768]{1,0:T(8,128)} %collective-permute-done.22.rest_2_), channel_id=1, source_target_pairs={{0,1},{1,0},{2,3},{3,2},{4,5},{5,4},{6,7},{7,6},{8,9},{9,8},{10,11... | collective-permute-start | bytes 2359304 | tf_op jit(solution)/shard_map/ppermute | solution.py:470
  172.5 13.7 %collective-permute-start.29 = (f32[1048,768]{1,0:T(8,128)S(1)}, f32[1048,768]{1,0:T(8,128)S(1)}, u32[]{:S(2)}, u32[]{:S(2)}) collective-permute-start(f32[1048,768]{1,0:T(8,128)S(1)} %get-tuple-element.67), channel_id=1, source_target_pairs={{0,1},{1,0},{2,3},{3,2},{4,5},{5,4},{6,7},{7,6},{8,9},{9,8},{10,11... | collective-permute-start | bytes 9658376 | tf_op jit(solution)/shard_map/ppermute | solution.py:470
  185.8 14.8 %collective-permute-start.28 = (f32[1048,768]{1,0:T(8,128)S(1)}, f32[1048,768]{1,0:T(8,128)S(1)}, u32[]{:S(2)}, u32[]{:S(2)}) collective-permute-start(f32[1048,768]{1,0:T(8,128)S(1)} %get-tuple-element.66), channel_id=1, source_target_pairs={{0,1},{1,0},{2,3},{3,2},{4,5},{5,4},{6,7},{7,6},{8,9},{9,8},{10,11... | collective-permute-start | bytes 9658376 | tf_op jit(solution)/shard_map/ppermute | solution.py:470
  200.4 16.5 %collective-permute-start.31 = (f32[1048,768]{1,0:T(8,128)S(1)}, f32[1048,768]{1,0:T(8,128)S(1)}, u32[]{:S(2)}, u32[]{:S(2)}) collective-permute-start(f32[1048,768]{1,0:T(8,128)S(1)} %get-tuple-element.71), channel_id=1, source_target_pairs={{0,1},{1,0},{2,3},{3,2},{4,5},{5,4},{6,7},{7,6},{8,9},{9,8},{10,11... | collective-permute-start | bytes 9658376 | tf_op jit(solution)/shard_map/ppermute | solution.py:470
  216.1 15.2 %collective-permute-start.30 = (f32[1048,768]{1,0:T(8,128)S(1)}, f32[1048,768]{1,0:T(8,128)S(1)}, u32[]{:S(2)}, u32[]{:S(2)}) collective-permute-start(f32[1048,768]{1,0:T(8,128)S(1)} %get-tuple-element.70), channel_id=1, source_target_pairs={{0,1},{1,0},{2,3},{3,2},{4,5},{5,4},{6,7},{7,6},{8,9},{9,8},{10,11... | collective-permute-start | bytes 9658376 | tf_op jit(solution)/shard_map/ppermute | solution.py:470
  216.5 29.5 %collective-permute-start.4 = (f32[4,256,768]{2,1,0:T(8,128)S(1)}, f32[4,256,768]{2,1,0:T(8,128)S(1)}, u32[]{:S(2)}, u32[]{:S(2)}) collective-permute-start(f32[4,256,768]{2,1,0:T(8,128)S(1)} %copy-done.15), channel_id=1, source_target_pairs={{0,1},{1,0},{2,3},{3,2},{4,5},{5,4},{6,7},{7,6},{8,9},{9,8},{10,11... | collective-permute-start | bytes 9437192 | tf_op jit(solution)/shard_map/ppermute | solution.py:470
  245.4 85.4 %collective-permute-start.32 = (f32[1048,768]{1,0:T(8,128)S(1)}, f32[1048,768]{1,0:T(8,128)S(1)}, u32[]{:S(2)}, u32[]{:S(2)}) collective-permute-start(f32[1048,768]{1,0:T(8,128)S(1)} %get-tuple-element.74), channel_id=1, source_target_pairs={{0,1},{1,0},{2,3},{3,2},{4,5},{5,4},{6,7},{7,6},{8,9},{9,8},{10,11... | collective-permute-start | bytes 9658376 | tf_op jit(solution)/shard_map/ppermute | solution.py:470
  245.9 82.7 %collective-permute-start.33 = (f32[1048,768]{1,0:T(8,128)S(1)}, f32[1048,768]{1,0:T(8,128)S(1)}, u32[]{:S(2)}, u32[]{:S(2)}) collective-permute-start(f32[1048,768]{1,0:T(8,128)S(1)} %get-tuple-element.75), channel_id=1, source_target_pairs={{0,1},{1,0},{2,3},{3,2},{4,5},{5,4},{6,7},{7,6},{8,9},{9,8},{10,11... | collective-permute-start | bytes 9658376 | tf_op jit(solution)/shard_map/ppermute | solution.py:470
  246.4 19.9 %collective-permute-start.5 = (f32[2,128,768]{2,1,0:T(8,128)S(1)}, f32[2,128,768]{2,1,0:T(8,128)S(1)}, u32[]{:S(2)}, u32[]{:S(2)}) collective-permute-start(f32[2,128,768]{2,1,0:T(8,128)S(1)} %fusion.3), channel_id=1, source_target_pairs={{0,4},{4,0},{8,12},{12,8},{1,5},{5,1},{9,13},{13,9},{2,6},{6,2},{1... | collective-permute-start | bytes 2359304 | tf_op jit(solution)/shard_map/ppermute | solution.py:470
  247.2 20.8 %collective-permute-start.6 = (f32[2,128,768]{2,1,0:T(8,128)S(1)}, f32[2,128,768]{2,1,0:T(8,128)S(1)}, u32[]{:S(2)}, u32[]{:S(2)}) collective-permute-start(f32[2,128,768]{2,1,0:T(8,128)S(1)} %fusion), channel_id=1, source_target_pairs={{0,8},{4,12},{8,0},{12,4},{1,9},{5,13},{9,1},{13,5},{2,10},{6,14},... | collective-permute-start | bytes 2359304 | tf_op jit(solution)/shard_map/ppermute | solution.py:470
  266.6 10.6 %collective-permute-start.7 = (f32[128,768]{1,0:T(8,128)S(1)}, f32[128,768]{1,0:T(8,128)S(1)}, u32[]{:S(2)}, u32[]{:S(2)}) collective-permute-start(f32[128,768]{1,0:T(8,128)S(1)} %get-tuple-element.87), channel_id=1, source_target_pairs={{0,8},{4,12},{8,0},{12,4},{1,9},{5,13},{9,1},{13,5},{2,10},{6,14},... | collective-permute-start | bytes 1179656 | tf_op jit(solution)/shard_map/ppermute | solution.py:470
  268.3 10.3 %collective-permute-start.8 = (f32[128,768]{1,0:T(8,128)S(1)}, f32[128,768]{1,0:T(8,128)S(1)}, u32[]{:S(2)}, u32[]{:S(2)}) collective-permute-start(f32[128,768]{1,0:T(8,128)S(1)} %get-tuple-element.85), channel_id=1, source_target_pairs={{0,4},{4,0},{8,12},{12,8},{1,5},{5,1},{9,13},{13,9},{2,6},{6,2},{1... | collective-permute-start | bytes 1179656 | tf_op jit(solution)/shard_map/ppermute | solution.py:470
  280.3 14.4 %collective-permute-start.10 = (f32[8,768]{1,0:T(8,128)S(1)}, f32[8,768]{1,0:T(8,128)S(1)}, u32[]{:S(2)}, u32[]{:S(2)}) collective-permute-start(f32[8,768]{1,0:T(8,128)S(1)} %add.96), channel_id=1, source_target_pairs={{0,2},{1,3},{2,0},{3,1},{4,6},{5,7},{6,4},{7,5},{8,10},{9,11},{10,... | collective-permute-start | bytes 73736 | tf_op jit(solution)/shard_map/ppermute | solution.py:470
  295.2 5.0 %collective-permute-start.13 = (f32[8,768]{1,0:T(8,128)S(1)}, f32[8,768]{1,0:T(8,128)S(1)}, u32[]{:S(2)}, u32[]{:S(2)}) collective-permute-start(f32[8,768]{1,0:T(8,128)S(1)} %add.97), channel_id=1, source_target_pairs={{0,12},{4,8},{8,4},{12,0},{1,13},{5,9},{9,5},{13,1},{2,14},{6,10},... | collective-permute-start | bytes 73736 | tf_op jit(solution)/shard_map/ppermute | solution.py:470
  296.8 4.5 %collective-permute-start.11 = (f32[8,768]{1,0:T(8,128)S(1)}, f32[8,768]{1,0:T(8,128)S(1)}, u32[]{:S(2)}, u32[]{:S(2)}) collective-permute-start(f32[8,768]{1,0:T(8,128)S(1)} %add.97), channel_id=1, source_target_pairs={{0,4},{4,0},{8,12},{12,8},{1,5},{5,1},{9,13},{13,9},{2,6},{6,2},{1... | collective-permute-start | bytes 73736 | tf_op jit(solution)/shard_map/ppermute | solution.py:470
  298.5 12.0 %collective-permute-start.14 = (f32[128,768]{1,0:T(8,128)S(1)}, f32[128,768]{1,0:T(8,128)S(1)}, u32[]{:S(2)}, u32[]{:S(2)}) collective-permute-start(f32[128,768]{1,0:T(8,128)S(1)} %get-tuple-element.56.refs_0_), channel_id=1, source_target_pairs={{0,4},{4,0},{8,12},{12,8},{1,5},{5,1},{9,13},{13,9},{2,6},{6,2},{1... | collective-permute-start | bytes 1179656 | tf_op jit(solution)/shard_map/ppermute | solution.py:470
  300.2 16.4 %collective-permute-start.15 = (f32[128,768]{1,0:T(8,128)S(1)}, f32[128,768]{1,0:T(8,128)S(1)}, u32[]{:S(2)}, u32[]{:S(2)}) collective-permute-start(f32[128,768]{1,0:T(8,128)S(1)} %get-tuple-element.57.refs_1_), channel_id=1, source_target_pairs={{0,4},{4,0},{8,12},{12,8},{1,5},{5,1},{9,13},{13,9},{2,6},{6,2},{1... | collective-permute-start | bytes 1179656 | tf_op jit(solution)/shard_map/ppermute | solution.py:470
  301.2 15.9 %collective-permute-start.17 = (f32[128,768]{1,0:T(8,128)S(1)}, f32[128,768]{1,0:T(8,128)S(1)}, u32[]{:S(2)}, u32[]{:S(2)}) collective-permute-start(f32[128,768]{1,0:T(8,128)S(1)} %get-tuple-element.57.refs_1_), channel_id=1, source_target_pairs={{0,8},{4,12},{8,0},{12,4},{1,9},{5,13},{9,1},{13,5},{2,10},{6,14},... | collective-permute-start | bytes 1179656 | tf_op jit(solution)/shard_map/ppermute | solution.py:470
  310.5 9.0 %collective-permute-start.16 = (f32[128,768]{1,0:T(8,128)S(1)}, f32[128,768]{1,0:T(8,128)S(1)}, u32[]{:S(2)}, u32[]{:S(2)}) collective-permute-start(f32[128,768]{1,0:T(8,128)S(1)} %get-tuple-element.56.refs_0_), channel_id=1, source_target_pairs={{0,8},{4,12},{8,0},{12,4},{1,9},{5,13},{9,1},{13,5},{2,10},{6,14},... | collective-permute-start | bytes 1179656 | tf_op jit(solution)/shard_map/ppermute | solution.py:470
  316.6 10.1 %collective-permute-start.18 = (f32[128,768]{1,0:T(8,128)S(1)}, f32[128,768]{1,0:T(8,128)S(1)}, u32[]{:S(2)}, u32[]{:S(2)}) collective-permute-start(f32[128,768]{1,0:T(8,128)S(1)} %collective-permute-done.14.refs_2_), channel_id=1, source_target_pairs={{0,8},{4,12},{8,0},{12,4},{1,9},{5,13},{9,1},{13,5},{2,10},{6,14},... | collective-permute-start | bytes 1179656 | tf_op jit(solution)/shard_map/ppermute | solution.py:470
  317.2 9.5 %collective-permute-start.19 = (f32[128,768]{1,0:T(8,128)S(1)}, f32[128,768]{1,0:T(8,128)S(1)}, u32[]{:S(2)}, u32[]{:S(2)}) collective-permute-start(f32[128,768]{1,0:T(8,128)S(1)} %collective-permute-done.17.refs_5_), channel_id=1, source_target_pairs={{0,4},{4,0},{8,12},{12,8},{1,5},{5,1},{9,13},{13,9},{2,6},{6,2},{1... | collective-permute-start | bytes 1179656 | tf_op jit(solution)/shard_map/ppermute | solution.py:470
  (20 other events, 352.0 us)

commit v3 on v2

--- a/solution.py
+++ b/solution.py
@@ -14,6 +14,7 @@
 BIG = 1e30
 VMEM_LIMIT = 62 * 1024 * 1024
 DE_VMEM = 16 * 1024 * 1024
+EARLY_OUT = True
 
 
 CORE, NEAR_PAIRS, FAR_PAIRS, ALL_PAIRS, ROW_START = 0, 1, 2, 3, 4
@@ -24,14 +25,26 @@
     return [(start, min(size, total - start)) for start in range(0, total, size)]
 
 
+def split_copy(source, target, sem, size):
+    return [pltpu.make_async_copy(source.at[pl.ds(a, n), :], target.at[pl.ds(a, n), :], sem) for a, n in chunk_list(target.shape[0], size)]
+
+
+def start(copies):
+    for copy in copies:
+        copy.start()
+
+
 def last(i, count):
     return jnp.minimum(i, count - 1)
 
 
-def logits_kernel(count, order, n_pieces, idx_ref, e_ref, gamma_ref, beta_ref, *rest):
+def logits_kernel(count, base, order, n_pieces, idx_ref, e_hbm, gamma_ref, beta_ref, *rest):
     pieces = rest[:n_pieces]
-    l_ref, zc_ref, st_ref, x_ref, sem = rest[-5:]
+    l_hbm, zc_ref, st_ref, x_ref, e_ref, l_ref, sem, e_sem, l_sem = rest[-9:]
     i = pl.program_id(0)
+    live = i < idx_ref[count]
+    rows = e_ref.shape[0]
+    slot = i % 2
 
     def copies(block, slot, h):
         target = x_ref.at[slot, pl.ds(h * BLOCK, BLOCK), :]
@@ -44,37 +57,55 @@
             for chosen, copy in copies(idx_ref[order + 2 * pair + h], pair % 2, h):
                 pl.when(chosen)(copy.start)
 
-    pl.when(i == 0)(lambda: fetch(0))
+    def flush(k):
+        pltpu.make_async_copy(l_ref.at[k], l_hbm.at[0], l_sem.at[k]).wait()
+
+    @pl.when(i == 0)
+    def _():
+        fetch(0)
+        table = e_hbm.at[pl.ds(pl.multiple_of(idx_ref[CORE] * rows, 16), rows), :]
+        start(split_copy(table, e_ref, e_sem, 528))
+        pltpu.make_async_copy(table, e_ref, e_sem).wait()
+
     pl.when(i + 1 < idx_ref[count])(lambda: fetch(i + 1))
-
-    @pl.when(i < idx_ref[count])
+    pl.when(live & (i >= 2))(lambda: flush(slot))
+
+    @pl.when(live)
     def _():
         for h in range(2):
-            copies(0, i % 2, h)[0][1].wait()
-        zc_ref[0] = (x_ref[i % 2] * gamma_ref[...] + beta_ref[...]).astype(jnp.bfloat16)
-        logits_step(e_ref, l_ref, zc_ref, st_ref)
-
-
-def logits_step(e_ref, l_ref, zc_ref, st_ref):
+            copies(0, slot, h)[0][1].wait()
+        zc_ref[0] = (x_ref[slot] * gamma_ref[...] + beta_ref[...]).astype(jnp.bfloat16)
+        logits_step(e_ref, l_ref.at[slot], zc_ref, st_ref, split_copy(l_ref.at[slot], l_hbm.at[base + i], l_sem.at[slot], 528))
+
+    @pl.when(i == idx_ref[count] - 1)
+    def _():
+        flush(slot)
+        pl.when(i > 0)(lambda: flush(1 - slot))
+
+
+def logits_step(e_ref, l_ref, zc_ref, st_ref, out):
     rows = e_ref.shape[0]
     size = 528
-
     top = jnp.full((1, PAIR), -BIG, jnp.float32)
     total = jnp.zeros((1, PAIR), jnp.float32)
 
     def add(start, n, old_top, top, total):
-        return total * jnp.exp(old_top - top) + jnp.sum(jnp.exp(l_ref[0, start:start + n, :] - top), axis=0, keepdims=True)
+        return total * jnp.exp(old_top - top) + jnp.sum(jnp.exp(l_ref[start:start + n, :] - top), axis=0, keepdims=True)
 
     waiting = None
     for start, n in chunk_list(rows, size):
         tile = lax.dot_general(e_ref[start:start + n, :], zc_ref[0], (((1,), (1,)), ((), ())), preferred_element_type=jnp.float32)
-        l_ref[0, start:start + n, :] = tile
+        l_ref[start:start + n, :] = tile
         new_top = jnp.maximum(top, jnp.max(tile, axis=0, keepdims=True))
         if waiting is not None:
             total = add(*waiting, total)
+            if EARLY_OUT:
+                out[waiting[0] // size].start()
         waiting = (start, n, top, new_top)
         top = new_top
     total = add(*waiting, total)
+    for copy in out[-1:] if EARLY_OUT else out:
+        copy.start()
     st_ref[0, 0:1, :] = top
     st_ref[0, 1:2, :] = total
 
@@ -84,17 +115,26 @@
     return (jnp.where(is_target, probs - 1.0, probs) * weight).astype(jnp.bfloat16)
 
 
-def dz_kernel(idx_ref, e_ref, l_ref, tok_ref, lab_ref, own_ref, mate_ref, tl_ref, l_out_ref, acc_ref, out_ref, et_ref, sem):
+def dz_kernel(idx_ref, e_hbm, l_hbm, tok_ref, lab_ref, own_ref, mate_ref, tl_ref, l_out_ref, acc_ref, out_ref, et_ref, e_ref, l_ref, sem, e_sem, l_sem):
     i = pl.program_id(0)
     rows = e_ref.shape[0]
     size = 512
     full = rows // size
+    slot = i % 2
+
+    def fetch(pair):
+        start(split_copy(l_hbm.at[pair], l_ref.at[pair % 2], l_sem.at[pair % 2], size))
 
     @pl.when(i == 0)
     def _():
+        table = e_hbm.at[pl.ds(pl.multiple_of(idx_ref[CORE] * rows, 16), rows), :]
+        start(split_copy(table, e_ref, e_sem, size))
+        fetch(0)
+        pltpu.make_async_copy(table, e_ref, e_sem).wait()
+
         def turn(k, carry):
-            start = pl.multiple_of(k * size, size)
-            et_ref[:, pl.ds(start, size)] = e_ref[pl.ds(start, size), :].T
+            at = pl.multiple_of(k * size, size)
+            et_ref[:, pl.ds(at, size)] = e_ref[pl.ds(at, size), :].T
             return carry
 
         lax.fori_loop(0, full, turn, 0)
@@ -102,7 +142,12 @@
             et_ref[:, full * size:] = e_ref[full * size:, :].T
 
     live = i < idx_ref[NEAR_PAIRS]
-    pl.when(live)(lambda: dz_step(idx_ref, et_ref, l_ref, tok_ref, lab_ref, tl_ref, acc_ref))
+    pl.when(i + 1 < idx_ref[NEAR_PAIRS])(lambda: fetch(i + 1))
+
+    @pl.when(live)
+    def _():
+        pltpu.make_async_copy(l_hbm.at[0], l_ref.at[slot], l_sem.at[slot]).wait()
+        dz_step(idx_ref, et_ref, l_ref.at[slot], tok_ref, lab_ref, tl_ref, acc_ref)
 
     @pl.when(live)
     def _():
@@ -128,7 +173,7 @@
     label = lab_ref[0] - idx_ref[ROW_START]
     target = jnp.zeros((1, PAIR), jnp.float32)
     for start, n in chunk_list(et_ref.shape[1], 1024):
-        tile = l_ref[0, start:start + n, :]
+        tile = l_ref[start:start + n, :]
         is_target = lax.broadcasted_iota(jnp.int32, (n, PAIR), 0) == label - start
         grad = grad_tile(tile, lse, weight, is_target)
         target = target + jnp.sum(jnp.where(is_target, tile, 0.0), axis=0, keepdims=True)
@@ -150,43 +195,48 @@
     def rows_at(side, start, n):
         return out_ref.at[pl.ds(pl.multiple_of(side * half + start, 8), n), :]
 
+    def source(i):
+        return l_ref.at[idx_ref[PAIR_IDS + i], pl.ds(offset, rows), :]
+
     def fetch(i):
-        return pltpu.make_async_copy(l_ref.at[idx_ref[PAIR_IDS + i], pl.ds(offset, rows), :], buf_ref.at[i % 2], sem.at[i % 2])
-
-    fetch(0).start()
+        start(split_copy(source(i), buf_ref.at[i % 3], sem.at[i % 3], 264))
+
+    fetch(0)
+    pl.when(count > 1)(lambda: fetch(1))
     got = None
     if got_ref is not None:
-        got = pltpu.make_async_copy(got_ref, rows_at(1 - core, got_offset, got_ref.shape[0]), sem.at[2])
-        got.start()
+        target = rows_at(1 - core, got_offset, got_ref.shape[0])
+        start(split_copy(got_ref, target, sem.at[3], 264))
+        got = pltpu.make_async_copy(got_ref, target, sem.at[3])
     part_ref[...] = jnp.zeros_like(part_ref)
 
     def step(i, carry):
-        fetch(i).wait()
-        pl.when(i + 1 < count)(lambda: fetch(i + 1).start())
+        pltpu.make_async_copy(source(i), buf_ref.at[i % 3], sem.at[i % 3]).wait()
+        pl.when(i + 2 < count)(lambda: fetch(i + 2))
         pair = idx_ref[PAIR_IDS + i]
         lse = tok_ref[pair, 0:1, :]
         weight = tok_ref[pair, 1:2, :]
         label = lab_ref[pair] - idx_ref[ROW_START] - offset
-        for start, n in chunk_list(rows, 528):
-            is_target = lax.broadcasted_iota(jnp.int32, (n, PAIR), 0) == label - start
-            grad = grad_tile(buf_ref[i % 2, start:start + n, :], lse, weight, is_target)
-            part_ref[start:start + n, :] += jnp.dot(grad, z_ref[pair], preferred_element_type=jnp.float32)
+        for at, n in chunk_list(rows, 528):
+            is_target = lax.broadcasted_iota(jnp.int32, (n, PAIR), 0) == label - at
+            grad = grad_tile(buf_ref[i % 3, at:at + n, :], lse, weight, is_target)
+            part_ref[at:at + n, :] += jnp.dot(grad, z_ref[pair], preferred_element_type=jnp.float32)
         return carry
 
     lax.fori_loop(0, count, step, 0)
-    own = pltpu.make_async_copy(part_ref, rows_at(core, offset, rows), sem.at[3])
-    own.start()
-    own.wait()
+    target = rows_at(core, offset, rows)
+    start(split_copy(part_ref, target, sem.at[4], 264))
+    pltpu.make_async_copy(part_ref, target, sem.at[4]).wait()
     if got is not None:
         got.wait()
 
 
 def place_kernel(got_offset, idx_ref, got_ref, de_ref, out_ref, sem):
     half = out_ref.shape[0] // 2
-    start = pl.multiple_of((1 - idx_ref[CORE]) * half + got_offset, 8)
-    copy = pltpu.make_async_copy(got_ref, out_ref.at[pl.ds(start, got_ref.shape[0]), :], sem)
-    copy.start()
-    copy.wait()
+    at = pl.multiple_of((1 - idx_ref[CORE]) * half + got_offset, 8)
+    target = out_ref.at[pl.ds(at, got_ref.shape[0]), :]
+    start(split_copy(got_ref, target, sem, 264))
+    pltpu.make_async_copy(got_ref, target, sem).wait()
 
 
 def lse_kernel(st_ref, lab_ref, scale_ref, tok_ref, got_ref, send_sem, recv_sem):
@@ -343,18 +393,25 @@
     spec = pltpu.PrefetchScalarGridSpec(
         num_scalar_prefetch=1,
         grid=(4,),
-        in_specs=[pl.BlockSpec((rows, width), lambda i, s: (s[CORE], 0), pipeline_mode=pl.Buffered(1))]
+        in_specs=[ANY]
         + [pl.BlockSpec((1, width), lambda i, s: (0, 0))] * 2 + [ANY] * (len(pieces) + len(extra)),
         out_specs=[
-            pl.BlockSpec((1, rows, PAIR), lambda i, s: (base + last(i, s[count]), 0, 0)),
+            ANY,
             pl.BlockSpec((1, PAIR, width), lambda i, s: (base + last(i, s[count]), 0, 0)),
             pl.BlockSpec((1, 2, PAIR), lambda i, s: (last(i, s[count]), 0, 0)),
         ],
-        scratch_shapes=[pltpu.VMEM((2, PAIR, width), jnp.float32), pltpu.SemaphoreType.DMA((2, 2))],
+        scratch_shapes=[
+            pltpu.VMEM((2, PAIR, width), jnp.float32),
+            pltpu.VMEM((rows, width), jnp.bfloat16),
+            pltpu.VMEM((2, rows, PAIR), jnp.float32),
+            pltpu.SemaphoreType.DMA((2, 2)),
+            pltpu.SemaphoreType.DMA,
+            pltpu.SemaphoreType.DMA((2,)),
+        ],
     )
     first = 4 + len(pieces)
     return pl.pallas_call(
-        functools.partial(logits_kernel, count, order, len(pieces)),
+        functools.partial(logits_kernel, count, base, order, len(pieces)),
         grid_spec=spec,
         out_shape=[
             jax.ShapeDtypeStruct((pairs, rows, PAIR), jnp.float32),
@@ -375,8 +432,8 @@
         num_scalar_prefetch=1,
         grid=(4,),
         in_specs=[
-            pl.BlockSpec((rows, width), lambda i, s: (s[CORE], 0), pipeline_mode=pl.Buffered(1)),
-            pl.BlockSpec((1, rows, PAIR), pick_row),
+            ANY,
+            ANY,
             pl.BlockSpec((1, 2, PAIR), pick_row),
             pl.BlockSpec((1, 1, PAIR), pick_row),
         ],
@@ -385,6 +442,10 @@
             pltpu.VMEM((width, PAIR), jnp.float32),
             pltpu.VMEM((PAIR, width), jnp.float32),
             pltpu.VMEM((width, rows), jnp.bfloat16),
+            pltpu.VMEM((rows, width), jnp.bfloat16),
+            pltpu.VMEM((2, rows, PAIR), jnp.float32),
+            pltpu.SemaphoreType.DMA((2,)),
+            pltpu.SemaphoreType.DMA,
             pltpu.SemaphoreType.DMA((2,)),
         ],
     )
@@ -416,7 +477,7 @@
         grid=(1,),
         in_specs=[ANY, whole(zc), whole(tok), whole(lab)] + extra_specs,
         out_specs=[pl.BlockSpec((rows, width), lambda i, s: (0, 0), pipeline_mode=pl.Buffered(1)), ANY],
-        scratch_shapes=[pltpu.VMEM((2, rows, PAIR), jnp.float32), pltpu.SemaphoreType.DMA((4,))],
+        scratch_shapes=[pltpu.VMEM((3, rows, PAIR), jnp.float32), pltpu.SemaphoreType.DMA((5,))],
     )
     return pl.pallas_call(
         functools.partial(de_kernel, offset, rows, got_offset if got is not None else None),

time: 335 us -> 313 us (0.934)
  Pallas kernels: 196 us -> 176 us
    pallas_call x6, Pallas kernels: 84.2 us -> 69.8 us  [call_de(): pl.pallas_call(functools.partial(de_kernel, offset, rows, got_offset if g...]
    pallas_call x2, Pallas kernels: 62.6 us -> 56.1 us  [call_logits(): pl.pallas_call(functools.partial(logits_kernel, count, base, order, len(p...]
  transfers between devices with their start and end apart: 34 -> 34, of which waited for: 15 -> 15; matrix products, arithmetic and copies ran while one was open for 3% -> 3% of each run, Pallas kernels for 40% -> 38%
where the time goes in v3:
time: 313 us
  Pallas kernels  176 us (56%)
  waiting for transfers between devices  78.5 us (25%)
  starting transfers between devices  36.2 us (12%)
  local copies, waits for them, and re-layouts  13 us (4%)
  other arithmetic  4.64 us (1%)
  between operations  4.54 us (1%)
    ppermute x34, waiting for transfers between devices, flip(): return lax.ppermute(x, axis, [(k, k ^ bits) for k in range(n)])  78.5 us
    pallas_call x6, Pallas kernels, call_de(): pl.pallas_call(functools.partial(de_kernel, offset, rows, got_offset if g...  69.8 us
    pallas_call x2, Pallas kernels, call_logits(): pl.pallas_call(functools.partial(logits_kernel, count, base, order, len(p...  56.1 us
    ppermute x34, starting transfers between devices, flip(): return lax.ppermute(x, axis, [(k, k ^ bits) for k in range(n)])  36.2 us
    pallas_call x1, Pallas kernels, call_dz(): pl.pallas_call(dz_kernel, grid_spec=spec, out_shape=[half, half, jax.Shap...  29 us
    pallas_call x2, Pallas kernels, call_lse(): pl.pallas_call(lse_kernel, in_specs=[vmem, vmem, vmem], out_specs=vmem, o...  10.9 us
    unnamed x36, local copies, waits for them, and re-layouts  7.14 us
  transfers between devices with their start and end apart: 34, of which 15 were waited for; matrix products, arithmetic and copies ran while one was open for 3% of the time, Pallas kernels for 38%

profile of v3, /device:TPU:0, one launch (start us, length us, event | category | flops | bytes accessed | tf_op | source)
XLA Modules:
  0.0 312.7 jit_solution(173760712861180160)
XLA Ops:
  2.1 3.4 %norm.1 = (f32[4,256,768]{2,1,0:T(8,128)}, f32[256,128]{1,0:T(8,128)S(1)}, f32[256,768]{1,0:T(8,128)S(1)}, f32[256,768]{1,0:T(8,128)S(1)}) custom-call(s32[6]{0:T(128)S(1)} %stack.49.pick_ref, bf16[4,256,768]{2,1,0:T(8,128)(2,1)S(1)} %bitcast.76), custom_call_target="tpu_custom_call" | custom-call | flops 10000000 | bytes 8000000 | tf_op jit(solution)/shard_map/norm/pallas_call | solution.py:308
  6.9 2.5 collective-permute-start.1
  9.7 1.9 collective-permute-start.20
  18.9 11.1 %collective-permute-done.20.rest_0_ = f32[256,768]{1,0:T(8,128)S(1)} collective-permute-done((f32[256,768]{1,0:T(8,128)S(1)}, f32[256,768]{1,0:T(8,128)S(1)}, u32[]{:S(2)}, u32[]{:S(2)}) %collective-permute-start.20) | collective-permute-done | bytes 786464 | tf_op jit(solution)/shard_map/ppermute | solution.py:531
  30.1 1.9 collective-permute-start.21
  32.0 1.6 collective-permute-start.22
  35.2 11.4 %collective-permute-done.23.rest_3_ = f32[256,768]{1,0:T(8,128)} collective-permute-done((f32[256,768]{1,0:T(8,128)S(1)}, f32[256,768]{1,0:T(8,128)}, u32[]{:S(2)}, u32[]{:S(2)}) %collective-permute-start.23) | collective-permute-done | bytes 786464 | tf_op jit(solution)/shard_map/ppermute | solution.py:531
  46.6 2.2 collective-permute-done.21.rest_1_
  49.9 21.3 %logits_near.1 = (f32[8,6288,512]{2,1,0:T(8,128)}, bf16[8,512,768]{2,1,0:T(8,128)(2,1)}, f32[4,2,512]{2,1,0:T(2,128)}) custom-call(s32[40]{0:T(128)} %concatenate.11.idx_ref, bf16[12576,768]{1,0:T(8,128)(2,1)} %e_hbm.5, f32[1,768]{1,0:T(1,128)} %broadcast_in_dim.63.gamma_ref, f32[1,768]{1,0:T(1,128)} %broadcast_in_dim.64.beta_ref, ...), custom_call_target="tpu_custom_call" | custom-call | flops 14835253248 | bytes 38633472 | tf_op jit(solution)/shard_map/logits_near/pallas_call | solution.py:413
  71.9 5.6 %shard_map.101.tok_ref = f32[4,2,512]{2,1,0:T(2,128)S(1)} custom-call(f32[4,2,512]{2,1,0:T(2,128)S(1)} %copy-done.10, s32[4,1,512]{2,1,0:T(1,128)S(1)} %slice.65.lab_ref, f32[1,512]{1,0:T(1,128)S(1)} %broadcast_in_dim.68.scale_ref), custom_call_target="tpu_custom_call" | custom-call | flops 10000000 | bytes 1000000 | tf_op jit(solution)/shard_map/pallas_call | solution.py:274
  78.1 29.0 %dz_part.1 = (f32[4,256,768]{2,1,0:T(8,128)}, f32[4,256,768]{2,1,0:T(8,128)}, f32[4,1,512]{2,1,0:T(1,128)}, f32[8,6288,512]{2,1,0:T(8,128)}) custom-call(s32[40]{0:T(128)} %concatenate.11.idx_ref, bf16[12576,768]{1,0:T(8,128)(2,1)} %e_hbm.5, f32[8,6288,512]{2,1,0:T(8,128)} %get-tuple-element.43.l_hbm, ...), custom_call_target="tpu_custom_call", output_to_operand_aliasing={{3}: (2, {})} | custom-call | flops 14835253248 | bytes 38633472 | tf_op jit(solution)/shard_map/dz_part/pallas_call | solution.py:453
  109.9 34.8 %logits_far.1 = (f32[8,6288,512]{2,1,0:T(8,128)}, bf16[8,512,768]{2,1,0:T(8,128)(2,1)}, f32[4,2,512]{2,1,0:T(2,128)}) custom-call(s32[40]{0:T(128)} %concatenate.11.idx_ref, bf16[12576,768]{1,0:T(8,128)(2,1)} %e_hbm.5, f32[1,768]{1,0:T(1,128)} %broadcast_in_dim.63.gamma_ref, ...), custom_call_target="tpu_custom_call", output_to_operand_aliasing={{0}: (12, {}), {1}: (13, {})} | custom-call | flops 14835253248 | bytes 38633472 | tf_op jit(solution)/shard_map/logits_far/pallas_call | solution.py:413
  145.4 5.3 %shard_map.102 = f32[4,2,512]{2,1,0:T(2,128)S(1)} custom-call(f32[4,2,512]{2,1,0:T(2,128)S(1)} %copy-done.9, s32[4,1,512]{2,1,0:T(1,128)S(1)} %slice.73.lab_ref, f32[1,512]{1,0:T(1,128)S(1)} %broadcast_in_dim.68.scale_ref), custom_call_target="tpu_custom_call" | custom-call | flops 10000000 | bytes 1000000 | tf_op jit(solution)/shard_map/pallas_call | solution.py:274
  150.8 2.8 copy-done
  153.6 10.7 %shard_map.103 = (f32[1048,768]{1,0:T(8,128)S(1)}, f32[12576,768]{1,0:T(8,128)}) custom-call(s32[40]{0:T(128)S(1)} %copy-done.7, f32[8,6288,512]{2,1,0:T(8,128)} %get-tuple-element.62.l_ref, bf16[8,512,768]{2,1,0:T(8,128)(2,1)S(1)} %copy-done, f32[8,2,512]{2,1,0:T(2,128)S(1)} %pad_maximum_fusion.tok_ref, s32[8,1,512]{2,1,0:T(1,128)S(1)} %reshape.131.lab_ref), custom_call_target="tpu_custom_call" | custom-call | flops 4120903680 | bytes 10731520 | tf_op jit(solution)/shard_map/pallas_call | solution.py:482
  164.4 10.9 %shard_map.104 = (f32[1048,768]{1,0:T(8,128)S(1)}, f32[12576,768]{1,0:T(8,128)}) custom-call(s32[40]{0:T(128)S(1)} %copy-done.7, f32[8,6288,512]{2,1,0:T(8,128)} %get-tuple-element.62.l_ref, bf16[8,512,768]{2,1,0:T(8,128)(2,1)S(1)} %copy-done, f32[8,2,512]{2,1,0:T(2,128)S(1)} %pad_maximum_fusion.tok_ref, ...), custom_call_target="tpu_custom_call", output_to_operand_aliasing={{1}: (5, {})} | custom-call | flops 4120903680 | bytes 10731520 | tf_op jit(solution)/shard_map/pallas_call | solution.py:482
  175.8 11.9 %shard_map.105 = (f32[1048,768]{1,0:T(8,128)S(1)}, f32[12576,768]{1,0:T(8,128)}) custom-call(s32[40]{0:T(128)S(1)} %copy-done.7, f32[8,6288,512]{2,1,0:T(8,128)} %get-tuple-element.62.l_ref, bf16[8,512,768]{2,1,0:T(8,128)(2,1)S(1)} %copy-done, f32[8,2,512]{2,1,0:T(2,128)S(1)} %pad_maximum_fusion.tok_ref, ...), custom_call_target="tpu_custom_call", output_to_operand_aliasing={{1}: (6, {})} | custom-call | flops 4120903680 | bytes 10731520 | tf_op jit(solution)/shard_map/pallas_call | solution.py:482
  187.8 12.6 %shard_map.106 = (f32[1048,768]{1,0:T(8,128)S(1)}, f32[12576,768]{1,0:T(8,128)}) custom-call(s32[40]{0:T(128)S(1)} %copy-done.7, f32[8,6288,512]{2,1,0:T(8,128)} %get-tuple-element.62.l_ref, bf16[8,512,768]{2,1,0:T(8,128)(2,1)S(1)} %copy-done, f32[8,2,512]{2,1,0:T(2,128)S(1)} %pad_maximum_fusion.tok_ref, ...), custom_call_target="tpu_custom_call", output_to_operand_aliasing={{1}: (6, {})} | custom-call | flops 4120903680 | bytes 10731520 | tf_op jit(solution)/shard_map/pallas_call | solution.py:482
  201.3 11.9 %shard_map.107 = (f32[1048,768]{1,0:T(8,128)S(1)}, f32[12576,768]{1,0:T(8,128)}) custom-call(s32[40]{0:T(128)S(1)} %copy-done.7, f32[8,6288,512]{2,1,0:T(8,128)} %get-tuple-element.62.l_ref, bf16[8,512,768]{2,1,0:T(8,128)(2,1)S(1)} %bitcast.75, f32[8,2,512]{2,1,0:T(2,128)S(1)} %pad_maximum_fusion.tok_ref, ...), custom_call_target="tpu_custom_call", output_to_operand_aliasing={{1}: (6, {})} | custom-call | flops 4120903680 | bytes 10731520 | tf_op jit(solution)/shard_map/pallas_call | solution.py:482
  213.2 11.9 %shard_map.108 = (f32[1048,768]{1,0:T(8,128)S(1)}, f32[12576,768]{1,0:T(8,128)}) custom-call(s32[40]{0:T(128)S(1)} %copy-done.7, f32[8,6288,512]{2,1,0:T(8,128)} %get-tuple-element.62.l_ref, bf16[8,512,768]{2,1,0:T(8,128)(2,1)S(1)} %bitcast.75, f32[8,2,512]{2,1,0:T(2,128)S(1)} %pad_maximum_fusion.tok_ref, ...), custom_call_target="tpu_custom_call", output_to_operand_aliasing={{1}: (6, {})} | custom-call | flops 4120903680 | bytes 10731520 | tf_op jit(solution)/shard_map/pallas_call | solution.py:482
  226.8 1.5 collective-permute-start.6
  228.3 17.7 %collective-permute-done.5 = f32[2,128,768]{2,1,0:T(8,128)S(1)} collective-permute-done((f32[2,128,768]{2,1,0:T(8,128)S(1)}, f32[2,128,768]{2,1,0:T(8,128)S(1)}, u32[]{:S(2)}, u32[]{:S(2)}) %collective-permute-start.5) | collective-permute-done | bytes 786464 | tf_op jit(solution)/shard_map/ppermute | solution.py:531
  248.6 8.3 %collective-permute-done.7.a_got_ref = f32[128,768]{1,0:T(8,128)S(1)} collective-permute-done((f32[128,768]{1,0:T(8,128)S(1)}, f32[128,768]{1,0:T(8,128)S(1)}, u32[]{:S(2)}, u32[]{:S(2)}) %collective-permute-start.7) | collective-permute-done | bytes 393248 | tf_op jit(solution)/shard_map/ppermute | solution.py:531
  260.0 12.4 %collective-permute-start.10 = (f32[8,768]{1,0:T(8,128)S(1)}, f32[8,768]{1,0:T(8,128)S(1)}, u32[]{:S(2)}, u32[]{:S(2)}) collective-permute-start(f32[8,768]{1,0:T(8,128)S(1)} %add.96), channel_id=1, source_target_pairs={{0,2},{1,3},{2,0},{3,1},{4,6},{5,7},{6,4},{7,5},{8,10},{9,11},{10,... | collective-permute-start | bytes 73736 | tf_op jit(solution)/shard_map/ppermute | solution.py:531
  272.4 1.8 collective-permute-done.10
  274.8 1.5 collective-permute-start.13
  281.9 8.1 %collective-permute-done.14.refs_2_ = f32[128,768]{1,0:T(8,128)S(1)} collective-permute-done((f32[128,768]{1,0:T(8,128)S(1)}, f32[128,768]{1,0:T(8,128)S(1)}, u32[]{:S(2)}, u32[]{:S(2)}) %collective-permute-start.14) | collective-permute-done | bytes 393248 | tf_op jit(solution)/shard_map/ppermute | solution.py:531
  290.6 5.5 %collective-permute-done.15.refs_3_ = f32[128,768]{1,0:T(8,128)S(1)} collective-permute-done((f32[128,768]{1,0:T(8,128)S(1)}, f32[128,768]{1,0:T(8,128)S(1)}, u32[]{:S(2)}, u32[]{:S(2)}) %collective-permute-start.15) | collective-permute-done | bytes 393248 | tf_op jit(solution)/shard_map/ppermute | solution.py:531
  299.0 7.2 %collective-permute-done.18.refs_6_ = f32[128,768]{1,0:T(8,128)S(1)} collective-permute-done((f32[128,768]{1,0:T(8,128)S(1)}, f32[128,768]{1,0:T(8,128)S(1)}, u32[]{:S(2)}, u32[]{:S(2)}) %collective-permute-start.18) | collective-permute-done | bytes 393248 | tf_op jit(solution)/shard_map/ppermute | solution.py:531
  306.2 1.8 round.1
  308.1 2.2 place.2.de_ref
  310.3 2.2 place.3
  (135 shorter events, 33.3 us)
Async XLA Ops:
  5.5 44.4 %collective-permute-start.3 = (f32[4,256,768]{2,1,0:T(8,128)}, f32[4,256,768]{2,1,0:T(8,128)}, u32[]{:S(2)}, u32[]{:S(2)}) collective-permute-start(f32[4,256,768]{2,1,0:T(8,128)} %get-tuple-element.42.rest_0_), channel_id=1, source_target_pairs={{0,1},{1,0},{2,3},{3,2},{4,5},{5,4},{6,7},{7,6},{8,9},{9,8},{10,11... | collective-permute-start | bytes 9437192 | tf_op jit(solution)/shard_map/ppermute | solution.py:531
  6.9 8.2 %collective-permute-start.1 = (s32[1024]{0:T(1024)S(1)}, s32[1024]{0:T(1024)S(1)}, u32[]{:S(2)}, u32[]{:S(2)}) collective-permute-start(s32[1024]{0:T(1024)S(1)} %bitcast.79), channel_id=1, source_target_pairs={{0,2},{1,3},{2,0},{3,1},{4,6},{5,7},{6,4},{7,5},{8,10},{9,11},{10,... | collective-permute-start | bytes 12296 | tf_op jit(solution)/shard_map/ppermute | solution.py:531
  9.4 5.7 %collective-permute-start.2 = (s32[1024]{0:T(1024)S(1)}, s32[1024]{0:T(1024)S(1)}, u32[]{:S(2)}, u32[]{:S(2)}) collective-permute-start(s32[1024]{0:T(1024)S(1)} %bitcast.80), channel_id=1, source_target_pairs={{0,3},{1,2},{2,1},{3,0},{4,7},{5,6},{6,5},{7,4},{8,11},{9,10},{10,... | collective-permute-start | bytes 12296 | tf_op jit(solution)/shard_map/ppermute | solution.py:531
  9.6 5.4 %collective-permute-start = (s32[1024]{0:T(1024)S(1)}, s32[1024]{0:T(1024)S(1)}, u32[]{:S(2)}, u32[]{:S(2)}) collective-permute-start(s32[1024]{0:T(1024)S(1)} %bitcast.81), channel_id=1, source_target_pairs={{0,1},{1,0},{2,3},{3,2},{4,5},{5,4},{6,7},{7,6},{8,9},{9,8},{10,11... | collective-permute-start | bytes 12296 | tf_op jit(solution)/shard_map/ppermute | solution.py:531
  9.7 20.4 %collective-permute-start.20 = (f32[256,768]{1,0:T(8,128)S(1)}, f32[256,768]{1,0:T(8,128)S(1)}, u32[]{:S(2)}, u32[]{:S(2)}) collective-permute-start(f32[256,768]{1,0:T(8,128)S(1)} %get-tuple-element.51.hat_ref), channel_id=1, source_target_pairs={{0,2},{1,3},{2,0},{3,1},{4,6},{5,7},{6,4},{7,5},{8,10},{9,11},{10,... | collective-permute-start | bytes 2359304 | tf_op jit(solution)/shard_map/ppermute | solution.py:531
  15.0 31.6 %collective-permute-start.23 = (f32[256,768]{1,0:T(8,128)S(1)}, f32[256,768]{1,0:T(8,128)}, u32[]{:S(2)}, u32[]{:S(2)}) collective-permute-start(f32[256,768]{1,0:T(8,128)S(1)} %get-tuple-element.59), channel_id=1, source_target_pairs={{0,2},{1,3},{2,0},{3,1},{4,6},{5,7},{6,4},{7,5},{8,10},{9,11},{10,... | collective-permute-start | bytes 2359304 | tf_op jit(solution)/shard_map/ppermute | solution.py:531
  30.1 18.7 %collective-permute-start.21 = (f32[256,768]{1,0:T(8,128)S(1)}, f32[256,768]{1,0:T(8,128)}, u32[]{:S(2)}, u32[]{:S(2)}) collective-permute-start(f32[256,768]{1,0:T(8,128)S(1)} %collective-permute-done.20.rest_0_), channel_id=1, source_target_pairs={{0,4},{4,0},{8,12},{12,8},{1,5},{5,1},{9,13},{13,9},{2,6},{6,2},{1... | collective-permute-start | bytes 2359304 | tf_op jit(solution)/shard_map/ppermute | solution.py:531
  32.0 17.9 %collective-permute-start.22 = (f32[256,768]{1,0:T(8,128)S(1)}, f32[256,768]{1,0:T(8,128)}, u32[]{:S(2)}, u32[]{:S(2)}) collective-permute-start(f32[256,768]{1,0:T(8,128)S(1)} %collective-permute-done.20.rest_0_), channel_id=1, source_target_pairs={{0,8},{4,12},{8,0},{12,4},{1,9},{5,13},{9,1},{13,5},{2,10},{6,14},... | collective-permute-start | bytes 2359304 | tf_op jit(solution)/shard_map/ppermute | solution.py:531
  35.1 74.7 %collective-permute-start.24 = (f32[256,768]{1,0:T(8,128)S(1)}, f32[256,768]{1,0:T(8,128)}, u32[]{:S(2)}, u32[]{:S(2)}) collective-permute-start(f32[256,768]{1,0:T(8,128)S(1)} %collective-permute-done.20.rest_0_), channel_id=1, source_target_pairs={{0,1},{1,0},{2,3},{3,2},{4,5},{5,4},{6,7},{7,6},{8,9},{9,8},{10,11... | collective-permute-start | bytes 2359304 | tf_op jit(solution)/shard_map/ppermute | solution.py:531
  46.6 63.3 %collective-permute-start.27 = (f32[256,768]{1,0:T(8,128)}, f32[256,768]{1,0:T(8,128)}, u32[]{:S(2)}, u32[]{:S(2)}) collective-permute-start(f32[256,768]{1,0:T(8,128)} %collective-permute-done.23.rest_3_), channel_id=1, source_target_pairs={{0,1},{1,0},{2,3},{3,2},{4,5},{5,4},{6,7},{7,6},{8,9},{9,8},{10,11... | collective-permute-start | bytes 2359304 | tf_op jit(solution)/shard_map/ppermute | solution.py:531
  48.8 61.0 %collective-permute-start.25 = (f32[256,768]{1,0:T(8,128)}, f32[256,768]{1,0:T(8,128)}, u32[]{:S(2)}, u32[]{:S(2)}) collective-permute-start(f32[256,768]{1,0:T(8,128)} %collective-permute-done.21.rest_1_), channel_id=1, source_target_pairs={{0,1},{1,0},{2,3},{3,2},{4,5},{5,4},{6,7},{7,6},{8,9},{9,8},{10,11... | collective-permute-start | bytes 2359304 | tf_op jit(solution)/shard_map/ppermute | solution.py:531
  49.9 60.0 %collective-permute-start.26 = (f32[256,768]{1,0:T(8,128)}, f32[256,768]{1,0:T(8,128)}, u32[]{:S(2)}, u32[]{:S(2)}) collective-permute-start(f32[256,768]{1,0:T(8,128)} %collective-permute-done.22.rest_2_), channel_id=1, source_target_pairs={{0,1},{1,0},{2,3},{3,2},{4,5},{5,4},{6,7},{7,6},{8,9},{9,8},{10,11... | collective-permute-start | bytes 2359304 | tf_op jit(solution)/shard_map/ppermute | solution.py:531
  164.3 11.5 %collective-permute-start.29 = (f32[1048,768]{1,0:T(8,128)S(1)}, f32[1048,768]{1,0:T(8,128)S(1)}, u32[]{:S(2)}, u32[]{:S(2)}) collective-permute-start(f32[1048,768]{1,0:T(8,128)S(1)} %get-tuple-element.67), channel_id=1, source_target_pairs={{0,1},{1,0},{2,3},{3,2},{4,5},{5,4},{6,7},{7,6},{8,9},{9,8},{10,11... | collective-permute-start | bytes 9658376 | tf_op jit(solution)/shard_map/ppermute | solution.py:531
  175.3 12.5 %collective-permute-start.28 = (f32[1048,768]{1,0:T(8,128)S(1)}, f32[1048,768]{1,0:T(8,128)S(1)}, u32[]{:S(2)}, u32[]{:S(2)}) collective-permute-start(f32[1048,768]{1,0:T(8,128)S(1)} %get-tuple-element.66), channel_id=1, source_target_pairs={{0,1},{1,0},{2,3},{3,2},{4,5},{5,4},{6,7},{7,6},{8,9},{9,8},{10,11... | collective-permute-start | bytes 9658376 | tf_op jit(solution)/shard_map/ppermute | solution.py:531
  187.6 13.6 %collective-permute-start.31 = (f32[1048,768]{1,0:T(8,128)S(1)}, f32[1048,768]{1,0:T(8,128)S(1)}, u32[]{:S(2)}, u32[]{:S(2)}) collective-permute-start(f32[1048,768]{1,0:T(8,128)S(1)} %get-tuple-element.71), channel_id=1, source_target_pairs={{0,1},{1,0},{2,3},{3,2},{4,5},{5,4},{6,7},{7,6},{8,9},{9,8},{10,11... | collective-permute-start | bytes 9658376 | tf_op jit(solution)/shard_map/ppermute | solution.py:531
  200.3 12.8 %collective-permute-start.30 = (f32[1048,768]{1,0:T(8,128)S(1)}, f32[1048,768]{1,0:T(8,128)S(1)}, u32[]{:S(2)}, u32[]{:S(2)}) collective-permute-start(f32[1048,768]{1,0:T(8,128)S(1)} %get-tuple-element.70), channel_id=1, source_target_pairs={{0,1},{1,0},{2,3},{3,2},{4,5},{5,4},{6,7},{7,6},{8,9},{9,8},{10,11... | collective-permute-start | bytes 9658376 | tf_op jit(solution)/shard_map/ppermute | solution.py:531
  200.8 24.8 %collective-permute-start.4 = (f32[4,256,768]{2,1,0:T(8,128)S(1)}, f32[4,256,768]{2,1,0:T(8,128)S(1)}, u32[]{:S(2)}, u32[]{:S(2)}) collective-permute-start(f32[4,256,768]{2,1,0:T(8,128)S(1)} %copy-done.15), channel_id=1, source_target_pairs={{0,1},{1,0},{2,3},{3,2},{4,5},{5,4},{6,7},{7,6},{8,9},{9,8},{10,11... | collective-permute-start | bytes 9437192 | tf_op jit(solution)/shard_map/ppermute | solution.py:531
  225.0 85.3 %collective-permute-start.32 = (f32[1048,768]{1,0:T(8,128)S(1)}, f32[1048,768]{1,0:T(8,128)S(1)}, u32[]{:S(2)}, u32[]{:S(2)}) collective-permute-start(f32[1048,768]{1,0:T(8,128)S(1)} %get-tuple-element.74), channel_id=1, source_target_pairs={{0,1},{1,0},{2,3},{3,2},{4,5},{5,4},{6,7},{7,6},{8,9},{9,8},{10,11... | collective-permute-start | bytes 9658376 | tf_op jit(solution)/shard_map/ppermute | solution.py:531
  225.5 82.5 %collective-permute-start.33 = (f32[1048,768]{1,0:T(8,128)S(1)}, f32[1048,768]{1,0:T(8,128)S(1)}, u32[]{:S(2)}, u32[]{:S(2)}) collective-permute-start(f32[1048,768]{1,0:T(8,128)S(1)} %get-tuple-element.75), channel_id=1, source_target_pairs={{0,1},{1,0},{2,3},{3,2},{4,5},{5,4},{6,7},{7,6},{8,9},{9,8},{10,11... | collective-permute-start | bytes 9658376 | tf_op jit(solution)/shard_map/ppermute | solution.py:531
  226.0 19.9 %collective-permute-start.5 = (f32[2,128,768]{2,1,0:T(8,128)S(1)}, f32[2,128,768]{2,1,0:T(8,128)S(1)}, u32[]{:S(2)}, u32[]{:S(2)}) collective-permute-start(f32[2,128,768]{2,1,0:T(8,128)S(1)} %fusion.3), channel_id=1, source_target_pairs={{0,4},{4,0},{8,12},{12,8},{1,5},{5,1},{9,13},{13,9},{2,6},{6,2},{1... | collective-permute-start | bytes 2359304 | tf_op jit(solution)/shard_map/ppermute | solution.py:531
  226.8 20.9 %collective-permute-start.6 = (f32[2,128,768]{2,1,0:T(8,128)S(1)}, f32[2,128,768]{2,1,0:T(8,128)S(1)}, u32[]{:S(2)}, u32[]{:S(2)}) collective-permute-start(f32[2,128,768]{2,1,0:T(8,128)S(1)} %fusion), channel_id=1, source_target_pairs={{0,8},{4,12},{8,0},{12,4},{1,9},{5,13},{9,1},{13,5},{2,10},{6,14},... | collective-permute-start | bytes 2359304 | tf_op jit(solution)/shard_map/ppermute | solution.py:531
  246.2 10.7 %collective-permute-start.7 = (f32[128,768]{1,0:T(8,128)S(1)}, f32[128,768]{1,0:T(8,128)S(1)}, u32[]{:S(2)}, u32[]{:S(2)}) collective-permute-start(f32[128,768]{1,0:T(8,128)S(1)} %get-tuple-element.87), channel_id=1, source_target_pairs={{0,8},{4,12},{8,0},{12,4},{1,9},{5,13},{9,1},{13,5},{2,10},{6,14},... | collective-permute-start | bytes 1179656 | tf_op jit(solution)/shard_map/ppermute | solution.py:531
  247.9 10.4 %collective-permute-start.8 = (f32[128,768]{1,0:T(8,128)S(1)}, f32[128,768]{1,0:T(8,128)S(1)}, u32[]{:S(2)}, u32[]{:S(2)}) collective-permute-start(f32[128,768]{1,0:T(8,128)S(1)} %get-tuple-element.85), channel_id=1, source_target_pairs={{0,4},{4,0},{8,12},{12,8},{1,5},{5,1},{9,13},{13,9},{2,6},{6,2},{1... | collective-permute-start | bytes 1179656 | tf_op jit(solution)/shard_map/ppermute | solution.py:531
  260.0 14.2 %collective-permute-start.10 = (f32[8,768]{1,0:T(8,128)S(1)}, f32[8,768]{1,0:T(8,128)S(1)}, u32[]{:S(2)}, u32[]{:S(2)}) collective-permute-start(f32[8,768]{1,0:T(8,128)S(1)} %add.96), channel_id=1, source_target_pairs={{0,2},{1,3},{2,0},{3,1},{4,6},{5,7},{6,4},{7,5},{8,10},{9,11},{10,... | collective-permute-start | bytes 73736 | tf_op jit(solution)/shard_map/ppermute | solution.py:531
  274.8 5.0 %collective-permute-start.13 = (f32[8,768]{1,0:T(8,128)S(1)}, f32[8,768]{1,0:T(8,128)S(1)}, u32[]{:S(2)}, u32[]{:S(2)}) collective-permute-start(f32[8,768]{1,0:T(8,128)S(1)} %add.97), channel_id=1, source_target_pairs={{0,12},{4,8},{8,4},{12,0},{1,13},{5,9},{9,5},{13,1},{2,14},{6,10},... | collective-permute-start | bytes 73736 | tf_op jit(solution)/shard_map/ppermute | solution.py:531
  276.4 4.4 %collective-permute-start.11 = (f32[8,768]{1,0:T(8,128)S(1)}, f32[8,768]{1,0:T(8,128)S(1)}, u32[]{:S(2)}, u32[]{:S(2)}) collective-permute-start(f32[8,768]{1,0:T(8,128)S(1)} %add.97), channel_id=1, source_target_pairs={{0,4},{4,0},{8,12},{12,8},{1,5},{5,1},{9,13},{13,9},{2,6},{6,2},{1... | collective-permute-start | bytes 73736 | tf_op jit(solution)/shard_map/ppermute | solution.py:531
  278.0 12.0 %collective-permute-start.14 = (f32[128,768]{1,0:T(8,128)S(1)}, f32[128,768]{1,0:T(8,128)S(1)}, u32[]{:S(2)}, u32[]{:S(2)}) collective-permute-start(f32[128,768]{1,0:T(8,128)S(1)} %get-tuple-element.56.refs_0_), channel_id=1, source_target_pairs={{0,4},{4,0},{8,12},{12,8},{1,5},{5,1},{9,13},{13,9},{2,6},{6,2},{1... | collective-permute-start | bytes 1179656 | tf_op jit(solution)/shard_map/ppermute | solution.py:531
  279.8 16.4 %collective-permute-start.15 = (f32[128,768]{1,0:T(8,128)S(1)}, f32[128,768]{1,0:T(8,128)S(1)}, u32[]{:S(2)}, u32[]{:S(2)}) collective-permute-start(f32[128,768]{1,0:T(8,128)S(1)} %get-tuple-element.57.refs_1_), channel_id=1, source_target_pairs={{0,4},{4,0},{8,12},{12,8},{1,5},{5,1},{9,13},{13,9},{2,6},{6,2},{1... | collective-permute-start | bytes 1179656 | tf_op jit(solution)/shard_map/ppermute | solution.py:531
  280.8 16.0 %collective-permute-start.17 = (f32[128,768]{1,0:T(8,128)S(1)}, f32[128,768]{1,0:T(8,128)S(1)}, u32[]{:S(2)}, u32[]{:S(2)}) collective-permute-start(f32[128,768]{1,0:T(8,128)S(1)} %get-tuple-element.57.refs_1_), channel_id=1, source_target_pairs={{0,8},{4,12},{8,0},{12,4},{1,9},{5,13},{9,1},{13,5},{2,10},{6,14},... | collective-permute-start | bytes 1179656 | tf_op jit(solution)/shard_map/ppermute | solution.py:531
  290.0 9.0 %collective-permute-start.16 = (f32[128,768]{1,0:T(8,128)S(1)}, f32[128,768]{1,0:T(8,128)S(1)}, u32[]{:S(2)}, u32[]{:S(2)}) collective-permute-start(f32[128,768]{1,0:T(8,128)S(1)} %get-tuple-element.56.refs_0_), channel_id=1, source_target_pairs={{0,8},{4,12},{8,0},{12,4},{1,9},{5,13},{9,1},{13,5},{2,10},{6,14},... | collective-permute-start | bytes 1179656 | tf_op jit(solution)/shard_map/ppermute | solution.py:531
  296.2 10.1 %collective-permute-start.18 = (f32[128,768]{1,0:T(8,128)S(1)}, f32[128,768]{1,0:T(8,128)S(1)}, u32[]{:S(2)}, u32[]{:S(2)}) collective-permute-start(f32[128,768]{1,0:T(8,128)S(1)} %collective-permute-done.14.refs_2_), channel_id=1, source_target_pairs={{0,8},{4,12},{8,0},{12,4},{1,9},{5,13},{9,1},{13,5},{2,10},{6,14},... | collective-permute-start | bytes 1179656 | tf_op jit(solution)/shard_map/ppermute | solution.py:531
  296.8 9.5 %collective-permute-start.19 = (f32[128,768]{1,0:T(8,128)S(1)}, f32[128,768]{1,0:T(8,128)S(1)}, u32[]{:S(2)}, u32[]{:S(2)}) collective-permute-start(f32[128,768]{1,0:T(8,128)S(1)} %collective-permute-done.17.refs_5_), channel_id=1, source_target_pairs={{0,4},{4,0},{8,12},{12,8},{1,5},{5,1},{9,13},{13,9},{2,6},{6,2},{1... | collective-permute-start | bytes 1179656 | tf_op jit(solution)/shard_map/ppermute | solution.py:531
  (20 other events, 331.2 us)

commit v4 on v3

--- a/solution.py
+++ b/solution.py
@@ -13,8 +13,9 @@
 PAIR = 2 * BLOCK
 BIG = 1e30
 VMEM_LIMIT = 62 * 1024 * 1024
-DE_VMEM = 16 * 1024 * 1024
+DE_VMEM = 20 * 1024 * 1024
 EARLY_OUT = True
+DZ_CHUNK = 1024
 
 
 CORE, NEAR_PAIRS, FAR_PAIRS, ALL_PAIRS, ROW_START = 0, 1, 2, 3, 4
@@ -118,30 +119,35 @@
 def dz_kernel(idx_ref, e_hbm, l_hbm, tok_ref, lab_ref, own_ref, mate_ref, tl_ref, l_out_ref, acc_ref, out_ref, et_ref, e_ref, l_ref, sem, e_sem, l_sem):
     i = pl.program_id(0)
     rows = e_ref.shape[0]
+    slot = i % 2
+    live = i < idx_ref[NEAR_PAIRS]
     size = 512
     full = rows // size
-    slot = i % 2
 
     def fetch(pair):
         start(split_copy(l_hbm.at[pair], l_ref.at[pair % 2], l_sem.at[pair % 2], size))
 
+    def table(k, n):
+        at = pl.multiple_of(k * size, size)
+        return pltpu.make_async_copy(e_hbm.at[pl.ds(pl.multiple_of(idx_ref[CORE] * rows + at, 16), n), :], e_ref.at[pl.ds(at, n), :], e_sem.at[k])
+
     @pl.when(i == 0)
     def _():
-        table = e_hbm.at[pl.ds(pl.multiple_of(idx_ref[CORE] * rows, 16), rows), :]
-        start(split_copy(table, e_ref, e_sem, size))
+        for k, (_, n) in enumerate(chunk_list(rows, size)):
+            table(k, n).start()
         fetch(0)
-        pltpu.make_async_copy(table, e_ref, e_sem).wait()
 
         def turn(k, carry):
+            table(k, size).wait()
             at = pl.multiple_of(k * size, size)
             et_ref[:, pl.ds(at, size)] = e_ref[pl.ds(at, size), :].T
             return carry
 
         lax.fori_loop(0, full, turn, 0)
         if rows > full * size:
+            table(full, rows - full * size).wait()
             et_ref[:, full * size:] = e_ref[full * size:, :].T
 
-    live = i < idx_ref[NEAR_PAIRS]
     pl.when(i + 1 < idx_ref[NEAR_PAIRS])(lambda: fetch(i + 1))
 
     @pl.when(live)
@@ -172,7 +178,7 @@
     weight = tok_ref[0, 1:2, :]
     label = lab_ref[0] - idx_ref[ROW_START]
     target = jnp.zeros((1, PAIR), jnp.float32)
-    for start, n in chunk_list(et_ref.shape[1], 1024):
+    for start, n in chunk_list(et_ref.shape[1], DZ_CHUNK):
         tile = l_ref[start:start + n, :]
         is_target = lax.broadcasted_iota(jnp.int32, (n, PAIR), 0) == label - start
         grad = grad_tile(tile, lse, weight, is_target)
@@ -348,6 +354,29 @@
     )(*args)
 
 
+def part_kernel(pick_ref, own_ref, got_ref, a_send, b_send, a_keep, b_keep):
+    piece = a_send.shape[1]
+    y, not_y, z, not_z = (pick_ref[6 + k] for k in range(4))
+    for k in range(2):
+        for out, block, at in ((a_send, 2 * k + not_y, 0), (a_keep, 2 * k + y, 0), (b_send, 2 * not_z + k, piece), (b_keep, 2 * z + k, piece)):
+            out[k] = own_ref[block, at:at + piece, :] + got_ref[block, at:at + piece, :]
+
+
+def call_part(picks, own, got):
+    whole = pl.BlockSpec(own.shape, lambda i, s: (0, 0, 0), pipeline_mode=pl.Buffered(1))
+    shape = (2, own.shape[1] // 2, own.shape[2])
+    return pl.pallas_call(
+        part_kernel,
+        grid_spec=pltpu.PrefetchScalarGridSpec(
+            num_scalar_prefetch=1, grid=(1,), in_specs=[whole, whole], out_specs=[pl.BlockSpec(shape, lambda i, s: (0, 0, 0), pipeline_mode=pl.Buffered(1))] * 4,
+        ),
+        out_shape=[jax.ShapeDtypeStruct(shape, jnp.float32)] * 4,
+        compiler_params=params(DE_VMEM),
+        cost_estimate=pl.CostEstimate(flops=1_000_000, bytes_accessed=9_000_000, transcendentals=0),
+        name="part",
+    )(picks, own, got)
+
+
 def round_kernel(pick_ref, *refs):
     out_ref = refs[-1]
     piece = refs[0].shape[0]
@@ -445,7 +474,7 @@
             pltpu.VMEM((rows, width), jnp.bfloat16),
             pltpu.VMEM((2, rows, PAIR), jnp.float32),
             pltpu.SemaphoreType.DMA((2,)),
-            pltpu.SemaphoreType.DMA,
+            pltpu.SemaphoreType.DMA((pl.cdiv(rows, 512),)),
             pltpu.SemaphoreType.DMA((2,)),
         ],
     )
@@ -539,7 +568,7 @@
         y, z = (tp & 1).astype(jnp.uint32), (tp >> 1).astype(jnp.uint32)
         not_y, not_z = 1 - y, 1 - z
         seq, width = hidden.shape[1:]
-        quarters, piece = seq // BLOCK, BLOCK // 2
+        quarters = seq // BLOCK
         rows = embed_shard.shape[0] // 2
         row_start = tp * (2 * rows) + core * rows
 
@@ -550,7 +579,7 @@
         far_marks = [flip(marked, 'dp', 2), flip(marked, 'dp', 3)]
         mate_marks = flip(marked, 'dp', 1)
 
-        picks = jnp.stack([tp, tp ^ 3] + [tp ^ p for p in range(4)])
+        picks = jnp.stack([tp, tp ^ 3] + [tp ^ p for p in range(4)] + [tp & 1, 1 - (tp & 1), tp >> 1, 1 - (tp >> 1)])
         x_hat, inv_std, own_quarter, far_quarter = call_norm(picks, hidden.reshape(quarters, BLOCK, width))
         mate = flip(x_hat, 'dp', 1)
         far0, far3 = flip(own_quarter, 'dp', 2), flip(far_quarter, 'dp', 2)
@@ -583,17 +612,9 @@
         far_tok = call_lse(far_stats, lab[4:], scale, 1)
         dz_got = flip(dz_mate, 'dp', 1)
 
-        def part(column, half_z, half_y):
-            def cut(x):
-                x = x.reshape(2, 2, 2, piece, width)[:, :, column]
-                return pick(x, half_z) if half_y is None else lax.dynamic_index_in_dim(x, half_y, 1, keepdims=False)
-
-            return cut(dz_own) + cut(dz_got)
-
-        a_got = flip(part(0, None, not_y), 'tp', 1)
-        b_got = flip(part(1, not_z, None), 'tp', 2)
-        a_keep = part(0, None, y) + a_got
-        b_keep = part(1, z, None) + b_got
+        a_send, b_send, a_keep, b_keep = call_part(picks, dz_own, dz_got)
+        a_got, b_got = flip(a_send, 'tp', 1), flip(b_send, 'tp', 2)
+        a_keep, b_keep = a_keep + a_got, b_keep + b_got
         a_grad = flip(pick(a_keep, not_z), 'tp', 2)
         b_grad = flip(pick(b_keep, not_y), 'tp', 1)
         tok = jnp.concatenate([near_tok, far_tok])
@@ -604,19 +625,17 @@
         b1, b3 = flip(b0, 'tp', 1), flip(b2, 'tp', 1)
         d_hidden = call_round(picks, [a0, b0, a1, b1, a2, b2, a3, b3])
 
-        for bits in (1, 2):
-            got_sums = flip(sums, 'dp', bits)
-            sums = sums + got_sums
-        got_sums = [flip(sums, 'tp', k) for k in (1, 2, 3)]
-        sums = sums + got_sums[0] + (got_sums[1] + got_sums[2])
-
-        chunks = [(k * (rows // 6), rows // 6) for k in range(6)]
+        for axis in ('dp', 'tp'):
+            got_sums = [flip(sums, axis, k) for k in (1, 2, 3)]
+            sums = sums + got_sums[0] + (got_sums[1] + got_sums[2])
+
+        chunks = [(0, rows // 3), (rows // 3, rows // 3), (4 * (rows // 6), rows // 6), (5 * (rows // 6), rows // 6)]
         d_embed, got = None, []
         for n, (offset, size) in enumerate(chunks):
             arrived = got[n - 2] if n >= 2 else None
             d_chunk, d_embed = call_de(idx, logits, z_pairs, tok, lab, d_embed, offset, size, arrived, chunks[n - 2][0] if n >= 2 else None)
             got.append(flip(d_chunk, 'dp', 1))
-        for n in (4, 5):
+        for n in (2, 3):
             d_embed = call_place(idx, got[n], d_embed, chunks[n][0])
 
         return sums[2, 0], d_hidden, d_embed, sums[0], sums[1]

time: 313 us -> 303 us (0.968)
  Pallas kernels: 176 us -> 166 us
    pallas_call x6 -> x4, Pallas kernels: 69.8 us -> 62.3 us  [call_de(): pl.pallas_call(functools.partial(de_kernel, offset, rows, got_offset if g...]
    ppermute x34 -> x33, starting transfers between devices: 36.2 us -> 35.8 us  [flip(): return lax.ppermute(x, axis, [(k, k ^ bits) for k in range(n)])]
    ppermute x34 -> x33, waiting for transfers between devices: 78.5 us -> 78.8 us  [flip(): return lax.ppermute(x, axis, [(k, k ^ bits) for k in range(n)])]
    unnamed x36 -> x30, local copies, waits for them, and re-layouts: 7.14 us -> 7.11 us
  transfers between devices with their start and end apart: 34 -> 33, of which waited for: 15 -> 15; matrix products, arithmetic and copies ran while one was open for 3% -> 3% of each run, Pallas kernels for 38% -> 34%
where the time goes in v4:
time: 303 us; the launch traced here: 302 us
  Pallas kernels  166 us (55%)
  waiting for transfers between devices  78.8 us (26%)
  starting transfers between devices  35.8 us (12%)
  local copies, waits for them, and re-layouts  12.3 us (4%)
  between operations  4.51 us (1%)
  other arithmetic  4.35 us (1%)
    ppermute x33, waiting for transfers between devices, flip(): return lax.ppermute(x, axis, [(k, k ^ bits) for k in range(n)])  78.8 us
    pallas_call x4, Pallas kernels, call_de(): pl.pallas_call(functools.partial(de_kernel, offset, rows, got_offset if g...  62.3 us
    pallas_call x2, Pallas kernels, call_logits(): pl.pallas_call(functools.partial(logits_kernel, count, base, order, len(p...  56.1 us
    ppermute x33, starting transfers between devices, flip(): return lax.ppermute(x, axis, [(k, k ^ bits) for k in range(n)])  35.8 us
    pallas_call x1, Pallas kernels, call_dz(): pl.pallas_call(dz_kernel, grid_spec=spec, out_shape=[half, half, jax.Shap...  26 us
    pallas_call x2, Pallas kernels, call_lse(): pl.pallas_call(lse_kernel, in_specs=[vmem, vmem, vmem], out_specs=vmem, o...  10.9 us
    unnamed x30, local copies, waits for them, and re-layouts  7.11 us
  transfers between devices with their start and end apart: 33, of which 15 were waited for; matrix products, arithmetic and copies ran while one was open for 3% of the time, Pallas kernels for 34%

profile of v4, /device:TPU:0, one launch (start us, length us, event | category | flops | bytes accessed | tf_op | source)
XLA Modules:
  0.0 302.0 jit_solution(4544905630398337534)
XLA Ops:
  2.2 3.4 %norm.1 = (f32[4,256,768]{2,1,0:T(8,128)}, f32[256,128]{1,0:T(8,128)S(1)}, f32[256,768]{1,0:T(8,128)S(1)}, f32[256,768]{1,0:T(8,128)S(1)}) custom-call(s32[10]{0:T(128)S(1)} %stack.58.pick_ref, bf16[4,256,768]{2,1,0:T(8,128)(2,1)S(1)} %bitcast.34), custom_call_target="tpu_custom_call" | custom-call | flops 10000000 | bytes 8000000 | tf_op jit(solution)/shard_map/norm/pallas_call | solution.py:314
  7.0 2.5 collective-permute-start.1
  9.7 1.9 collective-permute-start.21
  19.0 11.1 %collective-permute-done.21.rest_0_ = f32[256,768]{1,0:T(8,128)S(1)} collective-permute-done((f32[256,768]{1,0:T(8,128)S(1)}, f32[256,768]{1,0:T(8,128)S(1)}, u32[]{:S(2)}, u32[]{:S(2)}) %collective-permute-start.21) | collective-permute-done | bytes 786464 | tf_op jit(solution)/shard_map/ppermute | solution.py:560
  30.1 1.9 collective-permute-start.22
  32.0 1.6 collective-permute-start.23
  35.2 11.4 %collective-permute-done.24.rest_3_ = f32[256,768]{1,0:T(8,128)} collective-permute-done((f32[256,768]{1,0:T(8,128)S(1)}, f32[256,768]{1,0:T(8,128)}, u32[]{:S(2)}, u32[]{:S(2)}) %collective-permute-start.24) | collective-permute-done | bytes 786464 | tf_op jit(solution)/shard_map/ppermute | solution.py:560
  46.6 2.2 collective-permute-done.22.rest_1_
  49.9 21.3 %logits_near.1 = (f32[8,6288,512]{2,1,0:T(8,128)}, bf16[8,512,768]{2,1,0:T(8,128)(2,1)}, f32[4,2,512]{2,1,0:T(2,128)}) custom-call(s32[40]{0:T(128)} %concatenate.11.idx_ref, bf16[12576,768]{1,0:T(8,128)(2,1)} %e_hbm.5, f32[1,768]{1,0:T(1,128)} %broadcast_in_dim.63.gamma_ref, f32[1,768]{1,0:T(1,128)} %broadcast_in_dim.64.beta_ref, ...), custom_call_target="tpu_custom_call" | custom-call | flops 14835253248 | bytes 38633472 | tf_op jit(solution)/shard_map/logits_near/pallas_call | solution.py:442
  71.9 5.6 %shard_map.101.tok_ref = f32[4,2,512]{2,1,0:T(2,128)S(1)} custom-call(f32[4,2,512]{2,1,0:T(2,128)S(1)} %copy-done.11, s32[4,1,512]{2,1,0:T(1,128)S(1)} %slice.49.lab_ref, f32[1,512]{1,0:T(1,128)S(1)} %broadcast_in_dim.68.scale_ref), custom_call_target="tpu_custom_call" | custom-call | flops 10000000 | bytes 1000000 | tf_op jit(solution)/shard_map/pallas_call | solution.py:280
  78.1 26.0 %dz_part.1 = (f32[4,256,768]{2,1,0:T(8,128)}, f32[4,256,768]{2,1,0:T(8,128)}, f32[4,1,512]{2,1,0:T(1,128)}, f32[8,6288,512]{2,1,0:T(8,128)}) custom-call(s32[40]{0:T(128)} %concatenate.11.idx_ref, bf16[12576,768]{1,0:T(8,128)(2,1)} %e_hbm.5, f32[8,6288,512]{2,1,0:T(8,128)} %get-tuple-element.43.l_hbm, ...), custom_call_target="tpu_custom_call", output_to_operand_aliasing={{3}: (2, {})} | custom-call | flops 14835253248 | bytes 38633472 | tf_op jit(solution)/shard_map/dz_part/pallas_call | solution.py:482
  107.0 34.8 %logits_far.1 = (f32[8,6288,512]{2,1,0:T(8,128)}, bf16[8,512,768]{2,1,0:T(8,128)(2,1)}, f32[4,2,512]{2,1,0:T(2,128)}) custom-call(s32[40]{0:T(128)} %concatenate.11.idx_ref, bf16[12576,768]{1,0:T(8,128)(2,1)} %e_hbm.5, f32[1,768]{1,0:T(1,128)} %broadcast_in_dim.63.gamma_ref, ...), custom_call_target="tpu_custom_call", output_to_operand_aliasing={{0}: (12, {}), {1}: (13, {})} | custom-call | flops 14835253248 | bytes 38633472 | tf_op jit(solution)/shard_map/logits_far/pallas_call | solution.py:442
  142.5 5.3 %shard_map.102 = f32[4,2,512]{2,1,0:T(2,128)S(1)} custom-call(f32[4,2,512]{2,1,0:T(2,128)S(1)} %copy-done.10, s32[4,1,512]{2,1,0:T(1,128)S(1)} %slice.53.lab_ref, f32[1,512]{1,0:T(1,128)S(1)} %broadcast_in_dim.68.scale_ref), custom_call_target="tpu_custom_call" | custom-call | flops 10000000 | bytes 1000000 | tf_op jit(solution)/shard_map/pallas_call | solution.py:280
  147.9 2.8 copy-done
  150.7 18.0 %shard_map.103 = (f32[2096,768]{1,0:T(8,128)S(1)}, f32[12576,768]{1,0:T(8,128)}) custom-call(s32[40]{0:T(128)S(1)} %copy-done.8, f32[8,6288,512]{2,1,0:T(8,128)} %get-tuple-element.66.l_ref, bf16[8,512,768]{2,1,0:T(8,128)(2,1)S(1)} %copy-done, f32[8,2,512]{2,1,0:T(2,128)S(1)} %pad_maximum_fusion.tok_ref, s32[8,1,512]{2,1,0:T(1,128)S(1)} %reshape.97.lab_ref), custom_call_target="tpu_custom_call" | custom-call | flops 8241807360 | bytes 21463040 | tf_op jit(solution)/shard_map/pallas_call | solution.py:511
  168.8 18.4 %shard_map.104 = (f32[2096,768]{1,0:T(8,128)S(1)}, f32[12576,768]{1,0:T(8,128)}) custom-call(s32[40]{0:T(128)S(1)} %copy-done.8, f32[8,6288,512]{2,1,0:T(8,128)} %get-tuple-element.66.l_ref, bf16[8,512,768]{2,1,0:T(8,128)(2,1)S(1)} %copy-done, f32[8,2,512]{2,1,0:T(2,128)S(1)} %pad_maximum_fusion.tok_ref, ...), custom_call_target="tpu_custom_call", output_to_operand_aliasing={{1}: (5, {})} | custom-call | flops 8241807360 | bytes 21463040 | tf_op jit(solution)/shard_map/pallas_call | solution.py:511
  187.7 12.6 %shard_map.105 = (f32[1048,768]{1,0:T(8,128)S(1)}, f32[12576,768]{1,0:T(8,128)}) custom-call(s32[40]{0:T(128)S(1)} %copy-done.8, f32[8,6288,512]{2,1,0:T(8,128)} %get-tuple-element.66.l_ref, bf16[8,512,768]{2,1,0:T(8,128)(2,1)S(1)} %copy-done, f32[8,2,512]{2,1,0:T(2,128)S(1)} %pad_maximum_fusion.tok_ref, ...), custom_call_target="tpu_custom_call", output_to_operand_aliasing={{1}: (6, {})} | custom-call | flops 4120903680 | bytes 10731520 | tf_op jit(solution)/shard_map/pallas_call | solution.py:511
  200.8 13.3 %shard_map.106 = (f32[1048,768]{1,0:T(8,128)S(1)}, f32[12576,768]{1,0:T(8,128)}) custom-call(s32[40]{0:T(128)S(1)} %copy-done.8, f32[8,6288,512]{2,1,0:T(8,128)} %get-tuple-element.66.l_ref, bf16[8,512,768]{2,1,0:T(8,128)(2,1)S(1)} %copy-done, f32[8,2,512]{2,1,0:T(2,128)S(1)} %pad_maximum_fusion.tok_ref, ...), custom_call_target="tpu_custom_call", output_to_operand_aliasing={{1}: (6, {})} | custom-call | flops 4120903680 | bytes 10731520 | tf_op jit(solution)/shard_map/pallas_call | solution.py:511
  215.8 1.5 collective-permute-start.6
  217.3 17.8 %collective-permute-done.5 = f32[2,128,768]{2,1,0:T(8,128)S(1)} collective-permute-done((f32[2,128,768]{2,1,0:T(8,128)S(1)}, f32[2,128,768]{2,1,0:T(8,128)S(1)}, u32[]{:S(2)}, u32[]{:S(2)}) %collective-permute-start.5) | collective-permute-done | bytes 786464 | tf_op jit(solution)/shard_map/ppermute | solution.py:560
  235.2 1.5 collective-permute-start.7
  237.5 8.3 %collective-permute-done.7.a_got_ref = f32[128,768]{1,0:T(8,128)S(1)} collective-permute-done((f32[128,768]{1,0:T(8,128)S(1)}, f32[128,768]{1,0:T(8,128)S(1)}, u32[]{:S(2)}, u32[]{:S(2)}) %collective-permute-start.7) | collective-permute-done | bytes 393248 | tf_op jit(solution)/shard_map/ppermute | solution.py:560
  247.7 12.6 %collective-permute-start.10 = (f32[8,768]{1,0:T(8,128)S(1)}, f32[8,768]{1,0:T(8,128)S(1)}, u32[]{:S(2)}, u32[]{:S(2)}) collective-permute-start(f32[8,768]{1,0:T(8,128)S(1)} %get-tuple-element.59), channel_id=1, source_target_pairs={{0,2},{1,3},{2,0},{3,1},{4,6},{5,7},{6,4},{7,5},{8,10},{9,11},{10,... | collective-permute-start | bytes 73736 | tf_op jit(solution)/shard_map/ppermute | solution.py:560
  260.4 1.6 collective-permute-done.10
  264.1 1.6 collective-permute-start.14
  271.2 8.1 %collective-permute-done.15.refs_2_ = f32[128,768]{1,0:T(8,128)S(1)} collective-permute-done((f32[128,768]{1,0:T(8,128)S(1)}, f32[128,768]{1,0:T(8,128)S(1)}, u32[]{:S(2)}, u32[]{:S(2)}) %collective-permute-start.15) | collective-permute-done | bytes 393248 | tf_op jit(solution)/shard_map/ppermute | solution.py:560
  279.9 4.9 %collective-permute-done.16.refs_3_ = f32[128,768]{1,0:T(8,128)S(1)} collective-permute-done((f32[128,768]{1,0:T(8,128)S(1)}, f32[128,768]{1,0:T(8,128)S(1)}, u32[]{:S(2)}, u32[]{:S(2)}) %collective-permute-start.16) | collective-permute-done | bytes 393248 | tf_op jit(solution)/shard_map/ppermute | solution.py:560
  287.5 2.1 collective-permute-done.17.refs_4_
  289.6 5.9 %collective-permute-done.19.refs_6_ = f32[128,768]{1,0:T(8,128)S(1)} collective-permute-done((f32[128,768]{1,0:T(8,128)S(1)}, f32[128,768]{1,0:T(8,128)S(1)}, u32[]{:S(2)}, u32[]{:S(2)}) %collective-permute-start.19) | collective-permute-done | bytes 393248 | tf_op jit(solution)/shard_map/ppermute | solution.py:560
  295.5 1.8 round.1
  297.4 2.2 place.2.de_ref
  299.6 2.2 place.3
  (120 shorter events, 31.3 us)
Async XLA Ops:
  5.5 44.4 %collective-permute-start.3 = (f32[4,256,768]{2,1,0:T(8,128)}, f32[4,256,768]{2,1,0:T(8,128)}, u32[]{:S(2)}, u32[]{:S(2)}) collective-permute-start(f32[4,256,768]{2,1,0:T(8,128)} %get-tuple-element.42.rest_0_), channel_id=1, source_target_pairs={{0,1},{1,0},{2,3},{3,2},{4,5},{5,4},{6,7},{7,6},{8,9},{9,8},{10,11... | collective-permute-start | bytes 9437192 | tf_op jit(solution)/shard_map/ppermute | solution.py:560
  7.0 8.2 %collective-permute-start.1 = (s32[1024]{0:T(1024)S(1)}, s32[1024]{0:T(1024)S(1)}, u32[]{:S(2)}, u32[]{:S(2)}) collective-permute-start(s32[1024]{0:T(1024)S(1)} %bitcast.35), channel_id=1, source_target_pairs={{0,2},{1,3},{2,0},{3,1},{4,6},{5,7},{6,4},{7,5},{8,10},{9,11},{10,... | collective-permute-start | bytes 12296 | tf_op jit(solution)/shard_map/ppermute | solution.py:560
  9.5 5.7 %collective-permute-start.2 = (s32[1024]{0:T(1024)S(1)}, s32[1024]{0:T(1024)S(1)}, u32[]{:S(2)}, u32[]{:S(2)}) collective-permute-start(s32[1024]{0:T(1024)S(1)} %bitcast.36), channel_id=1, source_target_pairs={{0,3},{1,2},{2,1},{3,0},{4,7},{5,6},{6,5},{7,4},{8,11},{9,10},{10,... | collective-permute-start | bytes 12296 | tf_op jit(solution)/shard_map/ppermute | solution.py:560
  9.6 5.4 %collective-permute-start = (s32[1024]{0:T(1024)S(1)}, s32[1024]{0:T(1024)S(1)}, u32[]{:S(2)}, u32[]{:S(2)}) collective-permute-start(s32[1024]{0:T(1024)S(1)} %bitcast.37), channel_id=1, source_target_pairs={{0,1},{1,0},{2,3},{3,2},{4,5},{5,4},{6,7},{7,6},{8,9},{9,8},{10,11... | collective-permute-start | bytes 12296 | tf_op jit(solution)/shard_map/ppermute | solution.py:560
  9.7 20.4 %collective-permute-start.21 = (f32[256,768]{1,0:T(8,128)S(1)}, f32[256,768]{1,0:T(8,128)S(1)}, u32[]{:S(2)}, u32[]{:S(2)}) collective-permute-start(f32[256,768]{1,0:T(8,128)S(1)} %get-tuple-element.55.hat_ref), channel_id=1, source_target_pairs={{0,2},{1,3},{2,0},{3,1},{4,6},{5,7},{6,4},{7,5},{8,10},{9,11},{10,... | collective-permute-start | bytes 2359304 | tf_op jit(solution)/shard_map/ppermute | solution.py:560
  15.0 31.6 %collective-permute-start.24 = (f32[256,768]{1,0:T(8,128)S(1)}, f32[256,768]{1,0:T(8,128)}, u32[]{:S(2)}, u32[]{:S(2)}) collective-permute-start(f32[256,768]{1,0:T(8,128)S(1)} %get-tuple-element.63), channel_id=1, source_target_pairs={{0,2},{1,3},{2,0},{3,1},{4,6},{5,7},{6,4},{7,5},{8,10},{9,11},{10,... | collective-permute-start | bytes 2359304 | tf_op jit(solution)/shard_map/ppermute | solution.py:560
  30.1 18.7 %collective-permute-start.22 = (f32[256,768]{1,0:T(8,128)S(1)}, f32[256,768]{1,0:T(8,128)}, u32[]{:S(2)}, u32[]{:S(2)}) collective-permute-start(f32[256,768]{1,0:T(8,128)S(1)} %collective-permute-done.21.rest_0_), channel_id=1, source_target_pairs={{0,4},{4,0},{8,12},{12,8},{1,5},{5,1},{9,13},{13,9},{2,6},{6,2},{1... | collective-permute-start | bytes 2359304 | tf_op jit(solution)/shard_map/ppermute | solution.py:560
  32.0 17.9 %collective-permute-start.23 = (f32[256,768]{1,0:T(8,128)S(1)}, f32[256,768]{1,0:T(8,128)}, u32[]{:S(2)}, u32[]{:S(2)}) collective-permute-start(f32[256,768]{1,0:T(8,128)S(1)} %collective-permute-done.21.rest_0_), channel_id=1, source_target_pairs={{0,8},{4,12},{8,0},{12,4},{1,9},{5,13},{9,1},{13,5},{2,10},{6,14},... | collective-permute-start | bytes 2359304 | tf_op jit(solution)/shard_map/ppermute | solution.py:560
  35.2 71.7 %collective-permute-start.25 = (f32[256,768]{1,0:T(8,128)S(1)}, f32[256,768]{1,0:T(8,128)}, u32[]{:S(2)}, u32[]{:S(2)}) collective-permute-start(f32[256,768]{1,0:T(8,128)S(1)} %collective-permute-done.21.rest_0_), channel_id=1, source_target_pairs={{0,1},{1,0},{2,3},{3,2},{4,5},{5,4},{6,7},{7,6},{8,9},{9,8},{10,11... | collective-permute-start | bytes 2359304 | tf_op jit(solution)/shard_map/ppermute | solution.py:560
  46.6 60.3 %collective-permute-start.28 = (f32[256,768]{1,0:T(8,128)}, f32[256,768]{1,0:T(8,128)}, u32[]{:S(2)}, u32[]{:S(2)}) collective-permute-start(f32[256,768]{1,0:T(8,128)} %collective-permute-done.24.rest_3_), channel_id=1, source_target_pairs={{0,1},{1,0},{2,3},{3,2},{4,5},{5,4},{6,7},{7,6},{8,9},{9,8},{10,11... | collective-permute-start | bytes 2359304 | tf_op jit(solution)/shard_map/ppermute | solution.py:560
  48.8 58.1 %collective-permute-start.26 = (f32[256,768]{1,0:T(8,128)}, f32[256,768]{1,0:T(8,128)}, u32[]{:S(2)}, u32[]{:S(2)}) collective-permute-start(f32[256,768]{1,0:T(8,128)} %collective-permute-done.22.rest_1_), channel_id=1, source_target_pairs={{0,1},{1,0},{2,3},{3,2},{4,5},{5,4},{6,7},{7,6},{8,9},{9,8},{10,11... | collective-permute-start | bytes 2359304 | tf_op jit(solution)/shard_map/ppermute | solution.py:560
  49.9 57.0 %collective-permute-start.27 = (f32[256,768]{1,0:T(8,128)}, f32[256,768]{1,0:T(8,128)}, u32[]{:S(2)}, u32[]{:S(2)}) collective-permute-start(f32[256,768]{1,0:T(8,128)} %collective-permute-done.23.rest_2_), channel_id=1, source_target_pairs={{0,1},{1,0},{2,3},{3,2},{4,5},{5,4},{6,7},{7,6},{8,9},{9,8},{10,11... | collective-permute-start | bytes 2359304 | tf_op jit(solution)/shard_map/ppermute | solution.py:560
  168.7 19.1 %collective-permute-start.30 = (f32[2096,768]{1,0:T(8,128)S(1)}, f32[2096,768]{1,0:T(8,128)S(1)}, u32[]{:S(2)}, u32[]{:S(2)}) collective-permute-start(f32[2096,768]{1,0:T(8,128)S(1)} %get-tuple-element.71), channel_id=1, source_target_pairs={{0,1},{1,0},{2,3},{3,2},{4,5},{5,4},{6,7},{7,6},{8,9},{9,8},{10,11... | collective-permute-start | bytes 19316744 | tf_op jit(solution)/shard_map/ppermute | solution.py:560
  187.2 13.6 %collective-permute-start.29 = (f32[2096,768]{1,0:T(8,128)S(1)}, f32[2096,768]{1,0:T(8,128)S(1)}, u32[]{:S(2)}, u32[]{:S(2)}) collective-permute-start(f32[2096,768]{1,0:T(8,128)S(1)} %get-tuple-element.70), channel_id=1, source_target_pairs={{0,1},{1,0},{2,3},{3,2},{4,5},{5,4},{6,7},{7,6},{8,9},{9,8},{10,11... | collective-permute-start | bytes 19316744 | tf_op jit(solution)/shard_map/ppermute | solution.py:560
  187.6 26.6 %collective-permute-start.4 = (f32[4,256,768]{2,1,0:T(8,128)}, f32[4,256,768]{2,1,0:T(8,128)S(1)}, u32[]{:S(2)}, u32[]{:S(2)}) collective-permute-start(f32[4,256,768]{2,1,0:T(8,128)} %get-tuple-element.46), channel_id=1, source_target_pairs={{0,1},{1,0},{2,3},{3,2},{4,5},{5,4},{6,7},{7,6},{8,9},{9,8},{10,11... | collective-permute-start | bytes 9437192 | tf_op jit(solution)/shard_map/ppermute | solution.py:560
  200.3 97.0 %collective-permute-start.32 = (f32[1048,768]{1,0:T(8,128)S(1)}, f32[1048,768]{1,0:T(8,128)S(1)}, u32[]{:S(2)}, u32[]{:S(2)}) collective-permute-start(f32[1048,768]{1,0:T(8,128)S(1)} %get-tuple-element.75), channel_id=1, source_target_pairs={{0,1},{1,0},{2,3},{3,2},{4,5},{5,4},{6,7},{7,6},{8,9},{9,8},{10,11... | collective-permute-start | bytes 9658376 | tf_op jit(solution)/shard_map/ppermute | solution.py:560
  214.1 85.5 %collective-permute-start.31 = (f32[1048,768]{1,0:T(8,128)S(1)}, f32[1048,768]{1,0:T(8,128)S(1)}, u32[]{:S(2)}, u32[]{:S(2)}) collective-permute-start(f32[1048,768]{1,0:T(8,128)S(1)} %get-tuple-element.74), channel_id=1, source_target_pairs={{0,1},{1,0},{2,3},{3,2},{4,5},{5,4},{6,7},{7,6},{8,9},{9,8},{10,11... | collective-permute-start | bytes 9658376 | tf_op jit(solution)/shard_map/ppermute | solution.py:560
  215.1 19.9 %collective-permute-start.5 = (f32[2,128,768]{2,1,0:T(8,128)S(1)}, f32[2,128,768]{2,1,0:T(8,128)S(1)}, u32[]{:S(2)}, u32[]{:S(2)}) collective-permute-start(f32[2,128,768]{2,1,0:T(8,128)S(1)} %get-tuple-element.48), channel_id=1, source_target_pairs={{0,4},{4,0},{8,12},{12,8},{1,5},{5,1},{9,13},{13,9},{2,6},{6,2},{1... | collective-permute-start | bytes 2359304 | tf_op jit(solution)/shard_map/ppermute | solution.py:560
  215.8 20.9 %collective-permute-start.6 = (f32[2,128,768]{2,1,0:T(8,128)S(1)}, f32[2,128,768]{2,1,0:T(8,128)S(1)}, u32[]{:S(2)}, u32[]{:S(2)}) collective-permute-start(f32[2,128,768]{2,1,0:T(8,128)S(1)} %get-tuple-element.51), channel_id=1, source_target_pairs={{0,8},{4,12},{8,0},{12,4},{1,9},{5,13},{9,1},{13,5},{2,10},{6,14},... | collective-permute-start | bytes 2359304 | tf_op jit(solution)/shard_map/ppermute | solution.py:560
  235.2 10.6 %collective-permute-start.7 = (f32[128,768]{1,0:T(8,128)S(1)}, f32[128,768]{1,0:T(8,128)S(1)}, u32[]{:S(2)}, u32[]{:S(2)}) collective-permute-start(f32[128,768]{1,0:T(8,128)S(1)} %get-tuple-element.83), channel_id=1, source_target_pairs={{0,8},{4,12},{8,0},{12,4},{1,9},{5,13},{9,1},{13,5},{2,10},{6,14},... | collective-permute-start | bytes 1179656 | tf_op jit(solution)/shard_map/ppermute | solution.py:560
  236.9 10.3 %collective-permute-start.8 = (f32[128,768]{1,0:T(8,128)S(1)}, f32[128,768]{1,0:T(8,128)S(1)}, u32[]{:S(2)}, u32[]{:S(2)}) collective-permute-start(f32[128,768]{1,0:T(8,128)S(1)} %get-tuple-element.81), channel_id=1, source_target_pairs={{0,4},{4,0},{8,12},{12,8},{1,5},{5,1},{9,13},{13,9},{2,6},{6,2},{1... | collective-permute-start | bytes 1179656 | tf_op jit(solution)/shard_map/ppermute | solution.py:560
  247.7 14.4 %collective-permute-start.10 = (f32[8,768]{1,0:T(8,128)S(1)}, f32[8,768]{1,0:T(8,128)S(1)}, u32[]{:S(2)}, u32[]{:S(2)}) collective-permute-start(f32[8,768]{1,0:T(8,128)S(1)} %get-tuple-element.59), channel_id=1, source_target_pairs={{0,2},{1,3},{2,0},{3,1},{4,6},{5,7},{6,4},{7,5},{8,10},{9,11},{10,... | collective-permute-start | bytes 73736 | tf_op jit(solution)/shard_map/ppermute | solution.py:560
  260.2 3.3 %collective-permute-start.11 = (f32[8,768]{1,0:T(8,128)S(1)}, f32[8,768]{1,0:T(8,128)S(1)}, u32[]{:S(2)}, u32[]{:S(2)}) collective-permute-start(f32[8,768]{1,0:T(8,128)S(1)} %get-tuple-element.59), channel_id=1, source_target_pairs={{0,3},{1,2},{2,1},{3,0},{4,7},{5,6},{6,5},{7,4},{8,11},{9,10},{10,... | collective-permute-start | bytes 73736 | tf_op jit(solution)/shard_map/ppermute | solution.py:560
  263.5 3.9 %collective-permute-start.13 = (f32[8,768]{1,0:T(8,128)S(1)}, f32[8,768]{1,0:T(8,128)S(1)}, u32[]{:S(2)}, u32[]{:S(2)}) collective-permute-start(f32[8,768]{1,0:T(8,128)S(1)} %add_add_fusion.1), channel_id=1, source_target_pairs={{0,8},{4,12},{8,0},{12,4},{1,9},{5,13},{9,1},{13,5},{2,10},{6,14},... | collective-permute-start | bytes 73736 | tf_op jit(solution)/shard_map/ppermute | solution.py:560
  264.1 5.0 %collective-permute-start.14 = (f32[8,768]{1,0:T(8,128)S(1)}, f32[8,768]{1,0:T(8,128)S(1)}, u32[]{:S(2)}, u32[]{:S(2)}) collective-permute-start(f32[8,768]{1,0:T(8,128)S(1)} %add_add_fusion.1), channel_id=1, source_target_pairs={{0,12},{4,8},{8,4},{12,0},{1,13},{5,9},{9,5},{13,1},{2,14},{6,10},... | collective-permute-start | bytes 73736 | tf_op jit(solution)/shard_map/ppermute | solution.py:560
  265.7 4.4 %collective-permute-start.12 = (f32[8,768]{1,0:T(8,128)S(1)}, f32[8,768]{1,0:T(8,128)S(1)}, u32[]{:S(2)}, u32[]{:S(2)}) collective-permute-start(f32[8,768]{1,0:T(8,128)S(1)} %add_add_fusion.1), channel_id=1, source_target_pairs={{0,4},{4,0},{8,12},{12,8},{1,5},{5,1},{9,13},{13,9},{2,6},{6,2},{1... | collective-permute-start | bytes 73736 | tf_op jit(solution)/shard_map/ppermute | solution.py:560
  267.3 12.0 %collective-permute-start.15 = (f32[128,768]{1,0:T(8,128)S(1)}, f32[128,768]{1,0:T(8,128)S(1)}, u32[]{:S(2)}, u32[]{:S(2)}) collective-permute-start(f32[128,768]{1,0:T(8,128)S(1)} %get-tuple-element.60.refs_0_), channel_id=1, source_target_pairs={{0,4},{4,0},{8,12},{12,8},{1,5},{5,1},{9,13},{13,9},{2,6},{6,2},{1... | collective-permute-start | bytes 1179656 | tf_op jit(solution)/shard_map/ppermute | solution.py:560
  269.1 15.8 %collective-permute-start.16 = (f32[128,768]{1,0:T(8,128)S(1)}, f32[128,768]{1,0:T(8,128)S(1)}, u32[]{:S(2)}, u32[]{:S(2)}) collective-permute-start(f32[128,768]{1,0:T(8,128)S(1)} %get-tuple-element.61.refs_1_), channel_id=1, source_target_pairs={{0,4},{4,0},{8,12},{12,8},{1,5},{5,1},{9,13},{13,9},{2,6},{6,2},{1... | collective-permute-start | bytes 1179656 | tf_op jit(solution)/shard_map/ppermute | solution.py:560
  270.1 15.4 %collective-permute-start.18 = (f32[128,768]{1,0:T(8,128)S(1)}, f32[128,768]{1,0:T(8,128)S(1)}, u32[]{:S(2)}, u32[]{:S(2)}) collective-permute-start(f32[128,768]{1,0:T(8,128)S(1)} %get-tuple-element.61.refs_1_), channel_id=1, source_target_pairs={{0,8},{4,12},{8,0},{12,4},{1,9},{5,13},{9,1},{13,5},{2,10},{6,14},... | collective-permute-start | bytes 1179656 | tf_op jit(solution)/shard_map/ppermute | solution.py:560
  279.3 10.3 %collective-permute-start.17 = (f32[128,768]{1,0:T(8,128)S(1)}, f32[128,768]{1,0:T(8,128)S(1)}, u32[]{:S(2)}, u32[]{:S(2)}) collective-permute-start(f32[128,768]{1,0:T(8,128)S(1)} %get-tuple-element.60.refs_0_), channel_id=1, source_target_pairs={{0,8},{4,12},{8,0},{12,4},{1,9},{5,13},{9,1},{13,5},{2,10},{6,14},... | collective-permute-start | bytes 1179656 | tf_op jit(solution)/shard_map/ppermute | solution.py:560
  284.8 10.7 %collective-permute-start.19 = (f32[128,768]{1,0:T(8,128)S(1)}, f32[128,768]{1,0:T(8,128)S(1)}, u32[]{:S(2)}, u32[]{:S(2)}) collective-permute-start(f32[128,768]{1,0:T(8,128)S(1)} %collective-permute-done.15.refs_2_), channel_id=1, source_target_pairs={{0,8},{4,12},{8,0},{12,4},{1,9},{5,13},{9,1},{13,5},{2,10},{6,14},... | collective-permute-start | bytes 1179656 | tf_op jit(solution)/shard_map/ppermute | solution.py:560
  285.4 10.1 %collective-permute-start.20 = (f32[128,768]{1,0:T(8,128)S(1)}, f32[128,768]{1,0:T(8,128)S(1)}, u32[]{:S(2)}, u32[]{:S(2)}) collective-permute-start(f32[128,768]{1,0:T(8,128)S(1)} %collective-permute-done.18.refs_5_), channel_id=1, source_target_pairs={{0,4},{4,0},{8,12},{12,8},{1,5},{5,1},{9,13},{13,9},{2,6},{6,2},{1... | collective-permute-start | bytes 1179656 | tf_op jit(solution)/shard_map/ppermute | solution.py:560
  (16 other events, 281.6 us)

commit v5 on v4

--- a/solution.py
+++ b/solution.py
@@ -13,9 +13,10 @@
 PAIR = 2 * BLOCK
 BIG = 1e30
 VMEM_LIMIT = 62 * 1024 * 1024
-DE_VMEM = 20 * 1024 * 1024
+DE_VMEM = 16 * 1024 * 1024
 EARLY_OUT = True
 DZ_CHUNK = 1024
+LOGITS_CHUNK = 272
 
 
 CORE, NEAR_PAIRS, FAR_PAIRS, ALL_PAIRS, ROW_START = 0, 1, 2, 3, 4
@@ -75,8 +76,8 @@
     def _():
         for h in range(2):
             copies(0, slot, h)[0][1].wait()
-        zc_ref[0] = (x_ref[slot] * gamma_ref[...] + beta_ref[...]).astype(jnp.bfloat16)
-        logits_step(e_ref, l_ref.at[slot], zc_ref, st_ref, split_copy(l_ref.at[slot], l_hbm.at[base + i], l_sem.at[slot], 528))
+        zc_ref[0] = (x_ref[slot] * gamma_ref[...][None, :] + beta_ref[...][None, :]).astype(jnp.bfloat16)
+        logits_step(e_ref, l_ref.at[slot], zc_ref, st_ref, split_copy(l_ref.at[slot], l_hbm.at[base + i], l_sem.at[slot], LOGITS_CHUNK))
 
     @pl.when(i == idx_ref[count] - 1)
     def _():
@@ -86,7 +87,7 @@
 
 def logits_step(e_ref, l_ref, zc_ref, st_ref, out):
     rows = e_ref.shape[0]
-    size = 528
+    size = LOGITS_CHUNK
     top = jnp.full((1, PAIR), -BIG, jnp.float32)
     total = jnp.zeros((1, PAIR), jnp.float32)
 
@@ -155,6 +156,12 @@
         pltpu.make_async_copy(l_hbm.at[0], l_ref.at[slot], l_sem.at[slot]).wait()
         dz_step(idx_ref, et_ref, l_ref.at[slot], tok_ref, lab_ref, tl_ref, acc_ref)
 
+    def sent():
+        for h in range(2):
+            pltpu.make_async_copy(out_ref.at[pl.ds(h * BLOCK, BLOCK), :], own_ref.at[0], sem.at[h]).wait()
+
+    pl.when(i > 0)(sent)
+
     @pl.when(live)
     def _():
         out_ref[...] = acc_ref[...].T
@@ -169,8 +176,7 @@
             target = own_ref if seq == 0 else mate_ref
             copy = pltpu.make_async_copy(out_ref.at[pl.ds(h * BLOCK, BLOCK), :], target.at[block % 4], sem.at[h])
             pl.when(block // 4 == (idx_ref[CORE] + seq) % 2)(copy.start)
-    for h in range(2):
-        pltpu.make_async_copy(out_ref.at[pl.ds(h * BLOCK, BLOCK), :], own_ref.at[0], sem.at[h]).wait()
+    pl.when(i == pl.num_programs(0) - 1)(sent)
 
 
 def dz_step(idx_ref, et_ref, l_ref, tok_ref, lab_ref, tl_ref, acc_ref):
@@ -201,14 +207,23 @@
     def rows_at(side, start, n):
         return out_ref.at[pl.ds(pl.multiple_of(side * half + start, 8), n), :]
 
+    block = buf_ref.shape[1]
+    steps = rows // block * count
+
     def source(i):
-        return l_ref.at[idx_ref[PAIR_IDS + i], pl.ds(offset, rows), :]
+        at = pl.multiple_of(offset + i // count * block, 8)
+        return l_ref.at[idx_ref[PAIR_IDS + i % count], pl.ds(at, block), :]
+
+    def write(k):
+        at = pl.multiple_of(k * block, 8)
+        half_start = pl.multiple_of(core * half + offset + at, 8)
+        return part_ref.at[pl.ds(at, block), :], out_ref.at[pl.ds(half_start, block), :]
 
     def fetch(i):
         start(split_copy(source(i), buf_ref.at[i % 3], sem.at[i % 3], 264))
 
     fetch(0)
-    pl.when(count > 1)(lambda: fetch(1))
+    pl.when(steps > 1)(lambda: fetch(1))
     got = None
     if got_ref is not None:
         target = rows_at(1 - core, got_offset, got_ref.shape[0])
@@ -218,21 +233,22 @@
 
     def step(i, carry):
         pltpu.make_async_copy(source(i), buf_ref.at[i % 3], sem.at[i % 3]).wait()
-        pl.when(i + 2 < count)(lambda: fetch(i + 2))
-        pair = idx_ref[PAIR_IDS + i]
+        pl.when(i + 2 < steps)(lambda: fetch(i + 2))
+        k = i // count
+        pair = idx_ref[PAIR_IDS + i % count]
         lse = tok_ref[pair, 0:1, :]
         weight = tok_ref[pair, 1:2, :]
-        label = lab_ref[pair] - idx_ref[ROW_START] - offset
-        for at, n in chunk_list(rows, 528):
+        label = lab_ref[pair] - idx_ref[ROW_START] - offset - k * block
+        for at, n in chunk_list(block, 528):
             is_target = lax.broadcasted_iota(jnp.int32, (n, PAIR), 0) == label - at
             grad = grad_tile(buf_ref[i % 3, at:at + n, :], lse, weight, is_target)
-            part_ref[at:at + n, :] += jnp.dot(grad, z_ref[pair], preferred_element_type=jnp.float32)
+            part_ref[pl.ds(pl.multiple_of(k * block + at, 8), n), :] += jnp.dot(grad, z_ref[pair], preferred_element_type=jnp.float32)
+        pl.when(i % count == count - 1)(lambda: start(split_copy(*write(k), sem.at[4], 264)))
         return carry
 
-    lax.fori_loop(0, count, step, 0)
-    target = rows_at(core, offset, rows)
-    start(split_copy(part_ref, target, sem.at[4], 264))
-    pltpu.make_async_copy(part_ref, target, sem.at[4]).wait()
+    lax.fori_loop(0, steps, step, 0)
+    for k in range(rows // block):
+        pltpu.make_async_copy(*write(k), sem.at[4]).wait()
     if got is not None:
         got.wait()
 
@@ -328,7 +344,7 @@
     piece = a_ref.shape[0]
     grad = jnp.concatenate([a_ref[...] + a_got_ref[...], b_ref[...] + b_got_ref[...]])
     hat = hat_ref[...]
-    scaled = grad * gamma_ref[...]
+    scaled = grad * gamma_ref[...][None, :]
     inner = scaled - jnp.mean(scaled, axis=-1, keepdims=True) - hat * jnp.mean(scaled * hat, axis=-1, keepdims=True)
     inner = inner * inv_ref[:, 0:1]
     a_out[...] = inner[:piece]
@@ -423,7 +439,7 @@
         num_scalar_prefetch=1,
         grid=(4,),
         in_specs=[ANY]
-        + [pl.BlockSpec((1, width), lambda i, s: (0, 0))] * 2 + [ANY] * (len(pieces) + len(extra)),
+        + [pl.BlockSpec((width,), lambda i, s: (0,))] * 2 + [ANY] * (len(pieces) + len(extra)),
         out_specs=[
             ANY,
             pl.BlockSpec((1, PAIR, width), lambda i, s: (base + last(i, s[count]), 0, 0)),
@@ -451,7 +467,7 @@
         compiler_params=params(),
         cost_estimate=cost(3, rows, width),
         name="logits_near" if previous is None else "logits_far",
-    )(idx, e, gamma[None], beta[None], *pieces, *extra)
+    )(idx, e, gamma, beta, *pieces, *extra)
 
 
 def call_dz(idx, e, l, tok, lab):
@@ -506,7 +522,7 @@
         grid=(1,),
         in_specs=[ANY, whole(zc), whole(tok), whole(lab)] + extra_specs,
         out_specs=[pl.BlockSpec((rows, width), lambda i, s: (0, 0), pipeline_mode=pl.Buffered(1)), ANY],
-        scratch_shapes=[pltpu.VMEM((3, rows, PAIR), jnp.float32), pltpu.SemaphoreType.DMA((5,))],
+        scratch_shapes=[pltpu.VMEM((3, total // 6, PAIR), jnp.float32), pltpu.SemaphoreType.DMA((5,))],
     )
     return pl.pallas_call(
         functools.partial(de_kernel, offset, rows, got_offset if got is not None else None),
@@ -619,7 +635,7 @@
         b_grad = flip(pick(b_keep, not_y), 'tp', 1)
         tok = jnp.concatenate([near_tok, far_tok])
 
-        a0, b0, sums = call_norm_bwd(pick(a_keep, z), pick(b_keep, y), a_grad, b_grad, own_quarter, inv_std, ln_gamma[None], loss)
+        a0, b0, sums = call_norm_bwd(pick(a_keep, z), pick(b_keep, y), a_grad, b_grad, own_quarter, inv_std, ln_gamma, loss)
         a1, b2 = flip(a0, 'tp', 1), flip(b0, 'tp', 2)
         a2, a3 = flip(a0, 'tp', 2), flip(a1, 'tp', 2)
         b1, b3 = flip(b0, 'tp', 1), flip(b2, 'tp', 1)

time: 303 us -> 293 us (0.967)
  Pallas kernels: 166 us -> 159 us
    pallas_call x2, Pallas kernels: 56.1 us -> 48.8 us  [call_logits(): pl.pallas_call(functools.partial(logits_kernel, count, base, order, len(p...]
    unnamed x30 -> x32, local copies, waits for them, and re-layouts: 7.11 us -> 7.12 us
  transfers between devices with their start and end apart: 33 -> 33, of which waited for: 15 -> 15; matrix products, arithmetic and copies ran while one was open for 3% -> 2% of each run, Pallas kernels for 34% -> 34%
where the time goes in v5:
time: 293 us
  Pallas kernels  159 us (54%)
  waiting for transfers between devices  79.2 us (27%)
  starting transfers between devices  36.3 us (12%)
  local copies, waits for them, and re-layouts  9.74 us (3%)
  between operations  4.56 us (2%)
  other arithmetic  4.35 us (1%)
    ppermute x33, waiting for transfers between devices, flip(): return lax.ppermute(x, axis, [(k, k ^ bits) for k in range(n)])  79.2 us
    pallas_call x4, Pallas kernels, call_de(): pl.pallas_call(functools.partial(de_kernel, offset, rows, got_offset if g...  62.6 us
    pallas_call x2, Pallas kernels, call_logits(): pl.pallas_call(functools.partial(logits_kernel, count, base, order, len(p...  48.8 us
    ppermute x33, starting transfers between devices, flip(): return lax.ppermute(x, axis, [(k, k ^ bits) for k in range(n)])  36.3 us
    pallas_call x1, Pallas kernels, call_dz(): pl.pallas_call(dz_kernel, grid_spec=spec, out_shape=[half, half, jax.Shap...  25.4 us
    pallas_call x2, Pallas kernels, call_lse(): pl.pallas_call(lse_kernel, in_specs=[vmem, vmem, vmem], out_specs=vmem, o...  10.9 us
    unnamed x32, local copies, waits for them, and re-layouts  7.12 us
  transfers between devices with their start and end apart: 33, of which 15 were waited for; matrix products, arithmetic and copies ran while one was open for 2% of the time, Pallas kernels for 34%

profile of v5, /device:TPU:0, one launch (start us, length us, event | category | flops | bytes accessed | tf_op | source)
XLA Modules:
  0.0 292.8 jit_solution(8242838499180440924)
XLA Ops:
  2.2 3.4 %norm.1 = (f32[4,256,768]{2,1,0:T(8,128)}, f32[256,128]{1,0:T(8,128)S(1)}, f32[256,768]{1,0:T(8,128)S(1)}, f32[256,768]{1,0:T(8,128)S(1)}) custom-call(s32[10]{0:T(128)S(1)} %stack.58.pick_ref, bf16[4,256,768]{2,1,0:T(8,128)(2,1)S(1)} %bitcast.34), custom_call_target="tpu_custom_call" | custom-call | flops 10000000 | bytes 8000000 | tf_op jit(solution)/shard_map/norm/pallas_call | solution.py:330
  7.0 2.5 collective-permute-start.1
  9.7 1.9 collective-permute-start.21
  12.5 2.2 collective-permute-start.24
  18.6 11.5 %collective-permute-done.21.rest_0_ = f32[256,768]{1,0:T(8,128)S(1)} collective-permute-done((f32[256,768]{1,0:T(8,128)S(1)}, f32[256,768]{1,0:T(8,128)S(1)}, u32[]{:S(2)}, u32[]{:S(2)}) %collective-permute-start.21) | collective-permute-done | bytes 786464 | tf_op jit(solution)/shard_map/ppermute | solution.py:576
  30.1 1.9 collective-permute-start.22
  32.0 1.6 collective-permute-start.23
  35.2 11.4 %collective-permute-done.24.rest_3_ = f32[256,768]{1,0:T(8,128)} collective-permute-done((f32[256,768]{1,0:T(8,128)S(1)}, f32[256,768]{1,0:T(8,128)}, u32[]{:S(2)}, u32[]{:S(2)}) %collective-permute-start.24) | collective-permute-done | bytes 786464 | tf_op jit(solution)/shard_map/ppermute | solution.py:576
  46.6 2.2 collective-permute-done.22.rest_1_
  49.9 18.7 %logits_near.1 = (f32[8,6288,512]{2,1,0:T(8,128)}, bf16[8,512,768]{2,1,0:T(8,128)(2,1)}, f32[4,2,512]{2,1,0:T(2,128)}) custom-call(s32[40]{0:T(128)} %concatenate.11.idx_ref, bf16[12576,768]{1,0:T(8,128)(2,1)} %e_hbm.5, f32[768]{0:T(1024)} %gamma_ref.5, f32[768]{0:T(1024)} %beta_ref.3, f32[4,256,768]{2,1,0:T(8,128)} %get-tuple-element.42.rest_0_, ...), custom_call_target="tpu_custom_call" | custom-call | flops 14835253248 | bytes 38633472 | tf_op jit(solution)/shard_map/logits_near/pallas_call | solution.py:458
  69.3 5.6 %shard_map.101.tok_ref = f32[4,2,512]{2,1,0:T(2,128)S(1)} custom-call(f32[4,2,512]{2,1,0:T(2,128)S(1)} %copy-done.11, s32[4,1,512]{2,1,0:T(1,128)S(1)} %slice.49.lab_ref, f32[1,512]{1,0:T(1,128)S(1)} %broadcast_in_dim.57.scale_ref), custom_call_target="tpu_custom_call" | custom-call | flops 10000000 | bytes 1000000 | tf_op jit(solution)/shard_map/pallas_call | solution.py:296
  75.5 25.4 %dz_part.1 = (f32[4,256,768]{2,1,0:T(8,128)}, f32[4,256,768]{2,1,0:T(8,128)}, f32[4,1,512]{2,1,0:T(1,128)}, f32[8,6288,512]{2,1,0:T(8,128)}) custom-call(s32[40]{0:T(128)} %concatenate.11.idx_ref, bf16[12576,768]{1,0:T(8,128)(2,1)} %e_hbm.5, f32[8,6288,512]{2,1,0:T(8,128)} %get-tuple-element.43.l_hbm, ...), custom_call_target="tpu_custom_call", output_to_operand_aliasing={{3}: (2, {})} | custom-call | flops 14835253248 | bytes 38633472 | tf_op jit(solution)/shard_map/dz_part/pallas_call | solution.py:498
  103.7 30.1 %logits_far.1 = (f32[8,6288,512]{2,1,0:T(8,128)}, bf16[8,512,768]{2,1,0:T(8,128)(2,1)}, f32[4,2,512]{2,1,0:T(2,128)}) custom-call(s32[40]{0:T(128)} %concatenate.11.idx_ref, bf16[12576,768]{1,0:T(8,128)(2,1)} %e_hbm.5, f32[768]{0:T(1024)} %gamma_ref.5, f32[768]{0:T(1024)} %beta_ref.3, ...), custom_call_target="tpu_custom_call", output_to_operand_aliasing={{0}: (12, {}), {1}: (13, {})} | custom-call | flops 14835253248 | bytes 38633472 | tf_op jit(solution)/shard_map/logits_far/pallas_call | solution.py:458
  134.5 5.3 %shard_map.102 = f32[4,2,512]{2,1,0:T(2,128)S(1)} custom-call(f32[4,2,512]{2,1,0:T(2,128)S(1)} %copy-done.10, s32[4,1,512]{2,1,0:T(1,128)S(1)} %slice.53.lab_ref, f32[1,512]{1,0:T(1,128)S(1)} %broadcast_in_dim.57.scale_ref), custom_call_target="tpu_custom_call" | custom-call | flops 10000000 | bytes 1000000 | tf_op jit(solution)/shard_map/pallas_call | solution.py:296
  139.8 2.8 copy-done
  142.6 18.6 %shard_map.103 = (f32[2096,768]{1,0:T(8,128)S(1)}, f32[12576,768]{1,0:T(8,128)}) custom-call(s32[40]{0:T(128)S(1)} %copy-done.8, f32[8,6288,512]{2,1,0:T(8,128)} %get-tuple-element.66.l_ref, bf16[8,512,768]{2,1,0:T(8,128)(2,1)S(1)} %copy-done, f32[8,2,512]{2,1,0:T(2,128)S(1)} %pad_maximum_fusion.tok_ref, s32[8,1,512]{2,1,0:T(1,128)S(1)} %reshape.97.lab_ref), custom_call_target="tpu_custom_call" | custom-call | flops 8241807360 | bytes 21463040 | tf_op jit(solution)/shard_map/pallas_call | solution.py:527
  161.4 18.6 %shard_map.104 = (f32[2096,768]{1,0:T(8,128)S(1)}, f32[12576,768]{1,0:T(8,128)}) custom-call(s32[40]{0:T(128)S(1)} %copy-done.8, f32[8,6288,512]{2,1,0:T(8,128)} %get-tuple-element.66.l_ref, bf16[8,512,768]{2,1,0:T(8,128)(2,1)S(1)} %copy-done, f32[8,2,512]{2,1,0:T(2,128)S(1)} %pad_maximum_fusion.tok_ref, ...), custom_call_target="tpu_custom_call", output_to_operand_aliasing={{1}: (5, {})} | custom-call | flops 8241807360 | bytes 21463040 | tf_op jit(solution)/shard_map/pallas_call | solution.py:527
  180.5 12.6 %shard_map.105 = (f32[1048,768]{1,0:T(8,128)S(1)}, f32[12576,768]{1,0:T(8,128)}) custom-call(s32[40]{0:T(128)S(1)} %copy-done.8, f32[8,6288,512]{2,1,0:T(8,128)} %get-tuple-element.66.l_ref, bf16[8,512,768]{2,1,0:T(8,128)(2,1)S(1)} %copy-done, f32[8,2,512]{2,1,0:T(2,128)S(1)} %pad_maximum_fusion.tok_ref, ...), custom_call_target="tpu_custom_call", output_to_operand_aliasing={{1}: (6, {})} | custom-call | flops 4120903680 | bytes 10731520 | tf_op jit(solution)/shard_map/pallas_call | solution.py:527
  193.5 12.9 %shard_map.106 = (f32[1048,768]{1,0:T(8,128)S(1)}, f32[12576,768]{1,0:T(8,128)}) custom-call(s32[40]{0:T(128)S(1)} %copy-done.8, f32[8,6288,512]{2,1,0:T(8,128)} %get-tuple-element.66.l_ref, bf16[8,512,768]{2,1,0:T(8,128)(2,1)S(1)} %copy-done, f32[8,2,512]{2,1,0:T(2,128)S(1)} %pad_maximum_fusion.tok_ref, ...), custom_call_target="tpu_custom_call", output_to_operand_aliasing={{1}: (6, {})} | custom-call | flops 4120903680 | bytes 10731520 | tf_op jit(solution)/shard_map/pallas_call | solution.py:527
  209.6 17.7 %collective-permute-done.5 = f32[2,128,768]{2,1,0:T(8,128)S(1)} collective-permute-done((f32[2,128,768]{2,1,0:T(8,128)S(1)}, f32[2,128,768]{2,1,0:T(8,128)S(1)}, u32[]{:S(2)}, u32[]{:S(2)}) %collective-permute-start.5) | collective-permute-done | bytes 786464 | tf_op jit(solution)/shard_map/ppermute | solution.py:576
  227.5 1.5 collective-permute-start.7
  229.9 8.2 %collective-permute-done.7.a_got_ref = f32[128,768]{1,0:T(8,128)S(1)} collective-permute-done((f32[128,768]{1,0:T(8,128)S(1)}, f32[128,768]{1,0:T(8,128)S(1)}, u32[]{:S(2)}, u32[]{:S(2)}) %collective-permute-start.7) | collective-permute-done | bytes 393248 | tf_op jit(solution)/shard_map/ppermute | solution.py:576
  240.0 11.0 %collective-permute-start.10 = (f32[8,768]{1,0:T(8,128)S(1)}, f32[8,768]{1,0:T(8,128)S(1)}, u32[]{:S(2)}, u32[]{:S(2)}) collective-permute-start(f32[8,768]{1,0:T(8,128)S(1)} %get-tuple-element.59), channel_id=1, source_target_pairs={{0,2},{1,3},{2,0},{3,1},{4,6},{5,7},{6,4},{7,5},{8,10},{9,11},{10,... | collective-permute-start | bytes 73736 | tf_op jit(solution)/shard_map/ppermute | solution.py:576
  251.1 1.6 collective-permute-done.10
  254.8 1.5 collective-permute-start.14
  261.9 8.2 %collective-permute-done.15.refs_2_ = f32[128,768]{1,0:T(8,128)S(1)} collective-permute-done((f32[128,768]{1,0:T(8,128)S(1)}, f32[128,768]{1,0:T(8,128)S(1)}, u32[]{:S(2)}, u32[]{:S(2)}) %collective-permute-start.15) | collective-permute-done | bytes 393248 | tf_op jit(solution)/shard_map/ppermute | solution.py:576
  270.7 4.9 %collective-permute-done.16.refs_3_ = f32[128,768]{1,0:T(8,128)S(1)} collective-permute-done((f32[128,768]{1,0:T(8,128)S(1)}, f32[128,768]{1,0:T(8,128)S(1)}, u32[]{:S(2)}, u32[]{:S(2)}) %collective-permute-start.16) | collective-permute-done | bytes 393248 | tf_op jit(solution)/shard_map/ppermute | solution.py:576
  278.2 2.1 collective-permute-done.17.refs_4_
  280.3 5.9 %collective-permute-done.19.refs_6_ = f32[128,768]{1,0:T(8,128)S(1)} collective-permute-done((f32[128,768]{1,0:T(8,128)S(1)}, f32[128,768]{1,0:T(8,128)S(1)}, u32[]{:S(2)}, u32[]{:S(2)}) %collective-permute-start.19) | collective-permute-done | bytes 393248 | tf_op jit(solution)/shard_map/ppermute | solution.py:576
  286.3 1.8 round.1
  288.1 2.2 place.2.de_ref
  290.4 2.2 place.3
  (120 shorter events, 30.1 us)
Async XLA Ops:
  5.5 44.4 %collective-permute-start.3 = (f32[4,256,768]{2,1,0:T(8,128)}, f32[4,256,768]{2,1,0:T(8,128)}, u32[]{:S(2)}, u32[]{:S(2)}) collective-permute-start(f32[4,256,768]{2,1,0:T(8,128)} %get-tuple-element.42.rest_0_), channel_id=1, source_target_pairs={{0,1},{1,0},{2,3},{3,2},{4,5},{5,4},{6,7},{7,6},{8,9},{9,8},{10,11... | collective-permute-start | bytes 9437192 | tf_op jit(solution)/shard_map/ppermute | solution.py:576
  7.0 7.8 %collective-permute-start.1 = (s32[1024]{0:T(1024)S(1)}, s32[1024]{0:T(1024)S(1)}, u32[]{:S(2)}, u32[]{:S(2)}) collective-permute-start(s32[1024]{0:T(1024)S(1)} %bitcast.35), channel_id=1, source_target_pairs={{0,2},{1,3},{2,0},{3,1},{4,6},{5,7},{6,4},{7,5},{8,10},{9,11},{10,... | collective-permute-start | bytes 12296 | tf_op jit(solution)/shard_map/ppermute | solution.py:576
  9.5 5.3 %collective-permute-start.2 = (s32[1024]{0:T(1024)S(1)}, s32[1024]{0:T(1024)S(1)}, u32[]{:S(2)}, u32[]{:S(2)}) collective-permute-start(s32[1024]{0:T(1024)S(1)} %bitcast.36), channel_id=1, source_target_pairs={{0,3},{1,2},{2,1},{3,0},{4,7},{5,6},{6,5},{7,4},{8,11},{9,10},{10,... | collective-permute-start | bytes 12296 | tf_op jit(solution)/shard_map/ppermute | solution.py:576
  9.7 20.4 %collective-permute-start.21 = (f32[256,768]{1,0:T(8,128)S(1)}, f32[256,768]{1,0:T(8,128)S(1)}, u32[]{:S(2)}, u32[]{:S(2)}) collective-permute-start(f32[256,768]{1,0:T(8,128)S(1)} %get-tuple-element.55.hat_ref), channel_id=1, source_target_pairs={{0,2},{1,3},{2,0},{3,1},{4,6},{5,7},{6,4},{7,5},{8,10},{9,11},{10,... | collective-permute-start | bytes 2359304 | tf_op jit(solution)/shard_map/ppermute | solution.py:576
  12.5 34.1 %collective-permute-start.24 = (f32[256,768]{1,0:T(8,128)S(1)}, f32[256,768]{1,0:T(8,128)}, u32[]{:S(2)}, u32[]{:S(2)}) collective-permute-start(f32[256,768]{1,0:T(8,128)S(1)} %get-tuple-element.63), channel_id=1, source_target_pairs={{0,2},{1,3},{2,0},{3,1},{4,6},{5,7},{6,4},{7,5},{8,10},{9,11},{10,... | collective-permute-start | bytes 2359304 | tf_op jit(solution)/shard_map/ppermute | solution.py:576
  30.1 18.7 %collective-permute-start.22 = (f32[256,768]{1,0:T(8,128)S(1)}, f32[256,768]{1,0:T(8,128)}, u32[]{:S(2)}, u32[]{:S(2)}) collective-permute-start(f32[256,768]{1,0:T(8,128)S(1)} %collective-permute-done.21.rest_0_), channel_id=1, source_target_pairs={{0,4},{4,0},{8,12},{12,8},{1,5},{5,1},{9,13},{13,9},{2,6},{6,2},{1... | collective-permute-start | bytes 2359304 | tf_op jit(solution)/shard_map/ppermute | solution.py:576
  32.0 17.9 %collective-permute-start.23 = (f32[256,768]{1,0:T(8,128)S(1)}, f32[256,768]{1,0:T(8,128)}, u32[]{:S(2)}, u32[]{:S(2)}) collective-permute-start(f32[256,768]{1,0:T(8,128)S(1)} %collective-permute-done.21.rest_0_), channel_id=1, source_target_pairs={{0,8},{4,12},{8,0},{12,4},{1,9},{5,13},{9,1},{13,5},{2,10},{6,14},... | collective-permute-start | bytes 2359304 | tf_op jit(solution)/shard_map/ppermute | solution.py:576
  35.2 68.5 %collective-permute-start.25 = (f32[256,768]{1,0:T(8,128)S(1)}, f32[256,768]{1,0:T(8,128)}, u32[]{:S(2)}, u32[]{:S(2)}) collective-permute-start(f32[256,768]{1,0:T(8,128)S(1)} %collective-permute-done.21.rest_0_), channel_id=1, source_target_pairs={{0,1},{1,0},{2,3},{3,2},{4,5},{5,4},{6,7},{7,6},{8,9},{9,8},{10,11... | collective-permute-start | bytes 2359304 | tf_op jit(solution)/shard_map/ppermute | solution.py:576
  46.6 57.1 %collective-permute-start.28 = (f32[256,768]{1,0:T(8,128)}, f32[256,768]{1,0:T(8,128)}, u32[]{:S(2)}, u32[]{:S(2)}) collective-permute-start(f32[256,768]{1,0:T(8,128)} %collective-permute-done.24.rest_3_), channel_id=1, source_target_pairs={{0,1},{1,0},{2,3},{3,2},{4,5},{5,4},{6,7},{7,6},{8,9},{9,8},{10,11... | collective-permute-start | bytes 2359304 | tf_op jit(solution)/shard_map/ppermute | solution.py:576
  48.8 54.9 %collective-permute-start.26 = (f32[256,768]{1,0:T(8,128)}, f32[256,768]{1,0:T(8,128)}, u32[]{:S(2)}, u32[]{:S(2)}) collective-permute-start(f32[256,768]{1,0:T(8,128)} %collective-permute-done.22.rest_1_), channel_id=1, source_target_pairs={{0,1},{1,0},{2,3},{3,2},{4,5},{5,4},{6,7},{7,6},{8,9},{9,8},{10,11... | collective-permute-start | bytes 2359304 | tf_op jit(solution)/shard_map/ppermute | solution.py:576
  49.9 53.8 %collective-permute-start.27 = (f32[256,768]{1,0:T(8,128)}, f32[256,768]{1,0:T(8,128)}, u32[]{:S(2)}, u32[]{:S(2)}) collective-permute-start(f32[256,768]{1,0:T(8,128)} %collective-permute-done.23.rest_2_), channel_id=1, source_target_pairs={{0,1},{1,0},{2,3},{3,2},{4,5},{5,4},{6,7},{7,6},{8,9},{9,8},{10,11... | collective-permute-start | bytes 2359304 | tf_op jit(solution)/shard_map/ppermute | solution.py:576
  161.2 19.3 %collective-permute-start.30 = (f32[2096,768]{1,0:T(8,128)S(1)}, f32[2096,768]{1,0:T(8,128)S(1)}, u32[]{:S(2)}, u32[]{:S(2)}) collective-permute-start(f32[2096,768]{1,0:T(8,128)S(1)} %get-tuple-element.71), channel_id=1, source_target_pairs={{0,1},{1,0},{2,3},{3,2},{4,5},{5,4},{6,7},{7,6},{8,9},{9,8},{10,11... | collective-permute-start | bytes 19316744 | tf_op jit(solution)/shard_map/ppermute | solution.py:576
  180.0 13.6 %collective-permute-start.29 = (f32[2096,768]{1,0:T(8,128)S(1)}, f32[2096,768]{1,0:T(8,128)S(1)}, u32[]{:S(2)}, u32[]{:S(2)}) collective-permute-start(f32[2096,768]{1,0:T(8,128)S(1)} %get-tuple-element.70), channel_id=1, source_target_pairs={{0,1},{1,0},{2,3},{3,2},{4,5},{5,4},{6,7},{7,6},{8,9},{9,8},{10,11... | collective-permute-start | bytes 19316744 | tf_op jit(solution)/shard_map/ppermute | solution.py:576
  180.4 26.2 %collective-permute-start.4 = (f32[4,256,768]{2,1,0:T(8,128)S(1)}, f32[4,256,768]{2,1,0:T(8,128)S(1)}, u32[]{:S(2)}, u32[]{:S(2)}) collective-permute-start(f32[4,256,768]{2,1,0:T(8,128)S(1)} %copy-done.15), channel_id=1, source_target_pairs={{0,1},{1,0},{2,3},{3,2},{4,5},{5,4},{6,7},{7,6},{8,9},{9,8},{10,11... | collective-permute-start | bytes 9437192 | tf_op jit(solution)/shard_map/ppermute | solution.py:576
  193.1 95.0 %collective-permute-start.32 = (f32[1048,768]{1,0:T(8,128)S(1)}, f32[1048,768]{1,0:T(8,128)S(1)}, u32[]{:S(2)}, u32[]{:S(2)}) collective-permute-start(f32[1048,768]{1,0:T(8,128)S(1)} %get-tuple-element.75), channel_id=1, source_target_pairs={{0,1},{1,0},{2,3},{3,2},{4,5},{5,4},{6,7},{7,6},{8,9},{9,8},{10,11... | collective-permute-start | bytes 9658376 | tf_op jit(solution)/shard_map/ppermute | solution.py:576
  206.4 83.9 %collective-permute-start.31 = (f32[1048,768]{1,0:T(8,128)S(1)}, f32[1048,768]{1,0:T(8,128)S(1)}, u32[]{:S(2)}, u32[]{:S(2)}) collective-permute-start(f32[1048,768]{1,0:T(8,128)S(1)} %get-tuple-element.74), channel_id=1, source_target_pairs={{0,1},{1,0},{2,3},{3,2},{4,5},{5,4},{6,7},{7,6},{8,9},{9,8},{10,11... | collective-permute-start | bytes 9658376 | tf_op jit(solution)/shard_map/ppermute | solution.py:576
  207.5 19.9 %collective-permute-start.5 = (f32[2,128,768]{2,1,0:T(8,128)S(1)}, f32[2,128,768]{2,1,0:T(8,128)S(1)}, u32[]{:S(2)}, u32[]{:S(2)}) collective-permute-start(f32[2,128,768]{2,1,0:T(8,128)S(1)} %get-tuple-element.48), channel_id=1, source_target_pairs={{0,4},{4,0},{8,12},{12,8},{1,5},{5,1},{9,13},{13,9},{2,6},{6,2},{1... | collective-permute-start | bytes 2359304 | tf_op jit(solution)/shard_map/ppermute | solution.py:576
  208.2 20.9 %collective-permute-start.6 = (f32[2,128,768]{2,1,0:T(8,128)S(1)}, f32[2,128,768]{2,1,0:T(8,128)S(1)}, u32[]{:S(2)}, u32[]{:S(2)}) collective-permute-start(f32[2,128,768]{2,1,0:T(8,128)S(1)} %get-tuple-element.51), channel_id=1, source_target_pairs={{0,8},{4,12},{8,0},{12,4},{1,9},{5,13},{9,1},{13,5},{2,10},{6,14},... | collective-permute-start | bytes 2359304 | tf_op jit(solution)/shard_map/ppermute | solution.py:576
  227.5 10.6 %collective-permute-start.7 = (f32[128,768]{1,0:T(8,128)S(1)}, f32[128,768]{1,0:T(8,128)S(1)}, u32[]{:S(2)}, u32[]{:S(2)}) collective-permute-start(f32[128,768]{1,0:T(8,128)S(1)} %get-tuple-element.83), channel_id=1, source_target_pairs={{0,8},{4,12},{8,0},{12,4},{1,9},{5,13},{9,1},{13,5},{2,10},{6,14},... | collective-permute-start | bytes 1179656 | tf_op jit(solution)/shard_map/ppermute | solution.py:576
  229.2 10.3 %collective-permute-start.8 = (f32[128,768]{1,0:T(8,128)S(1)}, f32[128,768]{1,0:T(8,128)S(1)}, u32[]{:S(2)}, u32[]{:S(2)}) collective-permute-start(f32[128,768]{1,0:T(8,128)S(1)} %get-tuple-element.81), channel_id=1, source_target_pairs={{0,4},{4,0},{8,12},{12,8},{1,5},{5,1},{9,13},{13,9},{2,6},{6,2},{1... | collective-permute-start | bytes 1179656 | tf_op jit(solution)/shard_map/ppermute | solution.py:576
  240.0 12.8 %collective-permute-start.10 = (f32[8,768]{1,0:T(8,128)S(1)}, f32[8,768]{1,0:T(8,128)S(1)}, u32[]{:S(2)}, u32[]{:S(2)}) collective-permute-start(f32[8,768]{1,0:T(8,128)S(1)} %get-tuple-element.59), channel_id=1, source_target_pairs={{0,2},{1,3},{2,0},{3,1},{4,6},{5,7},{6,4},{7,5},{8,10},{9,11},{10,... | collective-permute-start | bytes 73736 | tf_op jit(solution)/shard_map/ppermute | solution.py:576
  251.0 3.3 %collective-permute-start.11 = (f32[8,768]{1,0:T(8,128)S(1)}, f32[8,768]{1,0:T(8,128)S(1)}, u32[]{:S(2)}, u32[]{:S(2)}) collective-permute-start(f32[8,768]{1,0:T(8,128)S(1)} %get-tuple-element.59), channel_id=1, source_target_pairs={{0,3},{1,2},{2,1},{3,0},{4,7},{5,6},{6,5},{7,4},{8,11},{9,10},{10,... | collective-permute-start | bytes 73736 | tf_op jit(solution)/shard_map/ppermute | solution.py:576
  251.0 3.3 %collective-permute-start.9 = (f32[8,768]{1,0:T(8,128)S(1)}, f32[8,768]{1,0:T(8,128)S(1)}, u32[]{:S(2)}, u32[]{:S(2)}) collective-permute-start(f32[8,768]{1,0:T(8,128)S(1)} %get-tuple-element.59), channel_id=1, source_target_pairs={{0,1},{1,0},{2,3},{3,2},{4,5},{5,4},{6,7},{7,6},{8,9},{9,8},{10,11... | collective-permute-start | bytes 73736 | tf_op jit(solution)/shard_map/ppermute | solution.py:576
  254.2 3.9 %collective-permute-start.13 = (f32[8,768]{1,0:T(8,128)S(1)}, f32[8,768]{1,0:T(8,128)S(1)}, u32[]{:S(2)}, u32[]{:S(2)}) collective-permute-start(f32[8,768]{1,0:T(8,128)S(1)} %add_add_fusion.1), channel_id=1, source_target_pairs={{0,8},{4,12},{8,0},{12,4},{1,9},{5,13},{9,1},{13,5},{2,10},{6,14},... | collective-permute-start | bytes 73736 | tf_op jit(solution)/shard_map/ppermute | solution.py:576
  254.8 5.0 %collective-permute-start.14 = (f32[8,768]{1,0:T(8,128)S(1)}, f32[8,768]{1,0:T(8,128)S(1)}, u32[]{:S(2)}, u32[]{:S(2)}) collective-permute-start(f32[8,768]{1,0:T(8,128)S(1)} %add_add_fusion.1), channel_id=1, source_target_pairs={{0,12},{4,8},{8,4},{12,0},{1,13},{5,9},{9,5},{13,1},{2,14},{6,10},... | collective-permute-start | bytes 73736 | tf_op jit(solution)/shard_map/ppermute | solution.py:576
  256.4 4.4 %collective-permute-start.12 = (f32[8,768]{1,0:T(8,128)S(1)}, f32[8,768]{1,0:T(8,128)S(1)}, u32[]{:S(2)}, u32[]{:S(2)}) collective-permute-start(f32[8,768]{1,0:T(8,128)S(1)} %add_add_fusion.1), channel_id=1, source_target_pairs={{0,4},{4,0},{8,12},{12,8},{1,5},{5,1},{9,13},{13,9},{2,6},{6,2},{1... | collective-permute-start | bytes 73736 | tf_op jit(solution)/shard_map/ppermute | solution.py:576
  258.1 12.0 %collective-permute-start.15 = (f32[128,768]{1,0:T(8,128)S(1)}, f32[128,768]{1,0:T(8,128)S(1)}, u32[]{:S(2)}, u32[]{:S(2)}) collective-permute-start(f32[128,768]{1,0:T(8,128)S(1)} %get-tuple-element.60.refs_0_), channel_id=1, source_target_pairs={{0,4},{4,0},{8,12},{12,8},{1,5},{5,1},{9,13},{13,9},{2,6},{6,2},{1... | collective-permute-start | bytes 1179656 | tf_op jit(solution)/shard_map/ppermute | solution.py:576
  259.8 15.8 %collective-permute-start.16 = (f32[128,768]{1,0:T(8,128)S(1)}, f32[128,768]{1,0:T(8,128)S(1)}, u32[]{:S(2)}, u32[]{:S(2)}) collective-permute-start(f32[128,768]{1,0:T(8,128)S(1)} %get-tuple-element.61.refs_1_), channel_id=1, source_target_pairs={{0,4},{4,0},{8,12},{12,8},{1,5},{5,1},{9,13},{13,9},{2,6},{6,2},{1... | collective-permute-start | bytes 1179656 | tf_op jit(solution)/shard_map/ppermute | solution.py:576
  260.8 15.4 %collective-permute-start.18 = (f32[128,768]{1,0:T(8,128)S(1)}, f32[128,768]{1,0:T(8,128)S(1)}, u32[]{:S(2)}, u32[]{:S(2)}) collective-permute-start(f32[128,768]{1,0:T(8,128)S(1)} %get-tuple-element.61.refs_1_), channel_id=1, source_target_pairs={{0,8},{4,12},{8,0},{12,4},{1,9},{5,13},{9,1},{13,5},{2,10},{6,14},... | collective-permute-start | bytes 1179656 | tf_op jit(solution)/shard_map/ppermute | solution.py:576
  270.1 10.3 %collective-permute-start.17 = (f32[128,768]{1,0:T(8,128)S(1)}, f32[128,768]{1,0:T(8,128)S(1)}, u32[]{:S(2)}, u32[]{:S(2)}) collective-permute-start(f32[128,768]{1,0:T(8,128)S(1)} %get-tuple-element.60.refs_0_), channel_id=1, source_target_pairs={{0,8},{4,12},{8,0},{12,4},{1,9},{5,13},{9,1},{13,5},{2,10},{6,14},... | collective-permute-start | bytes 1179656 | tf_op jit(solution)/shard_map/ppermute | solution.py:576
  275.6 10.7 %collective-permute-start.19 = (f32[128,768]{1,0:T(8,128)S(1)}, f32[128,768]{1,0:T(8,128)S(1)}, u32[]{:S(2)}, u32[]{:S(2)}) collective-permute-start(f32[128,768]{1,0:T(8,128)S(1)} %collective-permute-done.15.refs_2_), channel_id=1, source_target_pairs={{0,8},{4,12},{8,0},{12,4},{1,9},{5,13},{9,1},{13,5},{2,10},{6,14},... | collective-permute-start | bytes 1179656 | tf_op jit(solution)/shard_map/ppermute | solution.py:576
  276.2 10.1 %collective-permute-start.20 = (f32[128,768]{1,0:T(8,128)S(1)}, f32[128,768]{1,0:T(8,128)S(1)}, u32[]{:S(2)}, u32[]{:S(2)}) collective-permute-start(f32[128,768]{1,0:T(8,128)S(1)} %collective-permute-done.18.refs_5_), channel_id=1, source_target_pairs={{0,4},{4,0},{8,12},{12,8},{1,5},{5,1},{9,13},{13,9},{2,6},{6,2},{1... | collective-permute-start | bytes 1179656 | tf_op jit(solution)/shard_map/ppermute | solution.py:576
  (17 other events, 288.8 us)

commit v6 on v5

--- a/solution.py
+++ b/solution.py
@@ -117,44 +117,53 @@
     return (jnp.where(is_target, probs - 1.0, probs) * weight).astype(jnp.bfloat16)
 
 
-def dz_kernel(idx_ref, e_hbm, l_hbm, tok_ref, lab_ref, own_ref, mate_ref, tl_ref, l_out_ref, acc_ref, out_ref, et_ref, e_ref, l_ref, sem, e_sem, l_sem):
+def dz_kernel(idx_ref, e_hbm, l_hbm, tok_ref, lab_ref, own_ref, mate_ref, tl_ref, l_out_ref, acc_ref, out_ref, et_ref, e_ref, l_ref, sem, e_sem, l_sem, first_sem):
     i = pl.program_id(0)
     rows = e_ref.shape[0]
     slot = i % 2
     live = i < idx_ref[NEAR_PAIRS]
-    size = 512
-    full = rows // size
+    table = e_hbm.at[pl.ds(pl.multiple_of(idx_ref[CORE] * rows, 16), rows), :]
+    chunks = chunk_list(rows, DZ_CHUNK)
+
+    def first(k):
+        at = pl.ds(*chunks[k])
+        return (
+            pltpu.make_async_copy(table.at[at, :], e_ref.at[at, :], e_sem.at[k]),
+            pltpu.make_async_copy(l_hbm.at[0, at, :], l_ref.at[0, at, :], first_sem.at[k]),
+        )
 
     def fetch(pair):
-        start(split_copy(l_hbm.at[pair], l_ref.at[pair % 2], l_sem.at[pair % 2], size))
-
-    def table(k, n):
-        at = pl.multiple_of(k * size, size)
-        return pltpu.make_async_copy(e_hbm.at[pl.ds(pl.multiple_of(idx_ref[CORE] * rows + at, 16), n), :], e_ref.at[pl.ds(at, n), :], e_sem.at[k])
+        start(split_copy(l_hbm.at[pair], l_ref.at[pair % 2], l_sem.at[pair % 2], 512))
 
     @pl.when(i == 0)
     def _():
-        for k, (_, n) in enumerate(chunk_list(rows, size)):
-            table(k, n).start()
-        fetch(0)
-
-        def turn(k, carry):
-            table(k, size).wait()
-            at = pl.multiple_of(k * size, size)
-            et_ref[:, pl.ds(at, size)] = e_ref[pl.ds(at, size), :].T
-            return carry
-
-        lax.fori_loop(0, full, turn, 0)
-        if rows > full * size:
-            table(full, rows - full * size).wait()
-            et_ref[:, full * size:] = e_ref[full * size:, :].T
+        for k in range(len(chunks)):
+            start(first(k))
 
     pl.when(i + 1 < idx_ref[NEAR_PAIRS])(lambda: fetch(i + 1))
 
-    @pl.when(live)
+    @pl.when(i == 0)
+    def _():
+        def turn(k):
+            at, n = chunks[k]
+            et_ref[:, at:at + n] = e_ref[at:at + n, :].T
+
+        def ready(k):
+            if k == 0:
+                first(0)[0].wait()
+                turn(0)
+            if k + 1 < len(chunks):
+                first(k + 1)[0].wait()
+            first(k)[1].wait()
+            if k + 1 < len(chunks):
+                turn(k + 1)
+
+        dz_step(idx_ref, et_ref, l_ref.at[0], tok_ref, lab_ref, tl_ref, acc_ref, ready)
+
+    @pl.when(live & (i > 0))
     def _():
         pltpu.make_async_copy(l_hbm.at[0], l_ref.at[slot], l_sem.at[slot]).wait()
-        dz_step(idx_ref, et_ref, l_ref.at[slot], tok_ref, lab_ref, tl_ref, acc_ref)
+        dz_step(idx_ref, et_ref, l_ref.at[slot], tok_ref, lab_ref, tl_ref, acc_ref, None)
 
     def sent():
         for h in range(2):
@@ -179,12 +188,14 @@
     pl.when(i == pl.num_programs(0) - 1)(sent)
 
 
-def dz_step(idx_ref, et_ref, l_ref, tok_ref, lab_ref, tl_ref, acc_ref):
+def dz_step(idx_ref, et_ref, l_ref, tok_ref, lab_ref, tl_ref, acc_ref, ready):
     lse = tok_ref[0, 0:1, :]
     weight = tok_ref[0, 1:2, :]
     label = lab_ref[0] - idx_ref[ROW_START]
     target = jnp.zeros((1, PAIR), jnp.float32)
-    for start, n in chunk_list(et_ref.shape[1], DZ_CHUNK):
+    for k, (start, n) in enumerate(chunk_list(et_ref.shape[1], DZ_CHUNK)):
+        if ready is not None:
+            ready(k)
         tile = l_ref[start:start + n, :]
         is_target = lax.broadcasted_iota(jnp.int32, (n, PAIR), 0) == label - start
         grad = grad_tile(tile, lse, weight, is_target)
@@ -220,10 +231,9 @@
         return part_ref.at[pl.ds(at, block), :], out_ref.at[pl.ds(half_start, block), :]
 
     def fetch(i):
-        start(split_copy(source(i), buf_ref.at[i % 3], sem.at[i % 3], 264))
+        start(split_copy(source(i), buf_ref.at[i % 2], sem.at[i % 2], 264))
 
     fetch(0)
-    pl.when(steps > 1)(lambda: fetch(1))
     got = None
     if got_ref is not None:
         target = rows_at(1 - core, got_offset, got_ref.shape[0])
@@ -232,8 +242,8 @@
     part_ref[...] = jnp.zeros_like(part_ref)
 
     def step(i, carry):
-        pltpu.make_async_copy(source(i), buf_ref.at[i % 3], sem.at[i % 3]).wait()
-        pl.when(i + 2 < steps)(lambda: fetch(i + 2))
+        pltpu.make_async_copy(source(i), buf_ref.at[i % 2], sem.at[i % 2]).wait()
+        pl.when(i + 1 < steps)(lambda: fetch(i + 1))
         k = i // count
         pair = idx_ref[PAIR_IDS + i % count]
         lse = tok_ref[pair, 0:1, :]
@@ -241,7 +251,7 @@
         label = lab_ref[pair] - idx_ref[ROW_START] - offset - k * block
         for at, n in chunk_list(block, 528):
             is_target = lax.broadcasted_iota(jnp.int32, (n, PAIR), 0) == label - at
-            grad = grad_tile(buf_ref[i % 3, at:at + n, :], lse, weight, is_target)
+            grad = grad_tile(buf_ref[i % 2, at:at + n, :], lse, weight, is_target)
             part_ref[pl.ds(pl.multiple_of(k * block + at, 8), n), :] += jnp.dot(grad, z_ref[pair], preferred_element_type=jnp.float32)
         pl.when(i % count == count - 1)(lambda: start(split_copy(*write(k), sem.at[4], 264)))
         return carry
@@ -490,8 +500,9 @@
             pltpu.VMEM((rows, width), jnp.bfloat16),
             pltpu.VMEM((2, rows, PAIR), jnp.float32),
             pltpu.SemaphoreType.DMA((2,)),
-            pltpu.SemaphoreType.DMA((pl.cdiv(rows, 512),)),
+            pltpu.SemaphoreType.DMA((pl.cdiv(rows, DZ_CHUNK),)),
             pltpu.SemaphoreType.DMA((2,)),
+            pltpu.SemaphoreType.DMA((pl.cdiv(rows, DZ_CHUNK),)),
         ],
     )
     half = jax.ShapeDtypeStruct((4, BLOCK, width), jnp.float32)
@@ -522,7 +533,7 @@
         grid=(1,),
         in_specs=[ANY, whole(zc), whole(tok), whole(lab)] + extra_specs,
         out_specs=[pl.BlockSpec((rows, width), lambda i, s: (0, 0), pipeline_mode=pl.Buffered(1)), ANY],
-        scratch_shapes=[pltpu.VMEM((3, total // 6, PAIR), jnp.float32), pltpu.SemaphoreType.DMA((5,))],
+        scratch_shapes=[pltpu.VMEM((2, rows, PAIR), jnp.float32), pltpu.SemaphoreType.DMA((5,))],
     )
     return pl.pallas_call(
         functools.partial(de_kernel, offset, rows, got_offset if got is not None else None),

time: 293 us -> 300 us (1.024)
  Pallas kernels: 159 us -> 165 us
    pallas_call x4, Pallas kernels: 62.6 us -> 67.2 us  [call_de(): pl.pallas_call(functools.partial(de_kernel, offset, rows, got_offset if g...]
  transfers between devices with their start and end apart: 33 -> 33, of which waited for: 15 -> 15; matrix products, arithmetic and copies ran while one was open for 2% -> 2% of each run, Pallas kernels for 34% -> 35%
where the time goes in v6:
time: 300 us; the launch traced here: 299 us
  Pallas kernels  165 us (55%)
  waiting for transfers between devices  79.2 us (26%)
  starting transfers between devices  36.2 us (12%)
  local copies, waits for them, and re-layouts  9.74 us (3%)
  between operations  4.58 us (2%)
  other arithmetic  4.35 us (1%)
    ppermute x33, waiting for transfers between devices, flip(): return lax.ppermute(x, axis, [(k, k ^ bits) for k in range(n)])  79.2 us
    pallas_call x4, Pallas kernels, call_de(): pl.pallas_call(functools.partial(de_kernel, offset, rows, got_offset if g...  67.2 us
    pallas_call x2, Pallas kernels, call_logits(): pl.pallas_call(functools.partial(logits_kernel, count, base, order, len(p...  48.7 us
    ppermute x33, starting transfers between devices, flip(): return lax.ppermute(x, axis, [(k, k ^ bits) for k in range(n)])  36.2 us
    pallas_call x1, Pallas kernels, call_dz(): pl.pallas_call(dz_kernel, grid_spec=spec, out_shape=[half, half, jax.Shap...  27 us
    pallas_call x2, Pallas kernels, call_lse(): pl.pallas_call(lse_kernel, in_specs=[vmem, vmem, vmem], out_specs=vmem, o...  10.9 us
    unnamed x32, local copies, waits for them, and re-layouts  7.12 us
  transfers between devices with their start and end apart: 33, of which 15 were waited for; matrix products, arithmetic and copies ran while one was open for 2% of the time, Pallas kernels for 35%

profile of v6, /device:TPU:0, one launch (start us, length us, event | category | flops | bytes accessed | tf_op | source)
XLA Modules:
  0.0 298.9 jit_solution(14113164176613339270)
XLA Ops:
  2.2 3.4 %norm.1 = (f32[4,256,768]{2,1,0:T(8,128)}, f32[256,128]{1,0:T(8,128)S(1)}, f32[256,768]{1,0:T(8,128)S(1)}, f32[256,768]{1,0:T(8,128)S(1)}) custom-call(s32[10]{0:T(128)S(1)} %stack.58.pick_ref, bf16[4,256,768]{2,1,0:T(8,128)(2,1)S(1)} %bitcast.34), custom_call_target="tpu_custom_call" | custom-call | flops 10000000 | bytes 8000000 | tf_op jit(solution)/shard_map/norm/pallas_call | solution.py:340
  7.0 2.5 collective-permute-start.1
  9.7 1.9 collective-permute-start.21
  12.5 2.2 collective-permute-start.24
  18.6 11.5 %collective-permute-done.21.rest_0_ = f32[256,768]{1,0:T(8,128)S(1)} collective-permute-done((f32[256,768]{1,0:T(8,128)S(1)}, f32[256,768]{1,0:T(8,128)S(1)}, u32[]{:S(2)}, u32[]{:S(2)}) %collective-permute-start.21) | collective-permute-done | bytes 786464 | tf_op jit(solution)/shard_map/ppermute | solution.py:587
  30.1 1.9 collective-permute-start.22
  32.0 1.6 collective-permute-start.23
  35.2 11.4 %collective-permute-done.24.rest_3_ = f32[256,768]{1,0:T(8,128)} collective-permute-done((f32[256,768]{1,0:T(8,128)S(1)}, f32[256,768]{1,0:T(8,128)}, u32[]{:S(2)}, u32[]{:S(2)}) %collective-permute-start.24) | collective-permute-done | bytes 786464 | tf_op jit(solution)/shard_map/ppermute | solution.py:587
  46.6 2.2 collective-permute-done.22.rest_1_
  49.9 18.7 %logits_near.1 = (f32[8,6288,512]{2,1,0:T(8,128)}, bf16[8,512,768]{2,1,0:T(8,128)(2,1)}, f32[4,2,512]{2,1,0:T(2,128)}) custom-call(s32[40]{0:T(128)} %concatenate.11.idx_ref, bf16[12576,768]{1,0:T(8,128)(2,1)} %e_hbm.5, f32[768]{0:T(1024)} %gamma_ref.5, f32[768]{0:T(1024)} %beta_ref.3, f32[4,256,768]{2,1,0:T(8,128)} %get-tuple-element.42.rest_0_, ...), custom_call_target="tpu_custom_call" | custom-call | flops 14835253248 | bytes 38633472 | tf_op jit(solution)/shard_map/logits_near/pallas_call | solution.py:468
  69.3 5.6 %shard_map.101.tok_ref = f32[4,2,512]{2,1,0:T(2,128)S(1)} custom-call(f32[4,2,512]{2,1,0:T(2,128)S(1)} %copy-done.11, s32[4,1,512]{2,1,0:T(1,128)S(1)} %slice.49.lab_ref, f32[1,512]{1,0:T(1,128)S(1)} %broadcast_in_dim.57.scale_ref), custom_call_target="tpu_custom_call" | custom-call | flops 10000000 | bytes 1000000 | tf_op jit(solution)/shard_map/pallas_call | solution.py:306
  75.5 27.0 %dz_part.1 = (f32[4,256,768]{2,1,0:T(8,128)}, f32[4,256,768]{2,1,0:T(8,128)}, f32[4,1,512]{2,1,0:T(1,128)}, f32[8,6288,512]{2,1,0:T(8,128)}) custom-call(s32[40]{0:T(128)} %concatenate.11.idx_ref, bf16[12576,768]{1,0:T(8,128)(2,1)} %e_hbm.5, f32[8,6288,512]{2,1,0:T(8,128)} %get-tuple-element.43.l_hbm, ...), custom_call_target="tpu_custom_call", output_to_operand_aliasing={{3}: (2, {})} | custom-call | flops 14835253248 | bytes 38633472 | tf_op jit(solution)/shard_map/dz_part/pallas_call | solution.py:509
  105.3 30.0 %logits_far.1 = (f32[8,6288,512]{2,1,0:T(8,128)}, bf16[8,512,768]{2,1,0:T(8,128)(2,1)}, f32[4,2,512]{2,1,0:T(2,128)}) custom-call(s32[40]{0:T(128)} %concatenate.11.idx_ref, bf16[12576,768]{1,0:T(8,128)(2,1)} %e_hbm.5, f32[768]{0:T(1024)} %gamma_ref.5, f32[768]{0:T(1024)} %beta_ref.3, ...), custom_call_target="tpu_custom_call", output_to_operand_aliasing={{0}: (12, {}), {1}: (13, {})} | custom-call | flops 14835253248 | bytes 38633472 | tf_op jit(solution)/shard_map/logits_far/pallas_call | solution.py:468
  136.1 5.3 %shard_map.102 = f32[4,2,512]{2,1,0:T(2,128)S(1)} custom-call(f32[4,2,512]{2,1,0:T(2,128)S(1)} %copy-done.10, s32[4,1,512]{2,1,0:T(1,128)S(1)} %slice.53.lab_ref, f32[1,512]{1,0:T(1,128)S(1)} %broadcast_in_dim.57.scale_ref), custom_call_target="tpu_custom_call" | custom-call | flops 10000000 | bytes 1000000 | tf_op jit(solution)/shard_map/pallas_call | solution.py:306
  141.4 2.8 copy-done
  144.2 18.7 %shard_map.103 = (f32[2096,768]{1,0:T(8,128)S(1)}, f32[12576,768]{1,0:T(8,128)}) custom-call(s32[40]{0:T(128)S(1)} %copy-done.8, f32[8,6288,512]{2,1,0:T(8,128)} %get-tuple-element.66.l_ref, bf16[8,512,768]{2,1,0:T(8,128)(2,1)S(1)} %copy-done, f32[8,2,512]{2,1,0:T(2,128)S(1)} %pad_maximum_fusion.tok_ref, s32[8,1,512]{2,1,0:T(1,128)S(1)} %reshape.97.lab_ref), custom_call_target="tpu_custom_call" | custom-call | flops 8241807360 | bytes 21463040 | tf_op jit(solution)/shard_map/pallas_call | solution.py:538
  163.0 19.1 %shard_map.104 = (f32[2096,768]{1,0:T(8,128)S(1)}, f32[12576,768]{1,0:T(8,128)}) custom-call(s32[40]{0:T(128)S(1)} %copy-done.8, f32[8,6288,512]{2,1,0:T(8,128)} %get-tuple-element.66.l_ref, bf16[8,512,768]{2,1,0:T(8,128)(2,1)S(1)} %copy-done, f32[8,2,512]{2,1,0:T(2,128)S(1)} %pad_maximum_fusion.tok_ref, ...), custom_call_target="tpu_custom_call", output_to_operand_aliasing={{1}: (5, {})} | custom-call | flops 8241807360 | bytes 21463040 | tf_op jit(solution)/shard_map/pallas_call | solution.py:538
  182.7 14.2 %shard_map.105 = (f32[1048,768]{1,0:T(8,128)S(1)}, f32[12576,768]{1,0:T(8,128)}) custom-call(s32[40]{0:T(128)S(1)} %copy-done.8, f32[8,6288,512]{2,1,0:T(8,128)} %get-tuple-element.66.l_ref, bf16[8,512,768]{2,1,0:T(8,128)(2,1)S(1)} %copy-done, f32[8,2,512]{2,1,0:T(2,128)S(1)} %pad_maximum_fusion.tok_ref, ...), custom_call_target="tpu_custom_call", output_to_operand_aliasing={{1}: (6, {})} | custom-call | flops 4120903680 | bytes 10731520 | tf_op jit(solution)/shard_map/pallas_call | solution.py:538
  197.4 15.2 %shard_map.106 = (f32[1048,768]{1,0:T(8,128)S(1)}, f32[12576,768]{1,0:T(8,128)}) custom-call(s32[40]{0:T(128)S(1)} %copy-done.8, f32[8,6288,512]{2,1,0:T(8,128)} %get-tuple-element.66.l_ref, bf16[8,512,768]{2,1,0:T(8,128)(2,1)S(1)} %copy-done, f32[8,2,512]{2,1,0:T(2,128)S(1)} %pad_maximum_fusion.tok_ref, ...), custom_call_target="tpu_custom_call", output_to_operand_aliasing={{1}: (6, {})} | custom-call | flops 4120903680 | bytes 10731520 | tf_op jit(solution)/shard_map/pallas_call | solution.py:538
  215.8 17.7 %collective-permute-done.5 = f32[2,128,768]{2,1,0:T(8,128)S(1)} collective-permute-done((f32[2,128,768]{2,1,0:T(8,128)S(1)}, f32[2,128,768]{2,1,0:T(8,128)S(1)}, u32[]{:S(2)}, u32[]{:S(2)}) %collective-permute-start.5) | collective-permute-done | bytes 786464 | tf_op jit(solution)/shard_map/ppermute | solution.py:587
  233.7 1.5 collective-permute-start.7
  236.1 8.2 %collective-permute-done.7.a_got_ref = f32[128,768]{1,0:T(8,128)S(1)} collective-permute-done((f32[128,768]{1,0:T(8,128)S(1)}, f32[128,768]{1,0:T(8,128)S(1)}, u32[]{:S(2)}, u32[]{:S(2)}) %collective-permute-start.7) | collective-permute-done | bytes 393248 | tf_op jit(solution)/shard_map/ppermute | solution.py:587
  246.2 10.9 %collective-permute-start.10 = (f32[8,768]{1,0:T(8,128)S(1)}, f32[8,768]{1,0:T(8,128)S(1)}, u32[]{:S(2)}, u32[]{:S(2)}) collective-permute-start(f32[8,768]{1,0:T(8,128)S(1)} %get-tuple-element.59), channel_id=1, source_target_pairs={{0,2},{1,3},{2,0},{3,1},{4,6},{5,7},{6,4},{7,5},{8,10},{9,11},{10,... | collective-permute-start | bytes 73736 | tf_op jit(solution)/shard_map/ppermute | solution.py:587
  257.2 1.6 collective-permute-done.10
  261.0 1.5 collective-permute-start.14
  268.0 8.1 %collective-permute-done.15.refs_2_ = f32[128,768]{1,0:T(8,128)S(1)} collective-permute-done((f32[128,768]{1,0:T(8,128)S(1)}, f32[128,768]{1,0:T(8,128)S(1)}, u32[]{:S(2)}, u32[]{:S(2)}) %collective-permute-start.15) | collective-permute-done | bytes 393248 | tf_op jit(solution)/shard_map/ppermute | solution.py:587
  276.8 4.9 %collective-permute-done.16.refs_3_ = f32[128,768]{1,0:T(8,128)S(1)} collective-permute-done((f32[128,768]{1,0:T(8,128)S(1)}, f32[128,768]{1,0:T(8,128)S(1)}, u32[]{:S(2)}, u32[]{:S(2)}) %collective-permute-start.16) | collective-permute-done | bytes 393248 | tf_op jit(solution)/shard_map/ppermute | solution.py:587
  284.4 2.1 collective-permute-done.17.refs_4_
  286.4 5.9 %collective-permute-done.19.refs_6_ = f32[128,768]{1,0:T(8,128)S(1)} collective-permute-done((f32[128,768]{1,0:T(8,128)S(1)}, f32[128,768]{1,0:T(8,128)S(1)}, u32[]{:S(2)}, u32[]{:S(2)}) %collective-permute-start.19) | collective-permute-done | bytes 393248 | tf_op jit(solution)/shard_map/ppermute | solution.py:587
  292.4 1.8 round.1
  294.2 2.2 place.2.de_ref
  296.5 2.2 place.3
  (120 shorter events, 30.3 us)
Async XLA Ops:
  5.5 44.4 %collective-permute-start.3 = (f32[4,256,768]{2,1,0:T(8,128)}, f32[4,256,768]{2,1,0:T(8,128)}, u32[]{:S(2)}, u32[]{:S(2)}) collective-permute-start(f32[4,256,768]{2,1,0:T(8,128)} %get-tuple-element.42.rest_0_), channel_id=1, source_target_pairs={{0,1},{1,0},{2,3},{3,2},{4,5},{5,4},{6,7},{7,6},{8,9},{9,8},{10,11... | collective-permute-start | bytes 9437192 | tf_op jit(solution)/shard_map/ppermute | solution.py:587
  7.0 7.8 %collective-permute-start.1 = (s32[1024]{0:T(1024)S(1)}, s32[1024]{0:T(1024)S(1)}, u32[]{:S(2)}, u32[]{:S(2)}) collective-permute-start(s32[1024]{0:T(1024)S(1)} %bitcast.35), channel_id=1, source_target_pairs={{0,2},{1,3},{2,0},{3,1},{4,6},{5,7},{6,4},{7,5},{8,10},{9,11},{10,... | collective-permute-start | bytes 12296 | tf_op jit(solution)/shard_map/ppermute | solution.py:587
  9.5 5.3 %collective-permute-start.2 = (s32[1024]{0:T(1024)S(1)}, s32[1024]{0:T(1024)S(1)}, u32[]{:S(2)}, u32[]{:S(2)}) collective-permute-start(s32[1024]{0:T(1024)S(1)} %bitcast.36), channel_id=1, source_target_pairs={{0,3},{1,2},{2,1},{3,0},{4,7},{5,6},{6,5},{7,4},{8,11},{9,10},{10,... | collective-permute-start | bytes 12296 | tf_op jit(solution)/shard_map/ppermute | solution.py:587
  9.7 20.4 %collective-permute-start.21 = (f32[256,768]{1,0:T(8,128)S(1)}, f32[256,768]{1,0:T(8,128)S(1)}, u32[]{:S(2)}, u32[]{:S(2)}) collective-permute-start(f32[256,768]{1,0:T(8,128)S(1)} %get-tuple-element.55.hat_ref), channel_id=1, source_target_pairs={{0,2},{1,3},{2,0},{3,1},{4,6},{5,7},{6,4},{7,5},{8,10},{9,11},{10,... | collective-permute-start | bytes 2359304 | tf_op jit(solution)/shard_map/ppermute | solution.py:587
  12.5 34.1 %collective-permute-start.24 = (f32[256,768]{1,0:T(8,128)S(1)}, f32[256,768]{1,0:T(8,128)}, u32[]{:S(2)}, u32[]{:S(2)}) collective-permute-start(f32[256,768]{1,0:T(8,128)S(1)} %get-tuple-element.63), channel_id=1, source_target_pairs={{0,2},{1,3},{2,0},{3,1},{4,6},{5,7},{6,4},{7,5},{8,10},{9,11},{10,... | collective-permute-start | bytes 2359304 | tf_op jit(solution)/shard_map/ppermute | solution.py:587
  30.1 18.7 %collective-permute-start.22 = (f32[256,768]{1,0:T(8,128)S(1)}, f32[256,768]{1,0:T(8,128)}, u32[]{:S(2)}, u32[]{:S(2)}) collective-permute-start(f32[256,768]{1,0:T(8,128)S(1)} %collective-permute-done.21.rest_0_), channel_id=1, source_target_pairs={{0,4},{4,0},{8,12},{12,8},{1,5},{5,1},{9,13},{13,9},{2,6},{6,2},{1... | collective-permute-start | bytes 2359304 | tf_op jit(solution)/shard_map/ppermute | solution.py:587
  32.0 17.9 %collective-permute-start.23 = (f32[256,768]{1,0:T(8,128)S(1)}, f32[256,768]{1,0:T(8,128)}, u32[]{:S(2)}, u32[]{:S(2)}) collective-permute-start(f32[256,768]{1,0:T(8,128)S(1)} %collective-permute-done.21.rest_0_), channel_id=1, source_target_pairs={{0,8},{4,12},{8,0},{12,4},{1,9},{5,13},{9,1},{13,5},{2,10},{6,14},... | collective-permute-start | bytes 2359304 | tf_op jit(solution)/shard_map/ppermute | solution.py:587
  35.2 70.1 %collective-permute-start.25 = (f32[256,768]{1,0:T(8,128)S(1)}, f32[256,768]{1,0:T(8,128)}, u32[]{:S(2)}, u32[]{:S(2)}) collective-permute-start(f32[256,768]{1,0:T(8,128)S(1)} %collective-permute-done.21.rest_0_), channel_id=1, source_target_pairs={{0,1},{1,0},{2,3},{3,2},{4,5},{5,4},{6,7},{7,6},{8,9},{9,8},{10,11... | collective-permute-start | bytes 2359304 | tf_op jit(solution)/shard_map/ppermute | solution.py:587
  46.6 58.7 %collective-permute-start.28 = (f32[256,768]{1,0:T(8,128)}, f32[256,768]{1,0:T(8,128)}, u32[]{:S(2)}, u32[]{:S(2)}) collective-permute-start(f32[256,768]{1,0:T(8,128)} %collective-permute-done.24.rest_3_), channel_id=1, source_target_pairs={{0,1},{1,0},{2,3},{3,2},{4,5},{5,4},{6,7},{7,6},{8,9},{9,8},{10,11... | collective-permute-start | bytes 2359304 | tf_op jit(solution)/shard_map/ppermute | solution.py:587
  48.8 56.5 %collective-permute-start.26 = (f32[256,768]{1,0:T(8,128)}, f32[256,768]{1,0:T(8,128)}, u32[]{:S(2)}, u32[]{:S(2)}) collective-permute-start(f32[256,768]{1,0:T(8,128)} %collective-permute-done.22.rest_1_), channel_id=1, source_target_pairs={{0,1},{1,0},{2,3},{3,2},{4,5},{5,4},{6,7},{7,6},{8,9},{9,8},{10,11... | collective-permute-start | bytes 2359304 | tf_op jit(solution)/shard_map/ppermute | solution.py:587
  49.9 55.4 %collective-permute-start.27 = (f32[256,768]{1,0:T(8,128)}, f32[256,768]{1,0:T(8,128)}, u32[]{:S(2)}, u32[]{:S(2)}) collective-permute-start(f32[256,768]{1,0:T(8,128)} %collective-permute-done.23.rest_2_), channel_id=1, source_target_pairs={{0,1},{1,0},{2,3},{3,2},{4,5},{5,4},{6,7},{7,6},{8,9},{9,8},{10,11... | collective-permute-start | bytes 2359304 | tf_op jit(solution)/shard_map/ppermute | solution.py:587
  162.9 19.8 %collective-permute-start.30 = (f32[2096,768]{1,0:T(8,128)S(1)}, f32[2096,768]{1,0:T(8,128)S(1)}, u32[]{:S(2)}, u32[]{:S(2)}) collective-permute-start(f32[2096,768]{1,0:T(8,128)S(1)} %get-tuple-element.71), channel_id=1, source_target_pairs={{0,1},{1,0},{2,3},{3,2},{4,5},{5,4},{6,7},{7,6},{8,9},{9,8},{10,11... | collective-permute-start | bytes 19316744 | tf_op jit(solution)/shard_map/ppermute | solution.py:587
  182.2 15.2 %collective-permute-start.29 = (f32[2096,768]{1,0:T(8,128)S(1)}, f32[2096,768]{1,0:T(8,128)S(1)}, u32[]{:S(2)}, u32[]{:S(2)}) collective-permute-start(f32[2096,768]{1,0:T(8,128)S(1)} %get-tuple-element.70), channel_id=1, source_target_pairs={{0,1},{1,0},{2,3},{3,2},{4,5},{5,4},{6,7},{7,6},{8,9},{9,8},{10,11... | collective-permute-start | bytes 19316744 | tf_op jit(solution)/shard_map/ppermute | solution.py:587
  182.6 30.1 %collective-permute-start.4 = (f32[4,256,768]{2,1,0:T(8,128)S(1)}, f32[4,256,768]{2,1,0:T(8,128)S(1)}, u32[]{:S(2)}, u32[]{:S(2)}) collective-permute-start(f32[4,256,768]{2,1,0:T(8,128)S(1)} %copy-done.15), channel_id=1, source_target_pairs={{0,1},{1,0},{2,3},{3,2},{4,5},{5,4},{6,7},{7,6},{8,9},{9,8},{10,11... | collective-permute-start | bytes 9437192 | tf_op jit(solution)/shard_map/ppermute | solution.py:587
  197.0 97.3 %collective-permute-start.32 = (f32[1048,768]{1,0:T(8,128)S(1)}, f32[1048,768]{1,0:T(8,128)S(1)}, u32[]{:S(2)}, u32[]{:S(2)}) collective-permute-start(f32[1048,768]{1,0:T(8,128)S(1)} %get-tuple-element.75), channel_id=1, source_target_pairs={{0,1},{1,0},{2,3},{3,2},{4,5},{5,4},{6,7},{7,6},{8,9},{9,8},{10,11... | collective-permute-start | bytes 9658376 | tf_op jit(solution)/shard_map/ppermute | solution.py:587
  212.6 83.9 %collective-permute-start.31 = (f32[1048,768]{1,0:T(8,128)S(1)}, f32[1048,768]{1,0:T(8,128)S(1)}, u32[]{:S(2)}, u32[]{:S(2)}) collective-permute-start(f32[1048,768]{1,0:T(8,128)S(1)} %get-tuple-element.74), channel_id=1, source_target_pairs={{0,1},{1,0},{2,3},{3,2},{4,5},{5,4},{6,7},{7,6},{8,9},{9,8},{10,11... | collective-permute-start | bytes 9658376 | tf_op jit(solution)/shard_map/ppermute | solution.py:587
  213.6 19.9 %collective-permute-start.5 = (f32[2,128,768]{2,1,0:T(8,128)S(1)}, f32[2,128,768]{2,1,0:T(8,128)S(1)}, u32[]{:S(2)}, u32[]{:S(2)}) collective-permute-start(f32[2,128,768]{2,1,0:T(8,128)S(1)} %get-tuple-element.48), channel_id=1, source_target_pairs={{0,4},{4,0},{8,12},{12,8},{1,5},{5,1},{9,13},{13,9},{2,6},{6,2},{1... | collective-permute-start | bytes 2359304 | tf_op jit(solution)/shard_map/ppermute | solution.py:587
  214.3 20.9 %collective-permute-start.6 = (f32[2,128,768]{2,1,0:T(8,128)S(1)}, f32[2,128,768]{2,1,0:T(8,128)S(1)}, u32[]{:S(2)}, u32[]{:S(2)}) collective-permute-start(f32[2,128,768]{2,1,0:T(8,128)S(1)} %get-tuple-element.51), channel_id=1, source_target_pairs={{0,8},{4,12},{8,0},{12,4},{1,9},{5,13},{9,1},{13,5},{2,10},{6,14},... | collective-permute-start | bytes 2359304 | tf_op jit(solution)/shard_map/ppermute | solution.py:587
  233.7 10.6 %collective-permute-start.7 = (f32[128,768]{1,0:T(8,128)S(1)}, f32[128,768]{1,0:T(8,128)S(1)}, u32[]{:S(2)}, u32[]{:S(2)}) collective-permute-start(f32[128,768]{1,0:T(8,128)S(1)} %get-tuple-element.83), channel_id=1, source_target_pairs={{0,8},{4,12},{8,0},{12,4},{1,9},{5,13},{9,1},{13,5},{2,10},{6,14},... | collective-permute-start | bytes 1179656 | tf_op jit(solution)/shard_map/ppermute | solution.py:587
  235.4 10.3 %collective-permute-start.8 = (f32[128,768]{1,0:T(8,128)S(1)}, f32[128,768]{1,0:T(8,128)S(1)}, u32[]{:S(2)}, u32[]{:S(2)}) collective-permute-start(f32[128,768]{1,0:T(8,128)S(1)} %get-tuple-element.81), channel_id=1, source_target_pairs={{0,4},{4,0},{8,12},{12,8},{1,5},{5,1},{9,13},{13,9},{2,6},{6,2},{1... | collective-permute-start | bytes 1179656 | tf_op jit(solution)/shard_map/ppermute | solution.py:587
  246.2 12.7 %collective-permute-start.10 = (f32[8,768]{1,0:T(8,128)S(1)}, f32[8,768]{1,0:T(8,128)S(1)}, u32[]{:S(2)}, u32[]{:S(2)}) collective-permute-start(f32[8,768]{1,0:T(8,128)S(1)} %get-tuple-element.59), channel_id=1, source_target_pairs={{0,2},{1,3},{2,0},{3,1},{4,6},{5,7},{6,4},{7,5},{8,10},{9,11},{10,... | collective-permute-start | bytes 73736 | tf_op jit(solution)/shard_map/ppermute | solution.py:587
  257.1 3.3 %collective-permute-start.11 = (f32[8,768]{1,0:T(8,128)S(1)}, f32[8,768]{1,0:T(8,128)S(1)}, u32[]{:S(2)}, u32[]{:S(2)}) collective-permute-start(f32[8,768]{1,0:T(8,128)S(1)} %get-tuple-element.59), channel_id=1, source_target_pairs={{0,3},{1,2},{2,1},{3,0},{4,7},{5,6},{6,5},{7,4},{8,11},{9,10},{10,... | collective-permute-start | bytes 73736 | tf_op jit(solution)/shard_map/ppermute | solution.py:587
  257.1 3.3 %collective-permute-start.9 = (f32[8,768]{1,0:T(8,128)S(1)}, f32[8,768]{1,0:T(8,128)S(1)}, u32[]{:S(2)}, u32[]{:S(2)}) collective-permute-start(f32[8,768]{1,0:T(8,128)S(1)} %get-tuple-element.59), channel_id=1, source_target_pairs={{0,1},{1,0},{2,3},{3,2},{4,5},{5,4},{6,7},{7,6},{8,9},{9,8},{10,11... | collective-permute-start | bytes 73736 | tf_op jit(solution)/shard_map/ppermute | solution.py:587
  260.3 3.9 %collective-permute-start.13 = (f32[8,768]{1,0:T(8,128)S(1)}, f32[8,768]{1,0:T(8,128)S(1)}, u32[]{:S(2)}, u32[]{:S(2)}) collective-permute-start(f32[8,768]{1,0:T(8,128)S(1)} %add_add_fusion.1), channel_id=1, source_target_pairs={{0,8},{4,12},{8,0},{12,4},{1,9},{5,13},{9,1},{13,5},{2,10},{6,14},... | collective-permute-start | bytes 73736 | tf_op jit(solution)/shard_map/ppermute | solution.py:587
  261.0 5.0 %collective-permute-start.14 = (f32[8,768]{1,0:T(8,128)S(1)}, f32[8,768]{1,0:T(8,128)S(1)}, u32[]{:S(2)}, u32[]{:S(2)}) collective-permute-start(f32[8,768]{1,0:T(8,128)S(1)} %add_add_fusion.1), channel_id=1, source_target_pairs={{0,12},{4,8},{8,4},{12,0},{1,13},{5,9},{9,5},{13,1},{2,14},{6,10},... | collective-permute-start | bytes 73736 | tf_op jit(solution)/shard_map/ppermute | solution.py:587
  262.5 4.4 %collective-permute-start.12 = (f32[8,768]{1,0:T(8,128)S(1)}, f32[8,768]{1,0:T(8,128)S(1)}, u32[]{:S(2)}, u32[]{:S(2)}) collective-permute-start(f32[8,768]{1,0:T(8,128)S(1)} %add_add_fusion.1), channel_id=1, source_target_pairs={{0,4},{4,0},{8,12},{12,8},{1,5},{5,1},{9,13},{13,9},{2,6},{6,2},{1... | collective-permute-start | bytes 73736 | tf_op jit(solution)/shard_map/ppermute | solution.py:587
  264.2 12.0 %collective-permute-start.15 = (f32[128,768]{1,0:T(8,128)S(1)}, f32[128,768]{1,0:T(8,128)S(1)}, u32[]{:S(2)}, u32[]{:S(2)}) collective-permute-start(f32[128,768]{1,0:T(8,128)S(1)} %get-tuple-element.60.refs_0_), channel_id=1, source_target_pairs={{0,4},{4,0},{8,12},{12,8},{1,5},{5,1},{9,13},{13,9},{2,6},{6,2},{1... | collective-permute-start | bytes 1179656 | tf_op jit(solution)/shard_map/ppermute | solution.py:587
  266.0 15.7 %collective-permute-start.16 = (f32[128,768]{1,0:T(8,128)S(1)}, f32[128,768]{1,0:T(8,128)S(1)}, u32[]{:S(2)}, u32[]{:S(2)}) collective-permute-start(f32[128,768]{1,0:T(8,128)S(1)} %get-tuple-element.61.refs_1_), channel_id=1, source_target_pairs={{0,4},{4,0},{8,12},{12,8},{1,5},{5,1},{9,13},{13,9},{2,6},{6,2},{1... | collective-permute-start | bytes 1179656 | tf_op jit(solution)/shard_map/ppermute | solution.py:587
  266.9 15.4 %collective-permute-start.18 = (f32[128,768]{1,0:T(8,128)S(1)}, f32[128,768]{1,0:T(8,128)S(1)}, u32[]{:S(2)}, u32[]{:S(2)}) collective-permute-start(f32[128,768]{1,0:T(8,128)S(1)} %get-tuple-element.61.refs_1_), channel_id=1, source_target_pairs={{0,8},{4,12},{8,0},{12,4},{1,9},{5,13},{9,1},{13,5},{2,10},{6,14},... | collective-permute-start | bytes 1179656 | tf_op jit(solution)/shard_map/ppermute | solution.py:587
  276.2 10.3 %collective-permute-start.17 = (f32[128,768]{1,0:T(8,128)S(1)}, f32[128,768]{1,0:T(8,128)S(1)}, u32[]{:S(2)}, u32[]{:S(2)}) collective-permute-start(f32[128,768]{1,0:T(8,128)S(1)} %get-tuple-element.60.refs_0_), channel_id=1, source_target_pairs={{0,8},{4,12},{8,0},{12,4},{1,9},{5,13},{9,1},{13,5},{2,10},{6,14},... | collective-permute-start | bytes 1179656 | tf_op jit(solution)/shard_map/ppermute | solution.py:587
  281.7 10.7 %collective-permute-start.19 = (f32[128,768]{1,0:T(8,128)S(1)}, f32[128,768]{1,0:T(8,128)S(1)}, u32[]{:S(2)}, u32[]{:S(2)}) collective-permute-start(f32[128,768]{1,0:T(8,128)S(1)} %collective-permute-done.15.refs_2_), channel_id=1, source_target_pairs={{0,8},{4,12},{8,0},{12,4},{1,9},{5,13},{9,1},{13,5},{2,10},{6,14},... | collective-permute-start | bytes 1179656 | tf_op jit(solution)/shard_map/ppermute | solution.py:587
  282.3 10.1 %collective-permute-start.20 = (f32[128,768]{1,0:T(8,128)S(1)}, f32[128,768]{1,0:T(8,128)S(1)}, u32[]{:S(2)}, u32[]{:S(2)}) collective-permute-start(f32[128,768]{1,0:T(8,128)S(1)} %collective-permute-done.18.refs_5_), channel_id=1, source_target_pairs={{0,4},{4,0},{8,12},{12,8},{1,5},{5,1},{9,13},{13,9},{2,6},{6,2},{1... | collective-permute-start | bytes 1179656 | tf_op jit(solution)/shard_map/ppermute | solution.py:587
  (17 other events, 295.7 us)

commit v7 on v6

--- a/solution.py
+++ b/solution.py
@@ -137,10 +137,10 @@
 
     @pl.when(i == 0)
     def _():
-        for k in range(len(chunks)):
+        for k in range(min(3, len(chunks))):
             start(first(k))
 
-    pl.when(i + 1 < idx_ref[NEAR_PAIRS])(lambda: fetch(i + 1))
+    pl.when((i > 0) & (i + 1 < idx_ref[NEAR_PAIRS]))(lambda: fetch(i + 1))
 
     @pl.when(i == 0)
     def _():
@@ -149,6 +149,10 @@
             et_ref[:, at:at + n] = e_ref[at:at + n, :].T
 
         def ready(k):
+            if k + 3 < len(chunks):
+                start(first(k + 3))
+            elif k + 3 == len(chunks):
+                pl.when(idx_ref[NEAR_PAIRS] > 1)(lambda: fetch(1))
             if k == 0:
                 first(0)[0].wait()
                 turn(0)
@@ -231,9 +235,10 @@
         return part_ref.at[pl.ds(at, block), :], out_ref.at[pl.ds(half_start, block), :]
 
     def fetch(i):
-        start(split_copy(source(i), buf_ref.at[i % 2], sem.at[i % 2], 264))
+        start(split_copy(source(i), buf_ref.at[i % 3], sem.at[i % 3], 264))
 
     fetch(0)
+    pl.when(steps > 1)(lambda: fetch(1))
     got = None
     if got_ref is not None:
         target = rows_at(1 - core, got_offset, got_ref.shape[0])
@@ -242,8 +247,8 @@
     part_ref[...] = jnp.zeros_like(part_ref)
 
     def step(i, carry):
-        pltpu.make_async_copy(source(i), buf_ref.at[i % 2], sem.at[i % 2]).wait()
-        pl.when(i + 1 < steps)(lambda: fetch(i + 1))
+        pltpu.make_async_copy(source(i), buf_ref.at[i % 3], sem.at[i % 3]).wait()
+        pl.when(i + 2 < steps)(lambda: fetch(i + 2))
         k = i // count
         pair = idx_ref[PAIR_IDS + i % count]
         lse = tok_ref[pair, 0:1, :]
@@ -251,7 +256,7 @@
         label = lab_ref[pair] - idx_ref[ROW_START] - offset - k * block
         for at, n in chunk_list(block, 528):
             is_target = lax.broadcasted_iota(jnp.int32, (n, PAIR), 0) == label - at
-            grad = grad_tile(buf_ref[i % 2, at:at + n, :], lse, weight, is_target)
+            grad = grad_tile(buf_ref[i % 3, at:at + n, :], lse, weight, is_target)
             part_ref[pl.ds(pl.multiple_of(k * block + at, 8), n), :] += jnp.dot(grad, z_ref[pair], preferred_element_type=jnp.float32)
         pl.when(i % count == count - 1)(lambda: start(split_copy(*write(k), sem.at[4], 264)))
         return carry
@@ -533,7 +538,7 @@
         grid=(1,),
         in_specs=[ANY, whole(zc), whole(tok), whole(lab)] + extra_specs,
         out_specs=[pl.BlockSpec((rows, width), lambda i, s: (0, 0), pipeline_mode=pl.Buffered(1)), ANY],
-        scratch_shapes=[pltpu.VMEM((2, rows, PAIR), jnp.float32), pltpu.SemaphoreType.DMA((5,))],
+        scratch_shapes=[pltpu.VMEM((3, total // 6, PAIR), jnp.float32), pltpu.SemaphoreType.DMA((5,))],
     )
     return pl.pallas_call(
         functools.partial(de_kernel, offset, rows, got_offset if got is not None else None),

time: 300 us -> 293 us (0.977)
  Pallas kernels: 165 us -> 158 us
    pallas_call x4, Pallas kernels: 67.2 us -> 62.7 us  [call_de(): pl.pallas_call(functools.partial(de_kernel, offset, rows, got_offset if g...]
  transfers between devices with their start and end apart: 33 -> 33, of which waited for: 15 -> 15; matrix products, arithmetic and copies ran while one was open for 2% -> 2% of each run, Pallas kernels for 35% -> 34%
where the time goes in v7:
time: 293 us; the launch traced here: 292 us
  Pallas kernels  158 us (54%)
  waiting for transfers between devices  79.2 us (27%)
  starting transfers between devices  36.3 us (12%)
  local copies, waits for them, and re-layouts  9.74 us (3%)
  between operations  4.56 us (2%)
  other arithmetic  4.35 us (1%)
    ppermute x33, waiting for transfers between devices, flip(): return lax.ppermute(x, axis, [(k, k ^ bits) for k in range(n)])  79.2 us
    pallas_call x4, Pallas kernels, call_de(): pl.pallas_call(functools.partial(de_kernel, offset, rows, got_offset if g...  62.7 us
    pallas_call x2, Pallas kernels, call_logits(): pl.pallas_call(functools.partial(logits_kernel, count, base, order, len(p...  48.8 us
    ppermute x33, starting transfers between devices, flip(): return lax.ppermute(x, axis, [(k, k ^ bits) for k in range(n)])  36.3 us
    pallas_call x1, Pallas kernels, call_dz(): pl.pallas_call(dz_kernel, grid_spec=spec, out_shape=[half, half, jax.Shap...  24.9 us
    pallas_call x2, Pallas kernels, call_lse(): pl.pallas_call(lse_kernel, in_specs=[vmem, vmem, vmem], out_specs=vmem, o...  10.9 us
    unnamed x32, local copies, waits for them, and re-layouts  7.12 us
  transfers between devices with their start and end apart: 33, of which 15 were waited for; matrix products, arithmetic and copies ran while one was open for 2% of the time, Pallas kernels for 34%

profile of v7, /device:TPU:0, one launch (start us, length us, event | category | flops | bytes accessed | tf_op | source)
XLA Modules:
  0.0 292.3 jit_solution(12670995480031461867)
XLA Ops:
  2.2 3.4 %norm.1 = (f32[4,256,768]{2,1,0:T(8,128)}, f32[256,128]{1,0:T(8,128)S(1)}, f32[256,768]{1,0:T(8,128)S(1)}, f32[256,768]{1,0:T(8,128)S(1)}) custom-call(s32[10]{0:T(128)S(1)} %stack.58.pick_ref, bf16[4,256,768]{2,1,0:T(8,128)(2,1)S(1)} %bitcast.34), custom_call_target="tpu_custom_call" | custom-call | flops 10000000 | bytes 8000000 | tf_op jit(solution)/shard_map/norm/pallas_call | solution.py:345
  7.0 2.5 collective-permute-start.1
  9.7 1.9 collective-permute-start.21
  12.5 2.2 collective-permute-start.24
  18.6 11.5 %collective-permute-done.21.rest_0_ = f32[256,768]{1,0:T(8,128)S(1)} collective-permute-done((f32[256,768]{1,0:T(8,128)S(1)}, f32[256,768]{1,0:T(8,128)S(1)}, u32[]{:S(2)}, u32[]{:S(2)}) %collective-permute-start.21) | collective-permute-done | bytes 786464 | tf_op jit(solution)/shard_map/ppermute | solution.py:592
  30.1 1.9 collective-permute-start.22
  32.0 1.6 collective-permute-start.23
  35.2 11.4 %collective-permute-done.24.rest_3_ = f32[256,768]{1,0:T(8,128)} collective-permute-done((f32[256,768]{1,0:T(8,128)S(1)}, f32[256,768]{1,0:T(8,128)}, u32[]{:S(2)}, u32[]{:S(2)}) %collective-permute-start.24) | collective-permute-done | bytes 786464 | tf_op jit(solution)/shard_map/ppermute | solution.py:592
  46.6 2.2 collective-permute-done.22.rest_1_
  49.9 18.7 %logits_near.1 = (f32[8,6288,512]{2,1,0:T(8,128)}, bf16[8,512,768]{2,1,0:T(8,128)(2,1)}, f32[4,2,512]{2,1,0:T(2,128)}) custom-call(s32[40]{0:T(128)} %concatenate.11.idx_ref, bf16[12576,768]{1,0:T(8,128)(2,1)} %e_hbm.5, f32[768]{0:T(1024)} %gamma_ref.5, f32[768]{0:T(1024)} %beta_ref.3, f32[4,256,768]{2,1,0:T(8,128)} %get-tuple-element.42.rest_0_, ...), custom_call_target="tpu_custom_call" | custom-call | flops 14835253248 | bytes 38633472 | tf_op jit(solution)/shard_map/logits_near/pallas_call | solution.py:473
  69.3 5.6 %shard_map.101.tok_ref = f32[4,2,512]{2,1,0:T(2,128)S(1)} custom-call(f32[4,2,512]{2,1,0:T(2,128)S(1)} %copy-done.11, s32[4,1,512]{2,1,0:T(1,128)S(1)} %slice.49.lab_ref, f32[1,512]{1,0:T(1,128)S(1)} %broadcast_in_dim.57.scale_ref), custom_call_target="tpu_custom_call" | custom-call | flops 10000000 | bytes 1000000 | tf_op jit(solution)/shard_map/pallas_call | solution.py:311
  75.5 24.9 %dz_part.1 = (f32[4,256,768]{2,1,0:T(8,128)}, f32[4,256,768]{2,1,0:T(8,128)}, f32[4,1,512]{2,1,0:T(1,128)}, f32[8,6288,512]{2,1,0:T(8,128)}) custom-call(s32[40]{0:T(128)} %concatenate.11.idx_ref, bf16[12576,768]{1,0:T(8,128)(2,1)} %e_hbm.5, f32[8,6288,512]{2,1,0:T(8,128)} %get-tuple-element.43.l_hbm, ...), custom_call_target="tpu_custom_call", output_to_operand_aliasing={{3}: (2, {})} | custom-call | flops 14835253248 | bytes 38633472 | tf_op jit(solution)/shard_map/dz_part/pallas_call | solution.py:514
  103.2 30.1 %logits_far.1 = (f32[8,6288,512]{2,1,0:T(8,128)}, bf16[8,512,768]{2,1,0:T(8,128)(2,1)}, f32[4,2,512]{2,1,0:T(2,128)}) custom-call(s32[40]{0:T(128)} %concatenate.11.idx_ref, bf16[12576,768]{1,0:T(8,128)(2,1)} %e_hbm.5, f32[768]{0:T(1024)} %gamma_ref.5, f32[768]{0:T(1024)} %beta_ref.3, ...), custom_call_target="tpu_custom_call", output_to_operand_aliasing={{0}: (12, {}), {1}: (13, {})} | custom-call | flops 14835253248 | bytes 38633472 | tf_op jit(solution)/shard_map/logits_far/pallas_call | solution.py:473
  134.0 5.3 %shard_map.102 = f32[4,2,512]{2,1,0:T(2,128)S(1)} custom-call(f32[4,2,512]{2,1,0:T(2,128)S(1)} %copy-done.10, s32[4,1,512]{2,1,0:T(1,128)S(1)} %slice.53.lab_ref, f32[1,512]{1,0:T(1,128)S(1)} %broadcast_in_dim.57.scale_ref), custom_call_target="tpu_custom_call" | custom-call | flops 10000000 | bytes 1000000 | tf_op jit(solution)/shard_map/pallas_call | solution.py:311
  139.3 2.8 copy-done
  142.1 18.6 %shard_map.103 = (f32[2096,768]{1,0:T(8,128)S(1)}, f32[12576,768]{1,0:T(8,128)}) custom-call(s32[40]{0:T(128)S(1)} %copy-done.8, f32[8,6288,512]{2,1,0:T(8,128)} %get-tuple-element.66.l_ref, bf16[8,512,768]{2,1,0:T(8,128)(2,1)S(1)} %copy-done, f32[8,2,512]{2,1,0:T(2,128)S(1)} %pad_maximum_fusion.tok_ref, s32[8,1,512]{2,1,0:T(1,128)S(1)} %reshape.97.lab_ref), custom_call_target="tpu_custom_call" | custom-call | flops 8241807360 | bytes 21463040 | tf_op jit(solution)/shard_map/pallas_call | solution.py:543
  160.9 18.6 %shard_map.104 = (f32[2096,768]{1,0:T(8,128)S(1)}, f32[12576,768]{1,0:T(8,128)}) custom-call(s32[40]{0:T(128)S(1)} %copy-done.8, f32[8,6288,512]{2,1,0:T(8,128)} %get-tuple-element.66.l_ref, bf16[8,512,768]{2,1,0:T(8,128)(2,1)S(1)} %copy-done, f32[8,2,512]{2,1,0:T(2,128)S(1)} %pad_maximum_fusion.tok_ref, ...), custom_call_target="tpu_custom_call", output_to_operand_aliasing={{1}: (5, {})} | custom-call | flops 8241807360 | bytes 21463040 | tf_op jit(solution)/shard_map/pallas_call | solution.py:543
  180.0 12.6 %shard_map.105 = (f32[1048,768]{1,0:T(8,128)S(1)}, f32[12576,768]{1,0:T(8,128)}) custom-call(s32[40]{0:T(128)S(1)} %copy-done.8, f32[8,6288,512]{2,1,0:T(8,128)} %get-tuple-element.66.l_ref, bf16[8,512,768]{2,1,0:T(8,128)(2,1)S(1)} %copy-done, f32[8,2,512]{2,1,0:T(2,128)S(1)} %pad_maximum_fusion.tok_ref, ...), custom_call_target="tpu_custom_call", output_to_operand_aliasing={{1}: (6, {})} | custom-call | flops 4120903680 | bytes 10731520 | tf_op jit(solution)/shard_map/pallas_call | solution.py:543
  193.0 12.9 %shard_map.106 = (f32[1048,768]{1,0:T(8,128)S(1)}, f32[12576,768]{1,0:T(8,128)}) custom-call(s32[40]{0:T(128)S(1)} %copy-done.8, f32[8,6288,512]{2,1,0:T(8,128)} %get-tuple-element.66.l_ref, bf16[8,512,768]{2,1,0:T(8,128)(2,1)S(1)} %copy-done, f32[8,2,512]{2,1,0:T(2,128)S(1)} %pad_maximum_fusion.tok_ref, ...), custom_call_target="tpu_custom_call", output_to_operand_aliasing={{1}: (6, {})} | custom-call | flops 4120903680 | bytes 10731520 | tf_op jit(solution)/shard_map/pallas_call | solution.py:543
  209.1 17.7 %collective-permute-done.5 = f32[2,128,768]{2,1,0:T(8,128)S(1)} collective-permute-done((f32[2,128,768]{2,1,0:T(8,128)S(1)}, f32[2,128,768]{2,1,0:T(8,128)S(1)}, u32[]{:S(2)}, u32[]{:S(2)}) %collective-permute-start.5) | collective-permute-done | bytes 786464 | tf_op jit(solution)/shard_map/ppermute | solution.py:592
  227.0 1.5 collective-permute-start.7
  229.4 8.2 %collective-permute-done.7.a_got_ref = f32[128,768]{1,0:T(8,128)S(1)} collective-permute-done((f32[128,768]{1,0:T(8,128)S(1)}, f32[128,768]{1,0:T(8,128)S(1)}, u32[]{:S(2)}, u32[]{:S(2)}) %collective-permute-start.7) | collective-permute-done | bytes 393248 | tf_op jit(solution)/shard_map/ppermute | solution.py:592
  239.5 11.0 %collective-permute-start.10 = (f32[8,768]{1,0:T(8,128)S(1)}, f32[8,768]{1,0:T(8,128)S(1)}, u32[]{:S(2)}, u32[]{:S(2)}) collective-permute-start(f32[8,768]{1,0:T(8,128)S(1)} %get-tuple-element.59), channel_id=1, source_target_pairs={{0,2},{1,3},{2,0},{3,1},{4,6},{5,7},{6,4},{7,5},{8,10},{9,11},{10,... | collective-permute-start | bytes 73736 | tf_op jit(solution)/shard_map/ppermute | solution.py:592
  250.7 1.6 collective-permute-done.10
  254.3 1.6 collective-permute-start.14
  261.5 8.1 %collective-permute-done.15.refs_2_ = f32[128,768]{1,0:T(8,128)S(1)} collective-permute-done((f32[128,768]{1,0:T(8,128)S(1)}, f32[128,768]{1,0:T(8,128)S(1)}, u32[]{:S(2)}, u32[]{:S(2)}) %collective-permute-start.15) | collective-permute-done | bytes 393248 | tf_op jit(solution)/shard_map/ppermute | solution.py:592
  270.2 5.0 %collective-permute-done.16.refs_3_ = f32[128,768]{1,0:T(8,128)S(1)} collective-permute-done((f32[128,768]{1,0:T(8,128)S(1)}, f32[128,768]{1,0:T(8,128)S(1)}, u32[]{:S(2)}, u32[]{:S(2)}) %collective-permute-start.16) | collective-permute-done | bytes 393248 | tf_op jit(solution)/shard_map/ppermute | solution.py:592
  277.8 2.1 collective-permute-done.17.refs_4_
  279.9 5.9 %collective-permute-done.19.refs_6_ = f32[128,768]{1,0:T(8,128)S(1)} collective-permute-done((f32[128,768]{1,0:T(8,128)S(1)}, f32[128,768]{1,0:T(8,128)S(1)}, u32[]{:S(2)}, u32[]{:S(2)}) %collective-permute-start.19) | collective-permute-done | bytes 393248 | tf_op jit(solution)/shard_map/ppermute | solution.py:592
  285.8 1.8 round.1
  287.7 2.2 place.2.de_ref
  289.9 2.2 place.3
  (120 shorter events, 30.0 us)
Async XLA Ops:
  5.5 44.4 %collective-permute-start.3 = (f32[4,256,768]{2,1,0:T(8,128)}, f32[4,256,768]{2,1,0:T(8,128)}, u32[]{:S(2)}, u32[]{:S(2)}) collective-permute-start(f32[4,256,768]{2,1,0:T(8,128)} %get-tuple-element.42.rest_0_), channel_id=1, source_target_pairs={{0,1},{1,0},{2,3},{3,2},{4,5},{5,4},{6,7},{7,6},{8,9},{9,8},{10,11... | collective-permute-start | bytes 9437192 | tf_op jit(solution)/shard_map/ppermute | solution.py:592
  7.0 7.8 %collective-permute-start.1 = (s32[1024]{0:T(1024)S(1)}, s32[1024]{0:T(1024)S(1)}, u32[]{:S(2)}, u32[]{:S(2)}) collective-permute-start(s32[1024]{0:T(1024)S(1)} %bitcast.35), channel_id=1, source_target_pairs={{0,2},{1,3},{2,0},{3,1},{4,6},{5,7},{6,4},{7,5},{8,10},{9,11},{10,... | collective-permute-start | bytes 12296 | tf_op jit(solution)/shard_map/ppermute | solution.py:592
  9.5 5.3 %collective-permute-start.2 = (s32[1024]{0:T(1024)S(1)}, s32[1024]{0:T(1024)S(1)}, u32[]{:S(2)}, u32[]{:S(2)}) collective-permute-start(s32[1024]{0:T(1024)S(1)} %bitcast.36), channel_id=1, source_target_pairs={{0,3},{1,2},{2,1},{3,0},{4,7},{5,6},{6,5},{7,4},{8,11},{9,10},{10,... | collective-permute-start | bytes 12296 | tf_op jit(solution)/shard_map/ppermute | solution.py:592
  9.7 20.4 %collective-permute-start.21 = (f32[256,768]{1,0:T(8,128)S(1)}, f32[256,768]{1,0:T(8,128)S(1)}, u32[]{:S(2)}, u32[]{:S(2)}) collective-permute-start(f32[256,768]{1,0:T(8,128)S(1)} %get-tuple-element.55.hat_ref), channel_id=1, source_target_pairs={{0,2},{1,3},{2,0},{3,1},{4,6},{5,7},{6,4},{7,5},{8,10},{9,11},{10,... | collective-permute-start | bytes 2359304 | tf_op jit(solution)/shard_map/ppermute | solution.py:592
  12.5 34.1 %collective-permute-start.24 = (f32[256,768]{1,0:T(8,128)S(1)}, f32[256,768]{1,0:T(8,128)}, u32[]{:S(2)}, u32[]{:S(2)}) collective-permute-start(f32[256,768]{1,0:T(8,128)S(1)} %get-tuple-element.63), channel_id=1, source_target_pairs={{0,2},{1,3},{2,0},{3,1},{4,6},{5,7},{6,4},{7,5},{8,10},{9,11},{10,... | collective-permute-start | bytes 2359304 | tf_op jit(solution)/shard_map/ppermute | solution.py:592
  30.1 18.7 %collective-permute-start.22 = (f32[256,768]{1,0:T(8,128)S(1)}, f32[256,768]{1,0:T(8,128)}, u32[]{:S(2)}, u32[]{:S(2)}) collective-permute-start(f32[256,768]{1,0:T(8,128)S(1)} %collective-permute-done.21.rest_0_), channel_id=1, source_target_pairs={{0,4},{4,0},{8,12},{12,8},{1,5},{5,1},{9,13},{13,9},{2,6},{6,2},{1... | collective-permute-start | bytes 2359304 | tf_op jit(solution)/shard_map/ppermute | solution.py:592
  32.0 17.9 %collective-permute-start.23 = (f32[256,768]{1,0:T(8,128)S(1)}, f32[256,768]{1,0:T(8,128)}, u32[]{:S(2)}, u32[]{:S(2)}) collective-permute-start(f32[256,768]{1,0:T(8,128)S(1)} %collective-permute-done.21.rest_0_), channel_id=1, source_target_pairs={{0,8},{4,12},{8,0},{12,4},{1,9},{5,13},{9,1},{13,5},{2,10},{6,14},... | collective-permute-start | bytes 2359304 | tf_op jit(solution)/shard_map/ppermute | solution.py:592
  35.2 67.9 %collective-permute-start.25 = (f32[256,768]{1,0:T(8,128)S(1)}, f32[256,768]{1,0:T(8,128)}, u32[]{:S(2)}, u32[]{:S(2)}) collective-permute-start(f32[256,768]{1,0:T(8,128)S(1)} %collective-permute-done.21.rest_0_), channel_id=1, source_target_pairs={{0,1},{1,0},{2,3},{3,2},{4,5},{5,4},{6,7},{7,6},{8,9},{9,8},{10,11... | collective-permute-start | bytes 2359304 | tf_op jit(solution)/shard_map/ppermute | solution.py:592
  46.6 56.5 %collective-permute-start.28 = (f32[256,768]{1,0:T(8,128)}, f32[256,768]{1,0:T(8,128)}, u32[]{:S(2)}, u32[]{:S(2)}) collective-permute-start(f32[256,768]{1,0:T(8,128)} %collective-permute-done.24.rest_3_), channel_id=1, source_target_pairs={{0,1},{1,0},{2,3},{3,2},{4,5},{5,4},{6,7},{7,6},{8,9},{9,8},{10,11... | collective-permute-start | bytes 2359304 | tf_op jit(solution)/shard_map/ppermute | solution.py:592
  48.8 54.3 %collective-permute-start.26 = (f32[256,768]{1,0:T(8,128)}, f32[256,768]{1,0:T(8,128)}, u32[]{:S(2)}, u32[]{:S(2)}) collective-permute-start(f32[256,768]{1,0:T(8,128)} %collective-permute-done.22.rest_1_), channel_id=1, source_target_pairs={{0,1},{1,0},{2,3},{3,2},{4,5},{5,4},{6,7},{7,6},{8,9},{9,8},{10,11... | collective-permute-start | bytes 2359304 | tf_op jit(solution)/shard_map/ppermute | solution.py:592
  49.9 53.3 %collective-permute-start.27 = (f32[256,768]{1,0:T(8,128)}, f32[256,768]{1,0:T(8,128)}, u32[]{:S(2)}, u32[]{:S(2)}) collective-permute-start(f32[256,768]{1,0:T(8,128)} %collective-permute-done.23.rest_2_), channel_id=1, source_target_pairs={{0,1},{1,0},{2,3},{3,2},{4,5},{5,4},{6,7},{7,6},{8,9},{9,8},{10,11... | collective-permute-start | bytes 2359304 | tf_op jit(solution)/shard_map/ppermute | solution.py:592
  160.7 19.3 %collective-permute-start.30 = (f32[2096,768]{1,0:T(8,128)S(1)}, f32[2096,768]{1,0:T(8,128)S(1)}, u32[]{:S(2)}, u32[]{:S(2)}) collective-permute-start(f32[2096,768]{1,0:T(8,128)S(1)} %get-tuple-element.71), channel_id=1, source_target_pairs={{0,1},{1,0},{2,3},{3,2},{4,5},{5,4},{6,7},{7,6},{8,9},{9,8},{10,11... | collective-permute-start | bytes 19316744 | tf_op jit(solution)/shard_map/ppermute | solution.py:592
  179.4 13.6 %collective-permute-start.29 = (f32[2096,768]{1,0:T(8,128)S(1)}, f32[2096,768]{1,0:T(8,128)S(1)}, u32[]{:S(2)}, u32[]{:S(2)}) collective-permute-start(f32[2096,768]{1,0:T(8,128)S(1)} %get-tuple-element.70), channel_id=1, source_target_pairs={{0,1},{1,0},{2,3},{3,2},{4,5},{5,4},{6,7},{7,6},{8,9},{9,8},{10,11... | collective-permute-start | bytes 19316744 | tf_op jit(solution)/shard_map/ppermute | solution.py:592
  179.9 26.2 %collective-permute-start.4 = (f32[4,256,768]{2,1,0:T(8,128)S(1)}, f32[4,256,768]{2,1,0:T(8,128)S(1)}, u32[]{:S(2)}, u32[]{:S(2)}) collective-permute-start(f32[4,256,768]{2,1,0:T(8,128)S(1)} %copy-done.15), channel_id=1, source_target_pairs={{0,1},{1,0},{2,3},{3,2},{4,5},{5,4},{6,7},{7,6},{8,9},{9,8},{10,11... | collective-permute-start | bytes 9437192 | tf_op jit(solution)/shard_map/ppermute | solution.py:592
  192.6 95.1 %collective-permute-start.32 = (f32[1048,768]{1,0:T(8,128)S(1)}, f32[1048,768]{1,0:T(8,128)S(1)}, u32[]{:S(2)}, u32[]{:S(2)}) collective-permute-start(f32[1048,768]{1,0:T(8,128)S(1)} %get-tuple-element.75), channel_id=1, source_target_pairs={{0,1},{1,0},{2,3},{3,2},{4,5},{5,4},{6,7},{7,6},{8,9},{9,8},{10,11... | collective-permute-start | bytes 9658376 | tf_op jit(solution)/shard_map/ppermute | solution.py:592
  205.9 84.0 %collective-permute-start.31 = (f32[1048,768]{1,0:T(8,128)S(1)}, f32[1048,768]{1,0:T(8,128)S(1)}, u32[]{:S(2)}, u32[]{:S(2)}) collective-permute-start(f32[1048,768]{1,0:T(8,128)S(1)} %get-tuple-element.74), channel_id=1, source_target_pairs={{0,1},{1,0},{2,3},{3,2},{4,5},{5,4},{6,7},{7,6},{8,9},{9,8},{10,11... | collective-permute-start | bytes 9658376 | tf_op jit(solution)/shard_map/ppermute | solution.py:592
  207.0 19.9 %collective-permute-start.5 = (f32[2,128,768]{2,1,0:T(8,128)S(1)}, f32[2,128,768]{2,1,0:T(8,128)S(1)}, u32[]{:S(2)}, u32[]{:S(2)}) collective-permute-start(f32[2,128,768]{2,1,0:T(8,128)S(1)} %get-tuple-element.48), channel_id=1, source_target_pairs={{0,4},{4,0},{8,12},{12,8},{1,5},{5,1},{9,13},{13,9},{2,6},{6,2},{1... | collective-permute-start | bytes 2359304 | tf_op jit(solution)/shard_map/ppermute | solution.py:592
  207.6 20.9 %collective-permute-start.6 = (f32[2,128,768]{2,1,0:T(8,128)S(1)}, f32[2,128,768]{2,1,0:T(8,128)S(1)}, u32[]{:S(2)}, u32[]{:S(2)}) collective-permute-start(f32[2,128,768]{2,1,0:T(8,128)S(1)} %get-tuple-element.51), channel_id=1, source_target_pairs={{0,8},{4,12},{8,0},{12,4},{1,9},{5,13},{9,1},{13,5},{2,10},{6,14},... | collective-permute-start | bytes 2359304 | tf_op jit(solution)/shard_map/ppermute | solution.py:592
  227.0 10.6 %collective-permute-start.7 = (f32[128,768]{1,0:T(8,128)S(1)}, f32[128,768]{1,0:T(8,128)S(1)}, u32[]{:S(2)}, u32[]{:S(2)}) collective-permute-start(f32[128,768]{1,0:T(8,128)S(1)} %get-tuple-element.83), channel_id=1, source_target_pairs={{0,8},{4,12},{8,0},{12,4},{1,9},{5,13},{9,1},{13,5},{2,10},{6,14},... | collective-permute-start | bytes 1179656 | tf_op jit(solution)/shard_map/ppermute | solution.py:592
  228.7 10.3 %collective-permute-start.8 = (f32[128,768]{1,0:T(8,128)S(1)}, f32[128,768]{1,0:T(8,128)S(1)}, u32[]{:S(2)}, u32[]{:S(2)}) collective-permute-start(f32[128,768]{1,0:T(8,128)S(1)} %get-tuple-element.81), channel_id=1, source_target_pairs={{0,4},{4,0},{8,12},{12,8},{1,5},{5,1},{9,13},{13,9},{2,6},{6,2},{1... | collective-permute-start | bytes 1179656 | tf_op jit(solution)/shard_map/ppermute | solution.py:592
  239.5 12.8 %collective-permute-start.10 = (f32[8,768]{1,0:T(8,128)S(1)}, f32[8,768]{1,0:T(8,128)S(1)}, u32[]{:S(2)}, u32[]{:S(2)}) collective-permute-start(f32[8,768]{1,0:T(8,128)S(1)} %get-tuple-element.59), channel_id=1, source_target_pairs={{0,2},{1,3},{2,0},{3,1},{4,6},{5,7},{6,4},{7,5},{8,10},{9,11},{10,... | collective-permute-start | bytes 73736 | tf_op jit(solution)/shard_map/ppermute | solution.py:592
  250.5 3.3 %collective-permute-start.11 = (f32[8,768]{1,0:T(8,128)S(1)}, f32[8,768]{1,0:T(8,128)S(1)}, u32[]{:S(2)}, u32[]{:S(2)}) collective-permute-start(f32[8,768]{1,0:T(8,128)S(1)} %get-tuple-element.59), channel_id=1, source_target_pairs={{0,3},{1,2},{2,1},{3,0},{4,7},{5,6},{6,5},{7,4},{8,11},{9,10},{10,... | collective-permute-start | bytes 73736 | tf_op jit(solution)/shard_map/ppermute | solution.py:592
  250.5 3.3 %collective-permute-start.9 = (f32[8,768]{1,0:T(8,128)S(1)}, f32[8,768]{1,0:T(8,128)S(1)}, u32[]{:S(2)}, u32[]{:S(2)}) collective-permute-start(f32[8,768]{1,0:T(8,128)S(1)} %get-tuple-element.59), channel_id=1, source_target_pairs={{0,1},{1,0},{2,3},{3,2},{4,5},{5,4},{6,7},{7,6},{8,9},{9,8},{10,11... | collective-permute-start | bytes 73736 | tf_op jit(solution)/shard_map/ppermute | solution.py:592
  253.8 3.9 %collective-permute-start.13 = (f32[8,768]{1,0:T(8,128)S(1)}, f32[8,768]{1,0:T(8,128)S(1)}, u32[]{:S(2)}, u32[]{:S(2)}) collective-permute-start(f32[8,768]{1,0:T(8,128)S(1)} %add_add_fusion.1), channel_id=1, source_target_pairs={{0,8},{4,12},{8,0},{12,4},{1,9},{5,13},{9,1},{13,5},{2,10},{6,14},... | collective-permute-start | bytes 73736 | tf_op jit(solution)/shard_map/ppermute | solution.py:592
  254.3 5.0 %collective-permute-start.14 = (f32[8,768]{1,0:T(8,128)S(1)}, f32[8,768]{1,0:T(8,128)S(1)}, u32[]{:S(2)}, u32[]{:S(2)}) collective-permute-start(f32[8,768]{1,0:T(8,128)S(1)} %add_add_fusion.1), channel_id=1, source_target_pairs={{0,12},{4,8},{8,4},{12,0},{1,13},{5,9},{9,5},{13,1},{2,14},{6,10},... | collective-permute-start | bytes 73736 | tf_op jit(solution)/shard_map/ppermute | solution.py:592
  255.9 4.4 %collective-permute-start.12 = (f32[8,768]{1,0:T(8,128)S(1)}, f32[8,768]{1,0:T(8,128)S(1)}, u32[]{:S(2)}, u32[]{:S(2)}) collective-permute-start(f32[8,768]{1,0:T(8,128)S(1)} %add_add_fusion.1), channel_id=1, source_target_pairs={{0,4},{4,0},{8,12},{12,8},{1,5},{5,1},{9,13},{13,9},{2,6},{6,2},{1... | collective-permute-start | bytes 73736 | tf_op jit(solution)/shard_map/ppermute | solution.py:592
  257.6 12.0 %collective-permute-start.15 = (f32[128,768]{1,0:T(8,128)S(1)}, f32[128,768]{1,0:T(8,128)S(1)}, u32[]{:S(2)}, u32[]{:S(2)}) collective-permute-start(f32[128,768]{1,0:T(8,128)S(1)} %get-tuple-element.60.refs_0_), channel_id=1, source_target_pairs={{0,4},{4,0},{8,12},{12,8},{1,5},{5,1},{9,13},{13,9},{2,6},{6,2},{1... | collective-permute-start | bytes 1179656 | tf_op jit(solution)/shard_map/ppermute | solution.py:592
  259.3 15.9 %collective-permute-start.16 = (f32[128,768]{1,0:T(8,128)S(1)}, f32[128,768]{1,0:T(8,128)S(1)}, u32[]{:S(2)}, u32[]{:S(2)}) collective-permute-start(f32[128,768]{1,0:T(8,128)S(1)} %get-tuple-element.61.refs_1_), channel_id=1, source_target_pairs={{0,4},{4,0},{8,12},{12,8},{1,5},{5,1},{9,13},{13,9},{2,6},{6,2},{1... | collective-permute-start | bytes 1179656 | tf_op jit(solution)/shard_map/ppermute | solution.py:592
  260.3 15.3 %collective-permute-start.18 = (f32[128,768]{1,0:T(8,128)S(1)}, f32[128,768]{1,0:T(8,128)S(1)}, u32[]{:S(2)}, u32[]{:S(2)}) collective-permute-start(f32[128,768]{1,0:T(8,128)S(1)} %get-tuple-element.61.refs_1_), channel_id=1, source_target_pairs={{0,8},{4,12},{8,0},{12,4},{1,9},{5,13},{9,1},{13,5},{2,10},{6,14},... | collective-permute-start | bytes 1179656 | tf_op jit(solution)/shard_map/ppermute | solution.py:592
  269.6 10.3 %collective-permute-start.17 = (f32[128,768]{1,0:T(8,128)S(1)}, f32[128,768]{1,0:T(8,128)S(1)}, u32[]{:S(2)}, u32[]{:S(2)}) collective-permute-start(f32[128,768]{1,0:T(8,128)S(1)} %get-tuple-element.60.refs_0_), channel_id=1, source_target_pairs={{0,8},{4,12},{8,0},{12,4},{1,9},{5,13},{9,1},{13,5},{2,10},{6,14},... | collective-permute-start | bytes 1179656 | tf_op jit(solution)/shard_map/ppermute | solution.py:592
  275.2 10.6 %collective-permute-start.19 = (f32[128,768]{1,0:T(8,128)S(1)}, f32[128,768]{1,0:T(8,128)S(1)}, u32[]{:S(2)}, u32[]{:S(2)}) collective-permute-start(f32[128,768]{1,0:T(8,128)S(1)} %collective-permute-done.15.refs_2_), channel_id=1, source_target_pairs={{0,8},{4,12},{8,0},{12,4},{1,9},{5,13},{9,1},{13,5},{2,10},{6,14},... | collective-permute-start | bytes 1179656 | tf_op jit(solution)/shard_map/ppermute | solution.py:592
  275.6 10.2 %collective-permute-start.20 = (f32[128,768]{1,0:T(8,128)S(1)}, f32[128,768]{1,0:T(8,128)S(1)}, u32[]{:S(2)}, u32[]{:S(2)}) collective-permute-start(f32[128,768]{1,0:T(8,128)S(1)} %collective-permute-done.18.refs_5_), channel_id=1, source_target_pairs={{0,4},{4,0},{8,12},{12,8},{1,5},{5,1},{9,13},{13,9},{2,6},{6,2},{1... | collective-permute-start | bytes 1179656 | tf_op jit(solution)/shard_map/ppermute | solution.py:592
  (17 other events, 288.3 us)
